TPU v7x, 32 devices: a whole 2x2x4 slice. The times are simulated.
32 devices in a mesh: dp: 4 (over x, core), seq: 8 (over z, y).
Axes of the slice: x: 2, y: 2, z: 4, core: 2. Of those that a mesh axis runs over, the one named last changes fastest.
Arguments:
- tokens: bfloat16 [4096, 1152], P(('dp', 'seq')), may hold values from -6 to 6
- route: int32 [4096, 1], P(('dp', 'seq')), may hold values from 0 to 3; in each aligned block of 128 rows (0 to 127, 128 to 255, ...) at most 40 rows name the same one
- cotangent: bfloat16 [4096, 1152], P(('dp', 'seq')), may hold values from -6 to 6
- gain_mix: bfloat16 [1152], P(('dp', 'seq')), may hold values from 0.5 to 1.5
- w_in: bfloat16 [1152, 4608], P(('dp', 'seq')), may hold values from -0.1875 to 0.1875
- conv_w: bfloat16 [2304, 4], P(('dp', 'seq')), may hold values from -3 to 3
- w_x: bfloat16 [2304, 104], P(('dp', 'seq')), may hold values from -0.125 to 0.125
- w_dt: bfloat16 [2304, 72], P(('dp', 'seq')), may hold values from -0.75 to 0.75
- dt_bias: bfloat16 [2304], P(('dp', 'seq')), may hold values from -5 to -4.1875
- a_log: bfloat16 [2304, 16], P(('dp', 'seq')), as said below
- d_skip: bfloat16 [2304], P(('dp', 'seq')), may hold values from 0.5 to 1.5
- w_out: bfloat16 [2304, 1152], P(('dp', 'seq')), may hold values from -0.25 to 0.25
- gain_moe: bfloat16 [1152], P(('dp', 'seq')), may hold values from 0.5 to 1.5
- w_up: bfloat16 [4, 3072, 1152], P('dp', 'seq'), may hold values from -0.1875 to 0.1875
- w_down: bfloat16 [4, 3072, 1152], P('dp', 'seq'), may hold values from -0.21875 to 0.21875
Outputs:
- result: bfloat16 [4096, 1152], P(('dp', 'seq'))
- grad_tokens: float32 [4096, 1152], P(('dp', 'seq'))
- grad_gain_mix: float32 [1152], P(('dp', 'seq'))
- grad_w_in: float32 [1152, 4608], P(('dp', 'seq'))
- grad_conv_w: float32 [2304, 4], P(('dp', 'seq'))
- grad_w_x: float32 [2304, 104], P(('dp', 'seq'))
- grad_w_dt: float32 [2304, 72], P(('dp', 'seq'))
- grad_dt_bias: float32 [2304], P(('dp', 'seq'))
- grad_a_log: float32 [2304, 16], P(('dp', 'seq'))
- grad_d_skip: float32 [2304], P(('dp', 'seq'))
- grad_w_out: float32 [2304, 1152], P(('dp', 'seq'))
- grad_gain_moe: float32 [1152], P(('dp', 'seq'))
- grad_w_up: float32 [4, 3072, 1152], P('dp', 'seq')
- grad_w_down: float32 [4, 3072, 1152], P('dp', 'seq')
Inputs may be any that keep to these rules, and one draw needn't show every extreme that they name: `route`: in each aligned block of 128 tokens no expert is named by more than 40 tokens, a bound that some block reaches. `a_log`: finite values.
All inputs are finite; a program needn't handle non-finite values.
Results may differ from a plain program's by a relative error of at most 0.014.
Values may be sent and summed in bfloat16 or wider, within the bound.
A program may use at most 256 MiB of HBM per device.

v0:
```python
from functools import partial
import math

import jax
import jax.numpy as jnp
from jax import lax
from jax.sharding import PartitionSpec as P

D = 1152
DI = 2304
NS = 16
RANK = 72
E = 4
CAP = 40


eps = 1e-05


def from_behind(value, axis, by):
    peers = lax.axis_size(axis)
    pairs = [(i, i + by) for i in range(peers) if 0 <= i + by < peers]
    return lax.ppermute(value, axis, pairs)


def rms_norm(values, gain_vec):
    return values * lax.rsqrt(jnp.mean(values * values, axis=-1, keepdims=True) + eps) * gain_vec


def conv_silu(x_part, tail_prev, conv_w):
    padded = jnp.concatenate([tail_prev, x_part], axis=0)
    length = x_part.shape[0]
    mixed_taps = padded[0:length] * conv_w[:, 0] + padded[1 : length + 1] * conv_w[:, 1]
    mixed_taps = (
        mixed_taps + padded[2 : length + 2] * conv_w[:, 2] + padded[3 : length + 3] * conv_w[:, 3]
    )
    return jax.nn.silu(mixed_taps)


def rates(dt_pre, bias_vec, alog_mat):
    return (jax.nn.softplus(dt_pre + bias_vec), -jnp.exp(alog_mat).T)


def combine_pairs(earlier, later_map):
    return (earlier[0] * later_map[0], later_map[0] * earlier[1] + later_map[1])


def mixer_tail(delta, a_neg, b_c, u_vals, z_part, skip_vec, start_state, block_rows):
    length = delta.shape[0]
    block_count = length // block_rows

    def mixer_one_block(carry_state, row_values):
        delta_b, b_part, c_part, u_part = row_values
        decay_step = jnp.exp(delta_b[:, None, :] * a_neg[None])
        drive_step = (delta_b * u_part)[:, None, :] * b_part[:, :, None]
        cum_decay, cum_drive = lax.associative_scan(combine_pairs, (decay_step, drive_step), axis=0)
        states = cum_decay * carry_state[None] + cum_drive
        outputs = jnp.sum(states * c_part[:, :, None], axis=1)
        return (states[-1], outputs)

    shaped = tuple(
        (
            v.reshape(block_count, block_rows, v.shape[1])
            for v in (delta, b_c[:, :NS], b_c[:, NS:], u_vals)
        )
    )
    final_state, outputs = lax.scan(jax.checkpoint(mixer_one_block), start_state, shaped)
    ssm_out = outputs.reshape(length, delta.shape[1])
    gated = (ssm_out + skip_vec * u_vals) * jax.nn.silu(z_part)
    return (gated, final_state)


def decay_sum(offsets, weights, coefs, a_neg, block_rows):
    block_count = offsets.shape[0] // block_rows

    def decay_one_block(total, row_values):
        off_b, weight_b, coef_b = row_values
        terms = jnp.exp(off_b[:, None, :] * a_neg[None]) * weight_b[:, None, :] * coef_b[:, :, None]
        return (total + jnp.sum(terms, axis=0), None)

    shaped = tuple(
        (v.reshape(block_count, block_rows, v.shape[1]) for v in (offsets, weights, coefs))
    )
    total, _ = lax.scan(decay_one_block, jnp.zeros(a_neg.shape, jnp.float32), shaped)
    return total


def on_device(
    tokens,
    route,
    cotangent,
    gain_mix,
    w_in,
    conv_w,
    w_x,
    w_dt,
    dt_bias,
    a_log,
    d_skip,
    w_out,
    gain_moe,
    w_up,
    w_down,
):
    gathered = (
        lax.all_gather(gain_mix, ("dp", "seq"), axis=0, tiled=True),
        lax.all_gather(w_in, ("dp", "seq"), axis=0, tiled=True),
        lax.all_gather(conv_w, ("dp", "seq"), axis=0, tiled=True),
        lax.all_gather(w_x, ("dp", "seq"), axis=0, tiled=True),
        lax.all_gather(w_dt, ("dp", "seq"), axis=0, tiled=True),
        lax.all_gather(dt_bias, ("dp", "seq"), axis=0, tiled=True),
        lax.all_gather(a_log, ("dp", "seq"), axis=0, tiled=True),
        lax.all_gather(d_skip, ("dp", "seq"), axis=0, tiled=True),
        lax.all_gather(w_out, ("dp", "seq"), axis=0, tiled=True),
        lax.all_gather(gain_moe, ("dp", "seq"), axis=0, tiled=True),
    )
    (
        gmix_all,
        win_all,
        conv_all,
        wx_all,
        wdt_all,
        bias_all,
        alog_all,
        skip_all,
        wout_all,
        gmoe_all,
    ) = gathered
    up_all, down_all = (w_up, w_down)
    f32 = jnp.float32
    bf16 = jnp.bfloat16
    row_values = tokens.astype(f32)
    normed, norm_pullback = jax.vjp(rms_norm, row_values, gmix_all.astype(f32))
    normed_low = normed.astype(bf16)
    projected = jnp.dot(normed_low, win_all, preferred_element_type=f32)
    x_part = projected[:, :DI]
    z_part = projected[:, DI:]
    tail_prev = from_behind(x_part[-3:], "seq", 1)
    u_vals, conv_pullback = jax.vjp(conv_silu, x_part, tail_prev, conv_all.astype(f32))
    u_low = u_vals.astype(bf16)
    small = jnp.dot(u_low, wx_all, preferred_element_type=f32)
    rank_low = small[:, :RANK].astype(bf16)
    dt_pre = jnp.dot(rank_low, wdt_all.T, preferred_element_type=f32)
    (delta, a_neg), rate_pullback = jax.vjp(
        rates, dt_pre, bias_all.astype(f32), alog_all.astype(f32)
    )
    b_c = small[:, RANK:]
    block_rows = math.gcd(delta.shape[0], 8)
    cum_delta = jnp.cumsum(delta, axis=0)
    decay_all = jnp.exp(a_neg * cum_delta[-1][None, :])
    drive_end = decay_sum(
        cum_delta[-1][None, :] - cum_delta, delta * u_vals, b_c[:, :NS], a_neg, block_rows
    )
    empty_state = jnp.zeros_like(decay_all)

    def pass_forward(turn_index, incoming):
        return from_behind(decay_all * incoming + drive_end, "seq", 1)

    start_state = lax.fori_loop(0, lax.axis_size("seq") - 1, pass_forward, empty_state)
    (gated, final_state), tail_pullback = jax.vjp(
        partial(mixer_tail, block_rows=block_rows),
        delta,
        a_neg,
        b_c,
        u_vals,
        z_part,
        skip_all.astype(f32),
        start_state,
    )
    gated_low = gated.astype(bf16)
    mixer_out = jnp.dot(gated_low, wout_all, preferred_element_type=f32)
    resid = row_values + mixer_out
    normed2, norm2_pullback = jax.vjp(rms_norm, resid, gmoe_all.astype(f32))
    moe_in = normed2.astype(bf16)
    groups = lax.axis_size("dp")
    choose = route[:, 0]
    onehot = (choose[:, None] == jnp.arange(E, dtype=jnp.int32)[None, :]).astype(jnp.int32)
    slot_index = jnp.sum((jnp.cumsum(onehot, axis=0) - 1) * onehot, axis=1)
    target = choose * CAP + slot_index
    send_buffer = jnp.zeros((E * CAP, D), bf16).at[target].set(moe_in)
    received = lax.all_to_all(
        send_buffer.reshape(groups, E // groups, CAP, D),
        "dp",
        split_axis=0,
        concat_axis=0,
        tiled=True,
    )
    slot_rows = lax.all_gather(received, "seq", axis=2, tiled=True)
    pre_act = jnp.einsum("skcd,kfd->skcf", slot_rows, up_all, preferred_element_type=f32)
    hidden_f, gelu_pullback = jax.vjp(partial(jax.nn.gelu, approximate=False), pre_act)
    hidden_low = hidden_f.astype(bf16)
    out_terms = jnp.einsum("skcf,kfd->skcd", hidden_low, down_all, preferred_element_type=f32)
    expert_out = (
        lax.psum_scatter(out_terms.astype(jnp.bfloat16), "seq", scatter_dimension=2, tiled=True)
        .astype(jnp.float32)
        .astype(bf16)
    )
    returned = lax.all_to_all(expert_out, "dp", split_axis=0, concat_axis=0, tiled=True)
    moe_rows = returned.reshape(E * CAP, D)[target]
    result = (resid + moe_rows.astype(f32)).astype(bf16)
    grad_out = cotangent.astype(f32)
    grad_send = jnp.zeros((E * CAP, D), bf16).at[target].set(cotangent)
    grad_expert = lax.all_to_all(
        grad_send.reshape(groups, E // groups, CAP, D),
        "dp",
        split_axis=0,
        concat_axis=0,
        tiled=True,
    )
    grad_expert = lax.all_gather(grad_expert, "seq", axis=2, tiled=True)
    grad_hidden = jnp.einsum("skcd,kfd->skcf", grad_expert, down_all, preferred_element_type=f32)
    grad_down = jnp.einsum("skcf,skcd->kfd", hidden_low, grad_expert, preferred_element_type=f32)
    grad_pre = gelu_pullback(grad_hidden)[0].astype(bf16)
    grad_up = jnp.einsum("skcf,skcd->kfd", grad_pre, slot_rows, preferred_element_type=f32)
    row_terms = jnp.einsum("skcf,kfd->skcd", grad_pre, up_all, preferred_element_type=f32)
    grad_rows_low = lax.psum_scatter(row_terms, "seq", scatter_dimension=2, tiled=True).astype(bf16)
    grad_returned = lax.all_to_all(grad_rows_low, "dp", split_axis=0, concat_axis=0, tiled=True)
    grad_moe_in = grad_returned.reshape(E * CAP, D)[target].astype(f32)
    grad_w_up, grad_w_down = (grad_up, grad_down)
    grad_resid, grad_gmoe = norm2_pullback(grad_moe_in)
    grad_resid = grad_resid + grad_out
    grad_mixed_low = grad_resid.astype(bf16)
    grad_gated = jnp.dot(grad_mixed_low, wout_all.T, preferred_element_type=f32)
    grad_wout = jnp.dot(gated_low.T, grad_mixed_low, preferred_element_type=f32)
    grad_ssm = grad_gated * jax.nn.silu(z_part)
    local_start = decay_sum(cum_delta, grad_ssm, b_c[:, NS:], a_neg, block_rows)

    def pass_backward(turn_index, incoming):
        return from_behind(decay_all * incoming + local_start, "seq", -1)

    grad_final = lax.fori_loop(0, lax.axis_size("seq") - 1, pass_backward, empty_state)
    grad_delta, grad_aneg, grad_bc, grad_u_scan, grad_z, grad_skip, grad_start = tail_pullback(
        (grad_gated, grad_final)
    )
    grad_dt_pre, grad_bias, grad_alog = rate_pullback((grad_delta, grad_aneg))
    grad_dt_low = grad_dt_pre.astype(bf16)
    grad_rank = jnp.dot(grad_dt_low, wdt_all, preferred_element_type=f32)
    grad_wdt = jnp.dot(grad_dt_low.T, rank_low, preferred_element_type=f32)
    grad_small_low = jnp.concatenate([grad_rank, grad_bc], axis=1).astype(bf16)
    grad_u_proj = jnp.dot(grad_small_low, wx_all.T, preferred_element_type=f32)
    grad_wx = jnp.dot(u_low.T, grad_small_low, preferred_element_type=f32)
    grad_xpart, grad_tail, grad_conv = conv_pullback(grad_u_scan + grad_u_proj)
    tail_incoming = from_behind(grad_tail, "seq", -1)
    grad_xpart = grad_xpart.at[-3:].add(tail_incoming)
    grad_proj_low = jnp.concatenate([grad_xpart, grad_z], axis=1).astype(bf16)
    grad_normed = jnp.dot(grad_proj_low, win_all.T, preferred_element_type=f32)
    grad_win = jnp.dot(normed_low.T, grad_proj_low, preferred_element_type=f32)
    grad_row_norm, grad_gmix = norm_pullback(grad_normed)
    grad_tokens = grad_row_norm + grad_resid
    summed = (
        lax.psum_scatter(grad_gmix, ("dp", "seq"), scatter_dimension=0, tiled=True),
        lax.psum_scatter(grad_win, ("dp", "seq"), scatter_dimension=0, tiled=True),
        lax.psum_scatter(grad_conv, ("dp", "seq"), scatter_dimension=0, tiled=True),
        lax.psum_scatter(grad_wx, ("dp", "seq"), scatter_dimension=0, tiled=True),
        lax.psum_scatter(grad_wdt, ("dp", "seq"), scatter_dimension=0, tiled=True),
        lax.psum_scatter(grad_bias, ("dp", "seq"), scatter_dimension=0, tiled=True),
        lax.psum_scatter(grad_alog, ("dp", "seq"), scatter_dimension=0, tiled=True),
        lax.psum_scatter(grad_skip, ("dp", "seq"), scatter_dimension=0, tiled=True),
        lax.psum_scatter(grad_wout, ("dp", "seq"), scatter_dimension=0, tiled=True),
        lax.psum_scatter(grad_gmoe, ("dp", "seq"), scatter_dimension=0, tiled=True),
    )
    return (
        result,
        grad_tokens,
        summed[0],
        summed[1],
        summed[2],
        summed[3],
        summed[4],
        summed[5],
        summed[6],
        summed[7],
        summed[8],
        summed[9],
        grad_w_up,
        grad_w_down,
    )


def solution(mesh):
    placed = (
        P(("dp", "seq"), None),
        P(("dp", "seq"), None),
        P(("dp", "seq"), None),
        P(("dp", "seq")),
        P(("dp", "seq"), None),
        P(("dp", "seq"), None),
        P(("dp", "seq"), None),
        P(("dp", "seq"), None),
        P(("dp", "seq")),
        P(("dp", "seq"), None),
        P(("dp", "seq")),
        P(("dp", "seq"), None),
        P(("dp", "seq")),
        P("dp", "seq", None),
        P("dp", "seq", None),
    )
    return jax.shard_map(
        on_device,
        mesh=mesh,
        in_specs=placed,
        out_specs=(
            P(("dp", "seq"), None),
            P(("dp", "seq"), None),
            P(("dp", "seq")),
            P(("dp", "seq"), None),
            P(("dp", "seq"), None),
            P(("dp", "seq"), None),
            P(("dp", "seq"), None),
            P(("dp", "seq")),
            P(("dp", "seq"), None),
            P(("dp", "seq")),
            P(("dp", "seq"), None),
            P(("dp", "seq")),
            P("dp", "seq", None),
            P("dp", "seq", None),
        ),
        check_vma=False,
    )
```

profile of v0, /device:TPU:0, one launch (start us, length us, event | category | flops | bytes accessed | tf_op | source)
XLA Modules:
  0.0 3550.7 jit_solution(14231210340560168952)
XLA Ops:
  13.3 43.7 %all-reduce.75 = (bf16[2304]{0:T(1024)(128)(2,1)S(1)}, bf16[2304]{0:T(1024)(128)(2,1)}, bf16[1152]{0:T(1024)(128)(2,1)S(1)}, bf16[1152]{0:T(1024)(128)(2,1)S(1)}) all-reduce(bf16[2304]{0:T(1024)(128)(2,1)S(1)} %dynamic-update-slice.5, bf16[2304]{0:T(1024)(128)(2,1)S(1)} %dynamic-update-slice.4, ...), channel_id=1, replica_groups=mesh['dp'=4,'seq'=8] {'dp','seq'}, use_global_device_ids=true, to_apply=%add.61 | all-reduce | flops 6912 | bytes 27648
  57.0 68.3 %all-gather.2 = bf16[32,72,4]{1,2,0:T(4,128)(2,1)S(1)} all-gather(bf16[1,72,4]{1,2,0:T(4,128)(2,1)} %bitcast.343), channel_id=1, replica_groups=mesh['dp'=4,'seq'=8] {'dp','seq'}, dimensions={0}, use_global_device_ids=true | all-gather | bytes 19008 | tf_op jit(solution)/shard_map/all_gather | solution.py:108
  127.0 64.8 %all-gather = bf16[32,72,16]{1,2,0:T(8,128)(2,1)S(1)} all-gather(bf16[1,72,16]{1,2,0:T(8,128)(2,1)S(1)} %bitcast.340), channel_id=1, replica_groups=mesh['dp'=4,'seq'=8] {'dp','seq'}, dimensions={0}, use_global_device_ids=true | all-gather | bytes 76032 | tf_op jit(solution)/shard_map/all_gather | solution.py:112
  192.9 73.8 %all_gather.40 = bf16[2304,104]{1,0:T(8,128)(2,1)} all-gather(bf16[72,104]{1,0:T(8,128)(2,1)S(1)} %copy-done.94), channel_id=1, replica_groups=mesh['dp'=4,'seq'=8] {'dp','seq'}, dimensions={0}, use_global_device_ids=true | all-gather | bytes 494208 | tf_op jit(solution)/shard_map/all_gather | solution.py:109
  266.7 71.7 %all_gather.41 = bf16[2304,72]{1,0:T(8,128)(2,1)} all-gather(bf16[72,72]{1,0:T(8,128)(2,1)S(1)} %copy-done.95), channel_id=1, replica_groups=mesh['dp'=4,'seq'=8] {'dp','seq'}, dimensions={0}, use_global_device_ids=true | all-gather | bytes 342144 | tf_op jit(solution)/shard_map/all_gather | solution.py:110
  338.4 14.0 reshape.335
  352.4 5.9 fusion.93
  359.0 5.4 collective-permute-start.2
  378.9 30.9 while.85
  410.4 57.2 %while.82 = (s32[]{:T(128)}, f32[16,2304]{1,0:T(8,128)S(1)}, f32[16,2304]{1,0:T(8,128)S(1)}, f32[16,2304]{1,0:T(8,128)}, s32[]{:T(128)}) while((s32[]{:T(128)}, f32[16,2304]{1,0:T(8,128)S(1)}, f32[16,2304]{1,0:T(8,128)S(1)}, f32[16,2304]{1,0:T(8,128)}, s32[]{:T(128)}) %tuple.310), condition=%wide.region_6.7_spmd, body=%wide.region_5.6_spmd.sunk | while | flops 73730 | bytes 1179749 | solution.py:159
  417.8 4.4 collective-permute-start
  425.8 4.4 collective-permute-start
  433.7 4.6 collective-permute-start
  442.0 5.3 collective-permute-start
  450.8 5.3 collective-permute-start
  459.7 5.3 collective-permute-start
  468.7 608.0 %while.83 = (s32[]{:T(128)}, f32[16,2304]{1,0:T(8,128)S(1)}, f32[16,8,2304]{2,1,0:T(8,128)}, f32[16,16,2304]{2,1,0:T(8,128)}, f32[16,8,2304]{2,1,0:T(8,128)}, /*...) while((s32[]{:T(128)}, f32[16,2304]{1,0:T(8,128)S(1)}, ...), condition=%wide.region_9.10_spmd, body=%wide.region_7.9_spmd.sunk | while | flops 4755458 | bytes 60312960 | solution.py:67
  537.0 4.2 pad.877
  1084.5 10.2 all_to_all.20
  1096.1 10.2 all_to_all.21
  1106.5 48.5 %all-gather.10.cloned.1.call-done = bf16[4,1,320,1152]{3,2,0,1:T(8,128)(2,1)} async-done(((bf16[4,1,40,1152]{3,2,0,1:T(8,128)(2,1)}), bf16[4,1,320,1152]{3,2,0,1:T(8,128)(2,1)}) %all-gather.10.cloned.1.call-update) | async-done | bytes 2949136 | tf_op jit(solution)/shard_map/all_gather | solution.py:188
  1160.2 5.7 fusion.13
  1170.3 43.5 %all-gather.12.cloned.1.call-done = bf16[4,1,320,1152]{3,2,0,1:T(8,128)(2,1)} async-done(((bf16[4,1,40,1152]{3,2,0,1:T(8,128)(2,1)}), bf16[4,1,320,1152]{3,2,0,1:T(8,128)(2,1)}) %all-gather.12.cloned.1.call-update) | async-done | bytes 2949136 | tf_op jit(solution)/shard_map/all_gather | solution.py:210
  1213.8 9.0 fusion.40
  1222.8 5.8 convolution_bitcast_fusion
  1228.7 60.5 %reduce-scatter.20.cloned.1.call-done = bf16[40,4608]{1,0:T(8,128)(2,1)} async-done(((bf16[320,4608]{1,0:T(8,128)(2,1)}), bf16[40,4608]{1,0:T(8,128)(2,1)}) %reduce-scatter.20.cloned.1.call-update) | async-done | bytes 368656
  1294.5 109.8 %reduce-scatter.18.cloned.1.call-done = f32[4,1,40,1152]{3,2,0,1:T(8,128)} async-done(((f32[4,1,320,1152]{3,2,0,1:T(8,128)}), f32[4,1,40,1152]{3,2,0,1:T(8,128)}) %reduce-scatter.18.cloned.1.call-update) | async-done | bytes 737296 | tf_op jit(solution)/shard_map/reduce_scatter | solution.py:216
  1410.8 5.9 all-to-all-done.3
  1419.3 4.3 fusion.89
  1425.1 30.9 while.86
  1456.6 62.2 %while.84 = (s32[]{:T(128)}, f32[16,2304]{1,0:T(8,128)}, f32[16,2304]{1,0:T(8,128)S(1)}, f32[16,2304]{1,0:T(8,128)S(1)}, s32[]{:T(128)}) while((s32[]{:T(128)}, f32[16,2304]{1,0:T(8,128)}, f32[16,2304]{1,0:T(8,128)S(1)}, f32[16,2304]{1,0:T(8,128)S(1)}, s32[]{:T(128)}) %tuple.309), condition=%wide.region_22.23_spmd, body=%wide.region_21.22_spmd.sunk | while | flops 73730 | bytes 1179749 | solution.py:231
  1458.9 6.0 collective-permute-done.1
  1467.1 6.2 collective-permute-done.1
  1475.5 6.7 collective-permute-done.1
  1484.5 6.7 collective-permute-done.1
  1493.5 6.7 collective-permute-done.1
  1502.5 7.1 collective-permute-done.1
  1511.8 7.0 collective-permute-done.1
  1522.3 1316.4 %while.87 = (s32[]{:T(128)}, f32[16,2304]{1,0:T(8,128)}, f32[16,2304]{1,0:T(8,128)}, f32[16,8,2304]{2,1,0:T(8,128)}, f32[16,8,16]{2,1,0:T(8,128)}, /*index=5*/f3...) while((s32[]{:T(128)}, f32[16,2304]{1,0:T(8,128)}, ...), condition=%wide.region_30.31_spmd.clone, body=%wide.region_23.30_spmd.clone.sunk | while | flops 15593220 | bytes 175857200 | solution.py:67
  2848.7 9.0 convolution_bitcast_fusion.1
  2860.5 5.6 fusion.87
  2867.7 7.0 multiply_reduce_fusion.9
  2881.9 8.9 fusion.60
  2890.8 530.8 %fusion = f32[40,4608]{1,0:T(8,128)S(1)} fusion(f32[1152,4608]{1,0:T(8,128)} %fusion.60), kind=kCustom, calls=%all-reduce-scatter | all-reduce-scatter fusion | flops 5898241 | bytes 21970944
  3426.8 11.9 collective-permute-start.4
  3438.7 8.2 fusion.67
  3446.8 68.1 %all-reduce.74 = (f32[1152]{0:T(1024)S(1)}, f32[2304,4]{0,1:T(4,128)S(1)}, f32[2304]{0:T(1024)S(1)}, f32[2304]{0:T(1024)S(1)}, f32[1152]{0:T(1024)S(1)}) all-reduce(f32[1152]{0:T(1024)} %get-tuple-element.625, f32[2304,4]{0,1:T(4,128)} %pad_add_fusion.13, ...), channel_id=4, replica_groups=mesh['dp'=4,'seq'=8] {'dp','seq'}, use_global_device_ids=true, to_apply=%region_33.34.clone | all-reduce | flops 16128 | bytes 129024
  3524.4 17.1 concatenate.68
  (3589 shorter events, 2117.1 us)
Async XLA Ops:
  7.2 1153.0 %copy-start = (bf16[1,384,1152]{2,1,0:T(8,128)(2,1)S(1)}, bf16[1,384,1152]{2,1,0:T(8,128)(2,1)}, u32[]{:S(2)}) copy-start(bf16[1,384,1152]{2,1,0:T(8,128)(2,1)} %param.43) | copy-start | bytes 2654212
  7.2 119.1 %copy-start.99 = (s32[128,1]{0,1:T(1,128)S(1)}, s32[128,1]{0,1:T(1,128)}, u32[]{:S(2)}) copy-start(s32[128,1]{0,1:T(1,128)} %param.30) | copy-start | bytes 1540
  7.2 119.8 %copy-start.98 = (bf16[72,16]{0,1:T(8,128)(2,1)S(1)}, bf16[72,16]{0,1:T(8,128)(2,1)}, u32[]{:S(2)}) copy-start(bf16[72,16]{0,1:T(8,128)(2,1)} %param.38) | copy-start | bytes 6916
  7.2 331.2 %all-gather.14.cloned.1.call-start = ((), (), s32[]{:S(2)}) async-start(), calls=%async_computation.13 | async-start | bytes 12165120 | tf_op jit(solution)/shard_map/all_gather | solution.py:107
  8.0 1071.5 %all-gather.8.cloned.1.call-start = ((), (), s32[]{:S(2)}) async-start(), calls=%async_computation.9 | async-start | bytes 5474304 | tf_op jit(solution)/shard_map/all_gather | solution.py:114
  8.7 1146.3 %all-gather.10.cloned.1.call-start = ((), (), s32[]{:S(2)}) async-start(), calls=%async_computation.10 | async-start | bytes 3317760 | tf_op jit(solution)/shard_map/all_gather | solution.py:188
  9.9 117.1 %copy-start.100 = (f32[128]{0:T(128)}, f32[128]{0:T(128)S(1)}, u32[]{:S(2)}) copy-start(f32[128]{0:T(128)S(1)} %fusion.72) | copy-start | bytes 1540
  9.9 183.0 %copy-start.94 = (bf16[72,104]{1,0:T(8,128)(2,1)S(1)}, bf16[72,104]{1,0:T(8,128)(2,1)}, u32[]{:S(2)}) copy-start(bf16[72,104]{1,0:T(8,128)(2,1)} %param.35) | copy-start | bytes 44932
  9.9 342.5 %copy-start.92 = (f32[128]{0:T(128)}, f32[128]{0:T(128)S(1)}, u32[]{:S(2)}) copy-start(f32[128]{0:T(128)S(1)} %fusion.97) | copy-start | bytes 1540
  57.0 295.4 %copy-start.77 = (f32[1152]{0:T(1024)}, f32[1152]{0:T(1024)S(1)}, u32[]{:S(2)}) copy-start(f32[1152]{0:T(1024)S(1)} %convert_element_type.82) | copy-start | bytes 13828
  127.0 139.7 %copy-start.95 = (bf16[72,72]{1,0:T(8,128)(2,1)S(1)}, bf16[72,72]{1,0:T(8,128)(2,1)}, u32[]{:S(2)}) copy-start(bf16[72,72]{1,0:T(8,128)(2,1)} %param.36) | copy-start | bytes 31108
  192.2 146.2 %copy-start.70 = (f32[2304,16]{0,1:T(8,128)}, f32[2304,16]{0,1:T(8,128)S(1)}, u32[]{:S(2)}) copy-start(f32[2304,16]{0,1:T(8,128)S(1)} %reshape.340) | copy-start | bytes 442372
  359.0 7.5 collective-permute-start.2
  411.4 5.5 collective-permute-start
  417.8 7.0 collective-permute-start
  425.8 7.0 collective-permute-start
  433.7 7.3 collective-permute-start
  442.0 7.9 collective-permute-start
  450.8 7.9 collective-permute-start
  459.7 7.9 collective-permute-start
  1094.8 119.1 %all-gather.12.cloned.1.call-start = ((), (), s32[]{:S(2)}) async-start(), calls=%async_computation.11 | async-start | bytes 3317760 | tf_op jit(solution)/shard_map/all_gather | solution.py:210
  1106.3 182.8 %reduce-scatter.20.cloned.1.call-start = ((), (), s32[]{:S(2)}) async-start(), calls=%async_computation.14 | async-start | bytes 3317760
  1170.3 234.0 %reduce-scatter.18.cloned.1.call-start = ((), (), s32[]{:S(2)}) async-start(), calls=%async_computation.12 | async-start | bytes 6635520 | tf_op jit(solution)/shard_map/reduce_scatter | solution.py:216
  1291.0 115.1 %all-to-all-start.1 = ((bf16[4,1,40,1152]{3,2,1,0:T(8,128)(2,1)}), bf16[4,1,40,1152]{3,2,1,0:T(8,128)(2,1)S(1)}, u32[]{:S(2)}, u32[]{:S(2)}) async-start(bf16[4,1,40,1152]{3,2,1,0:T(8,128)(2,1)} %bitcast.285), calls=%async_computation.1 | async-start | bytes 737280 | tf_op jit(solution)/shard_map/all_to_all | solution.py:198
  1406.1 10.6 all-to-all-start.3
  1409.6 2113.4 %all-reduce.78.cloned.1.call-start = ((), (), s32[]{:S(2)}) async-start(), calls=%async_computation.15 | async-start | bytes 294912
  1457.6 7.3 collective-permute-start.1
  1465.8 7.5 collective-permute-start.1
  1474.2 8.0 collective-permute-start.1
  1483.2 8.0 collective-permute-start.1
  1492.2 8.0 collective-permute-start.1
  1501.2 8.4 collective-permute-start.1
  1510.5 8.3 collective-permute-start.1
  1528.9 34.1 copy-start.2
  1692.6 34.1 copy-start.2
  1774.9 34.1 copy-start.2
  1857.3 34.1 copy-start.2
  1939.6 34.1 copy-start.2
  2021.9 34.1 copy-start.2
  2843.6 700.1 %reduce-scatter.24.cloned.1.call-start = ((), (), s32[]{:S(2)}) async-start(), calls=%async_computation.17 | async-start | bytes 1216512
  2845.1 698.6 %reduce-scatter.22.cloned.1.call-start = ((), (), s32[]{:S(2)}) async-start(), calls=%async_computation.16 | async-start | bytes 1216512
  2848.3 695.4 %reduce-scatter.26.cloned.1.call-start = ((), (), s32[]{:S(2)}) async-start(), calls=%async_computation.18 | async-start | bytes 10948608
  2874.8 6.7 collective-permute-start.3
  3422.3 99.0 %copy-start.61 = (f32[128,1152]{1,0:T(8,128)S(1)}, f32[128,1152]{1,0:T(8,128)}, u32[]{:S(2)}) copy-start(f32[128,1152]{1,0:T(8,128)} %copy-done.59) | copy-start | bytes 1769476
  3422.3 102.1 %collective-permute-start.6 = (f32[40,4608]{1,0:T(8,128)S(1)}, f32[40,4608]{1,0:T(8,128)S(1)}, u32[]{:S(2)}, u32[]{:S(2)}) collective-permute-start(f32[40,4608]{1,0:T(8,128)S(1)} %fusion), channel_id=1, source_target_pairs={{0,3},{1,4},{2,5},{3,6},{4,7},{5,8},{6,9},{7,10},{8,11},{9,12},{10... | collective-permute-start | bytes 2211848
  3424.6 99.8 %collective-permute-start.5 = (f32[40,4608]{1,0:T(8,128)S(1)}, f32[40,4608]{1,0:T(8,128)}, u32[]{:S(2)}, u32[]{:S(2)}) collective-permute-start(f32[40,4608]{1,0:T(8,128)S(1)} %fusion), channel_id=1, source_target_pairs={{0,2},{1,3},{2,4},{3,5},{4,6},{5,7},{6,8},{7,9},{8,10},{9,11},{10,... | collective-permute-start | bytes 2211848
  3426.8 97.7 %collective-permute-start.4 = (f32[40,4608]{1,0:T(8,128)S(1)}, f32[40,4608]{1,0:T(8,128)}, u32[]{:S(2)}, u32[]{:S(2)}) collective-permute-start(f32[40,4608]{1,0:T(8,128)S(1)} %fusion), channel_id=1, source_target_pairs={{0,1},{1,2},{2,3},{3,4},{4,5},{5,6},{6,7},{7,8},{8,9},{9,10},{10,1... | collective-permute-start | bytes 2211848
  3517.3 7.1 collective-permute-start.7
  (873 other events, 3202.7 us)
Sparse Core Ops, SparseCore 0:
  10.9 95.3 all-gather.13
  109.2 64.4 all-gather.7
  1094.9 60.0 all-gather.9
  1157.1 56.7 all-gather.11
  1217.3 71.8 reduce-scatter.19
  1292.7 111.5 reduce-scatter.17
  2843.7 137.8 all-reduce.77
  2987.3 112.4 reduce-scatter.23
  3105.4 108.7 reduce-scatter.21
  3220.7 243.4 reduce-scatter.25
where the time goes:
time: 3580 us; the launch traced here: 3550 us
  local copies, waits for them, and re-layouts  1340 us (37%)
  blocking collectives  942 us (26%)
  other arithmetic  746 us (21%)
  waiting for transfers between devices  339 us (9%)
  matrix products  83.9 us (2%)
  starting transfers between devices  75.1 us (2%)
    pad x480, local copies, waits for them, and re-layouts, mixer_one_block(): lax.associative_scan(combine_pairs, (decay_step, drive_step), axis=0)  938 us
    unnamed x3, blocking collectives  643 us
    add x128, other arithmetic, mixer_one_block(): lax.associative_scan(combine_pairs, (decay_step, drive_step), axis=0)  159 us
    while x1488, local copies, waits for them, and re-layouts  140 us
    reduce_scatter x1, waiting for transfers between devices, on_device(): lax.psum_scatter(row_terms, 'seq', scatter_dimension=2, tiled=True)  110 us
    concatenate x128, other arithmetic, mixer_one_block(): lax.associative_scan(combine_pairs, (decay_step, drive_step), axis=0)  107 us
    mul x144, other arithmetic, combine_pairs(): return (earlier[0] * later_map[0], later_map[0] * earlier[1] + later_map[1])  102 us
    all_gather x1, blocking collectives, on_device(): lax.all_gather(w_x, ('dp', 'seq'), axis=0, tiled=True)  73.8 us
  transfers between devices with their start and end apart: 32, of which 20 were waited for; matrix products, arithmetic and copies ran while one was open for 37% of the time, Pallas kernels for 0%

commit v1 on v0

v1 whole, which is shorter than its diff:
```python
from functools import partial

import jax
import jax.numpy as jnp
from jax import lax
from jax.experimental import pallas as pl
from jax.experimental.pallas import tpu as pltpu
from jax.sharding import PartitionSpec as P

NS = 16
LN2 = 0.6931471805599453
LOG2E = 1.4426950408889634
eps = 1e-05
f32 = jnp.float32
bf16 = jnp.bfloat16

NN = (((1,), (0,)), ((), ()))
NT = (((1,), (1,)), ((), ()))
TN = (((0,), (0,)), ((), ()))


def mm(left, right, dims=NN):
    return lax.dot_general(left, right, dims, preferred_element_type=f32)


def up128(count):
    return -(-count // 128) * 128


def rms_norm(values, gain_vec):
    return values * lax.rsqrt(jnp.mean(values * values, axis=-1, keepdims=True) + eps) * gain_vec


def sigmoid(v):
    return 1.0 / (1.0 + jnp.exp(-v))


def softplus(v):
    return jnp.maximum(v, 0.0) + jnp.log1p(jnp.exp(-jnp.abs(v)))


def tree_step(first, second, by):
    row = lax.broadcasted_iota(jnp.int32, first.shape, 0)
    clear = (row & by) == 0
    return jnp.where(clear, first, second) + pltpu.roll(jnp.where(clear, second, first), by, 0)


def tree_push(stack, value, falling=False):
    level = 1
    while stack and stack[-1][0] == level:
        other = stack.pop()[1]
        value = tree_step(value, other, level) if falling else tree_step(other, value, level)
        level *= 2
    stack.append((level, value))


def in_kernel(xg, w, cw, wx, x_out, z_out, conv_out, small_out, buf):
    rows, cp = x_out.shape

    @pl.when(pl.program_id(0) == 0)
    def _():
        buf[0:8, :] = jnp.zeros((8, cp), f32)

    @pl.when(pl.program_id(0) > 0)
    def _():
        buf[0:8, :] = buf[rows : rows + 8, :]

    prod = mm(xg[...], w[...])
    x_part = prod[:, :cp]
    x_out[...] = x_part
    z_out[...] = prod[:, cp:]
    buf[8 : 8 + rows, :] = x_part
    conv = x_part * cw[3:4, :]
    for k in range(3):
        conv = conv + buf[5 + k : 5 + k + rows, :] * cw[k : k + 1, :]
    conv_out[...] = conv
    small_out[...] = mm((conv * sigmoid(conv)).astype(bf16), wx[...])


def scan_kernel(
    small, bct, wdtt, vecs, a2, conv, z, wout, dtp_out, h_out, ssm_out, gated_out, part_out,
    delta_s, du_s, state,
):
    rows, cp = conv.shape

    @pl.when(pl.program_id(0) == 0)
    def _():
        state[...] = jnp.zeros_like(state)

    dtp = mm(small[...].astype(bf16), wdtt[...]) + vecs[0:1, :]
    dtp_out[...] = dtp
    delta = softplus(dtp)
    cv = conv[...]
    u = cv * sigmoid(cv)
    delta_s[...] = delta
    du_s[...] = delta * u

    def group(g, h):
        base = pl.multiple_of(g * 8, 8)
        bc = bct[g]
        stack = []
        for t in range(8):
            d = jnp.broadcast_to(delta_s[pl.ds(base + t, 1), :], (NS, cp))
            du = jnp.broadcast_to(du_s[pl.ds(base + t, 1), :], (NS, cp))
            h = jnp.exp2(d * a2[...]) * h + du * bc[:NS, t : t + 1]
            h_out[base + t] = h
            prod = h * bc[NS:, t : t + 1]
            tree_push(stack, prod[:8] + prod[8:])
        ssm_out[pl.ds(base, 8), :] = stack[0][1]
        return h

    state[...] = lax.fori_loop(0, rows // 8, group, state[...])
    zv = z[...]
    gated = (ssm_out[...] + vecs[1:2, :] * u) * (zv * sigmoid(zv))
    low = gated.astype(bf16)
    gated_out[...] = low
    part_out[...] = mm(low, wout[...]).astype(part_out.dtype)


def back_kernel(
    gml, wout, gated, conv, z, ssm, dtp, hs, hlast, bct, small, wdt, vecs, a2,
    rank_out, gbct_out, gu_out, gz_out, gwout, gwdt, ga, gvecs,
    delta_s, du_s, gs_s, r1_s, r2_s, lam_s,
):
    rows, cp = conv.shape
    step = pl.program_id(0)
    last = pl.num_programs(0) - 1

    @pl.when(step == 0)
    def _():
        lam_s[...] = jnp.zeros_like(lam_s)
        gwout[...] = jnp.zeros_like(gwout)
        gwdt[...] = jnp.zeros_like(gwdt)
        ga[...] = jnp.zeros_like(ga)
        gvecs[...] = jnp.zeros_like(gvecs)

    grad_mixed = gml[...]
    gg = mm(grad_mixed, wout[...], NT)
    gwout[...] += mm(gated[...], grad_mixed, TN)
    zv = z[...]
    sz = sigmoid(zv)
    cv = conv[...]
    u = cv * sigmoid(cv)
    skip = vecs[1:2, :]
    gz_out[...] = (gg * (ssm[...] + skip * u) * (sz * (1.0 + zv * (1.0 - sz)))).astype(bf16)
    gs = gg * (zv * sz)
    delta = softplus(dtp[...])
    gs_s[...] = gs
    delta_s[...] = delta
    du_s[...] = delta * u
    lane = lax.broadcasted_iota(jnp.int32, (NS, 128), 1)
    keep_first = jnp.where(step == last, 0.0, 1.0)
    tiles = cp // 128

    def lane_fold(v):
        total = v[:, :128]
        for i in range(1, tiles):
            total = total + v[:, i * 128 : (i + 1) * 128]
        return jnp.sum(total, axis=1, keepdims=True)

    def group(k, carry):
        lamd, acc = carry
        g = rows // 8 - 1 - k
        base = pl.multiple_of(g * 8, 8)
        bc = bct[g]
        stack1, stack2 = [], []
        gb = jnp.zeros((NS, 128), f32)
        gc = jnp.zeros((NS, 128), f32)
        h = hs[base + 7]
        ones, twos = {}, {}
        for t in range(7, -1, -1):
            d = jnp.broadcast_to(delta_s[pl.ds(base + t, 1), :], (NS, cp))
            du = jnp.broadcast_to(du_s[pl.ds(base + t, 1), :], (NS, cp))
            g_s = jnp.broadcast_to(gs_s[pl.ds(base + t, 1), :], (NS, cp))
            if t > 0:
                before = hs[base + t - 1]
            else:
                inside = hs[jnp.maximum(base - 1, 0)]
                before = jnp.where(g == 0, hlast[0] * keep_first, inside)
            lam = lamd + g_s * bc[NS:, t : t + 1]
            gc = jnp.where(lane == t, lane_fold(g_s * h), gc)
            gb = jnp.where(lane == t, lane_fold(lam * du), gb)
            lamd = jnp.exp2(d * a2[...]) * lam
            w = lamd * before
            acc = acc + w * d
            wa = w * a2[...]
            lb = lam * bc[:NS, t : t + 1]
            tree_push(stack1, wa[:8] + wa[8:], True)
            tree_push(stack2, lb[:8] + lb[8:], True)
            h = before
        r1_s[pl.ds(base, 8), :] = stack1[0][1]
        r2_s[pl.ds(base, 8), :] = stack2[0][1]
        gbct_out[g, :NS, :] = gb[:, :8]
        gbct_out[g, NS:, :] = gc[:, :8]
        return lamd, acc

    lamd, acc = lax.fori_loop(0, rows // 8, group, (lam_s[...], jnp.zeros((NS, cp), f32)))
    lam_s[...] = lamd
    ga[...] += acc
    r2 = r2_s[...]
    gu_out[...] = skip * gs + delta * r2
    gdelta = r1_s[...] * LN2 + u * r2
    gdtp = gdelta * sigmoid(dtp[...])
    gvecs[0:1, :] += jnp.sum(gdtp, axis=0, keepdims=True)
    gvecs[1:2, :] += jnp.sum(gs * u, axis=0, keepdims=True)
    low = gdtp.astype(bf16)
    gwdt[...] += mm(low, small[...].astype(bf16), TN)
    rank_out[...] = mm(low, wdt[...])


def out_kernel(
    gsmall, wx, conv, x, gu, gz, xg, w, cw, part_out, gwx, gw, gcw, buf
):
    rows, cp = conv.shape

    @pl.when(pl.program_id(0) == 0)
    def _():
        buf[rows : rows + 8, :] = jnp.zeros((8, cp), f32)
        gwx[...] = jnp.zeros_like(gwx)
        gw[...] = jnp.zeros_like(gw)
        gcw[...] = jnp.zeros_like(gcw)

    @pl.when(pl.program_id(0) > 0)
    def _():
        buf[rows : rows + 8, :] = buf[0:8, :]

    gsl = gsmall[...].astype(bf16)
    cv = conv[...]
    s = sigmoid(cv)
    gwx[...] += mm((cv * s).astype(bf16), gsl, TN)
    gconv = (gu[...] + mm(gsl, wx[...], NT)) * (s * (1.0 + cv * (1.0 - s)))
    buf[0:rows, :] = gconv
    xv = x[...]
    gx = gconv * cw[3:4, :]
    gcw[3:4, :] += jnp.sum(gconv * xv, axis=0, keepdims=True)
    for k in range(3):
        moved = buf[3 - k : 3 - k + rows, :]
        gx = gx + moved * cw[k : k + 1, :]
        gcw[k : k + 1, :] += jnp.sum(moved * xv, axis=0, keepdims=True)
    gp = jnp.concatenate([gx.astype(bf16), gz[...]], axis=1)
    part_out[...] = mm(gp, w[...], NT).astype(part_out.dtype)
    gw[...] += mm(xg[...], gp, TN)


def chunked(kernel, steps, backward, ins, outs, scratch, name):
    def at(i):
        return steps - 1 - i if backward else i

    def spec(shape, rows):
        tail = (0,) * (len(shape) - 1)
        if rows == 0:
            return pl.BlockSpec(shape, lambda i: (0,) + tail)
        if rows < 0:
            return pl.BlockSpec((1,) + shape[1:], lambda i: (jnp.maximum(at(i) * -rows - 1, 0),) + tail)
        return pl.BlockSpec((rows,) + shape[1:], lambda i: (at(i),) + tail)

    return pl.pallas_call(
        kernel,
        grid=(steps,),
        in_specs=[spec(a.shape, r) for a, r in ins],
        out_specs=[spec(s.shape, r) for s, r in outs],
        out_shape=[s for s, _ in outs],
        scratch_shapes=scratch,
        name=name,
        compiler_params=pltpu.CompilerParams(
            dimension_semantics=("arbitrary",), vmem_limit_bytes=60 * 1024 * 1024
        ),
    )(*[a for a, _ in ins])


def on_device(
    tokens, route, cotangent, gain_mix, w_in, conv_w, w_x, w_dt, dt_bias, a_log, d_skip, w_out,
    gain_moe, w_up, w_down,
):
    n_seq, n_dp = lax.axis_size("seq"), lax.axis_size("dp")
    both = ("dp", "seq")
    here, d_model = tokens.shape
    cpd = conv_w.shape[0]
    chans = cpd * n_dp
    cp = up128(chans)
    rank = w_dt.shape[1]
    n_small = w_x.shape[1]
    sp = up128(n_small)
    tall = here * n_seq
    rows_in = w_in.shape[0]
    experts, slots = n_dp, 40

    gains = lax.all_gather(jnp.stack([gain_mix, gain_moe]), both, axis=1, tiled=True).astype(f32)
    gmix_all, gmoe_all = gains[0], gains[1]
    w_cols = w_in.reshape(rows_in, 2, n_dp, n_seq, cpd).transpose(3, 0, 1, 2, 4)
    w_cols = jnp.pad(
        w_cols.reshape(n_seq, rows_in, 2, chans), ((0, 0), (0, 0), (0, 0), (0, cp - chans))
    )
    w_cols = lax.all_to_all(w_cols.reshape(n_seq, rows_in, 2 * cp), "seq", 0, 0, tiled=True)
    w_mine = lax.all_gather(w_cols.reshape(n_seq * rows_in, 2 * cp), "dp", axis=0, tiled=True)
    packed = jnp.concatenate(
        [w_out, w_x, w_dt, conv_w, a_log, dt_bias[:, None], d_skip[:, None]], axis=1
    )
    packed = lax.all_gather(packed, "dp", axis=0, tiled=True)
    packed = jnp.pad(packed, ((0, cp - chans), (0, 0)))
    cuts = [d_model, n_small, rank, 4, NS, 1, 1]
    places = [sum(cuts[:i]) for i in range(len(cuts) + 1)]
    wout_m, wx_m, wdt_m, conv_m, alog_m, bias_m, skip_m = [
        packed[:, a:b] for a, b in zip(places[:-1], places[1:])
    ]
    wx_m = jnp.pad(wx_m, ((0, 0), (0, sp - n_small)))
    wdt_m = jnp.pad(wdt_m, ((0, 0), (0, sp - rank)))
    cw = jnp.pad(conv_m.T.astype(f32), ((0, 4), (0, 0)))
    a_neg = -jnp.exp(alog_m.astype(f32)).T
    a2 = a_neg * LOG2E
    vecs = jnp.pad(jnp.concatenate([bias_m, skip_m], axis=1).T.astype(f32), ((0, 6), (0, 0)))

    row_values = tokens.astype(f32)
    normed, norm_pullback = jax.vjp(rms_norm, row_values, gmix_all)
    normed_low = normed.astype(bf16)
    xg = lax.all_gather(normed_low, "seq", axis=0, tiled=True)
    tb = 128
    steps = tall // tb
    sds = jax.ShapeDtypeStruct
    wide = sds((tall, cp), f32)
    x, z, conv, small = chunked(
        in_kernel, steps, False,
        [(xg, tb), (w_mine, 0), (cw, 0), (wx_m, 0)],
        [(wide, tb), (wide, tb), (wide, tb), (sds((tall, sp), f32), tb)],
        [pltpu.VMEM((tb + 8, cp), f32)], "mix_in",
    )
    small = lax.psum(small, "seq")
    bct = small[:, rank:n_small].reshape(tall // 8, 8, 2 * NS).transpose(0, 2, 1)
    dtp, hs, ssm, gated, part = chunked(
        scan_kernel, steps, False,
        [(small, tb), (bct, tb // 8), (wdt_m.T, 0), (vecs, 0), (a2, 0), (conv, tb), (z, tb),
         (wout_m, 0)],
        [(wide, tb), (sds((tall, NS, cp), f32), tb), (wide, tb), (sds((tall, cp), bf16), tb),
         (sds((tall, d_model), bf16), tb)],
        [pltpu.VMEM((tb, cp), f32), pltpu.VMEM((tb, cp), f32), pltpu.VMEM((NS, cp), f32)],
        "scan_forward",
    )
    mixer_out = lax.psum_scatter(part, "seq", scatter_dimension=0, tiled=True).astype(f32)
    resid = row_values + mixer_out

    normed2, norm2_pullback = jax.vjp(rms_norm, resid, gmoe_all)
    moe_in = normed2.astype(bf16)
    choose = route[:, 0]
    onehot = (choose[:, None] == jnp.arange(experts, dtype=jnp.int32)[None, :]).astype(jnp.int32)
    slot_index = jnp.sum((jnp.cumsum(onehot, axis=0) - 1) * onehot, axis=1)
    target = choose * slots + slot_index
    pick = (target[None, :] == jnp.arange(experts * slots, dtype=jnp.int32)[:, None]).astype(bf16)

    def dispatch(values):
        send = mm(pick, values).astype(bf16).reshape(n_dp, slots, d_model)
        got = lax.all_to_all(send, "dp", 0, 0, tiled=True)
        return lax.all_gather(got.reshape(n_dp * slots, d_model), "seq", axis=0, tiled=True)

    def collect(values):
        got = lax.psum_scatter(values.astype(bf16), "seq", scatter_dimension=0, tiled=True)
        back = lax.all_to_all(got.reshape(n_dp, slots, d_model), "dp", 0, 0, tiled=True)
        return mm(pick, back.reshape(n_dp * slots, d_model), TN)

    up, down = w_up[0], w_down[0]
    grad_slots = dispatch(cotangent)
    grad_hidden = mm(grad_slots, down, NT)
    slot_rows = dispatch(moe_in)
    pre_act = mm(slot_rows, up, NT)
    hidden_f, gelu_pullback = jax.vjp(partial(jax.nn.gelu, approximate=False), pre_act)
    hidden = hidden_f.astype(bf16)
    grad_pre = gelu_pullback(grad_hidden)[0].astype(bf16)
    grad_moe_in = collect(mm(grad_pre, up))
    result = (resid + collect(mm(hidden, down))).astype(bf16)
    grad_down = mm(hidden, grad_slots, TN)
    grad_up = mm(grad_pre, slot_rows, TN)

    grad_resid, grad_gmoe = norm2_pullback(grad_moe_in)
    grad_resid = grad_resid + cotangent.astype(f32)
    gml = lax.all_gather(grad_resid.astype(bf16), "seq", axis=0, tiled=True)
    grad_rank, gbct, gu, gz, gwout, gwdt, ga, gvecs = chunked(
        back_kernel, steps, True,
        [(gml, tb), (wout_m, 0), (gated, tb), (conv, tb), (z, tb), (ssm, tb), (dtp, tb), (hs, tb),
         (hs, -tb), (bct, tb // 8), (small, tb), (wdt_m, 0), (vecs, 0), (a2, 0)],
        [(sds((tall, sp), f32), tb), (sds((tall // 8, 2 * NS, 8), f32), tb // 8), (wide, tb),
         (sds((tall, cp), bf16), tb), (sds((cp, d_model), f32), 0), (sds((cp, sp), f32), 0),
         (sds((NS, cp), f32), 0), (sds((8, cp), f32), 0)],
        [pltpu.VMEM((tb, cp), f32) for _ in range(5)] + [pltpu.VMEM((NS, cp), f32)],
        "scan_backward",
    )
    grad_bc = gbct.transpose(0, 2, 1).reshape(tall, 2 * NS)
    gsmall = jnp.concatenate([grad_rank[:, :rank], grad_bc], axis=1)
    gsmall = lax.psum(jnp.pad(gsmall, ((0, 0), (0, sp - n_small))), "seq")
    gpart, gwx, gw, gcw = chunked(
        out_kernel, steps, True,
        [(gsmall, tb), (wx_m, 0), (conv, tb), (x, tb), (gu, tb), (gz, tb), (xg, tb), (w_mine, 0),
         (cw, 0)],
        [(sds((tall, d_model), bf16), tb), (sds((cp, sp), f32), 0),
         (sds((d_model, 2 * cp), f32), 0), (sds((8, cp), f32), 0)],
        [pltpu.VMEM((tb + 8, cp), f32)], "mix_out",
    )
    grad_normed = lax.psum_scatter(gpart, "seq", scatter_dimension=0, tiled=True).astype(f32)
    grad_row_norm, grad_gmix = norm_pullback(grad_normed)
    grad_tokens = grad_row_norm + grad_resid

    ggains = lax.psum_scatter(
        jnp.stack([grad_gmix, grad_gmoe]), both, scatter_dimension=1, tiled=True
    )
    gw = gw.reshape(d_model, 2, cp)[:, :, :chans].reshape(d_model, 2 * chans).astype(bf16)
    gw = lax.psum_scatter(gw, "dp", scatter_dimension=0, tiled=True)
    gw = lax.all_to_all(gw.reshape(n_seq, rows_in, 2 * chans), "seq", 0, 0, tiled=True)
    gw = gw.reshape(n_seq, rows_in, 2, n_dp, cpd).transpose(1, 2, 3, 0, 4)
    grad_win = gw.reshape(rows_in, 2 * n_dp * n_seq * cpd).astype(f32)
    gpack = jnp.concatenate(
        [gwx[:, :n_small], gwdt[:, :rank], gcw[:4].T, (ga * a_neg).T, gvecs[:2].T], axis=1
    )[:chans]
    gpack = lax.psum_scatter(gpack, "dp", scatter_dimension=0, tiled=True)
    grad_wout = lax.psum_scatter(
        gwout[:chans].astype(bf16), "dp", scatter_dimension=0, tiled=True
    ).astype(f32)
    edges = [p - d_model for p in places[1:]]
    gwx_m, gwdt_m, gconv_m, galog_m, gbias_m, gskip_m = [
        gpack[:, a:b] for a, b in zip(edges[:-1], edges[1:])
    ]
    return (
        result, grad_tokens, ggains[0], grad_win, gconv_m, gwx_m, gwdt_m, gbias_m[:, 0], galog_m,
        gskip_m[:, 0], grad_wout, ggains[1], grad_up[None], grad_down[None],
    )


def solution(mesh):
    row2, row1 = P(("dp", "seq"), None), P(("dp", "seq"))
    mats = P("dp", "seq", None)
    return jax.shard_map(
        on_device,
        mesh=mesh,
        in_specs=(
            row2, row2, row2, row1, row2, row2, row2, row2, row1, row2, row1, row2, row1, mats, mats
        ),
        out_specs=(
            row2, row2, row1, row2, row2, row2, row2, row1, row2, row1, row2, row1, mats, mats
        ),
        check_vma=False,
    )
```

time: 3580 us -> 1020 us (0.28)
  local copies, waits for them, and re-layouts: 1340 us -> 42.6 us
  blocking collectives: 942 us -> 165 us
  other arithmetic: 746 us -> 13.7 us
  waiting for transfers between devices: 339 us -> 617 us
  Pallas kernels: 0 us -> 121 us
  starting transfers between devices: 75.1 us -> 9.94 us
  matrix products: 83.9 us -> 35.5 us
    pad x480 -> x3, local copies, waits for them, and re-layouts: 938 us -> 1.39 us  [the longest x1 0.67 us: on_device(): wx_m = jnp.pad(wx_m, ((0, 0), (0, sp - n_small)))]
    unnamed x3 -> x1, blocking collectives: 643 us -> 39.7 us
    all_gather x4 -> x2, blocking collectives: 279 us -> 73.5 us  [the longest x1 65.7 us: on_device(): lax.all_gather(jnp.stack([gain_mix, gain_moe]), both, axis=1, tiled=True)]
    add x208 -> x1, other arithmetic: 177 us -> 0.01 us  [on_device(): target = choose * slots + slot_index]
    reduce_scatter x1 -> x6, waiting for transfers between devices: 110 us -> 283 us  [the longest x2 118 us: collect(): lax.psum_scatter(values.astype(bf16), 'seq', scatter_dimension=0, tiled=T...]
    reduce_sum x97 -> x0, other arithmetic: 160 us -> none  [the longest x32 73.5 us: mixer_one_block(): outputs = jnp.sum(states * c_part[:, :, None], axis=1)]
    while x1488 -> x0, local copies, waits for them, and re-layouts: 140 us -> none
    psum x0 -> x2, waiting for transfers between devices: none -> 136 us  [the longest x1 69.4 us: on_device(): small = lax.psum(small, 'seq')]
  transfers between devices with their start and end apart: 32 -> 16, of which waited for: 20 -> 13; matrix products, arithmetic and copies ran while one was open for 37% -> 6% of each run, Pallas kernels for 0% -> 2%
where the time goes in v1:
time: 1020 us
  waiting for transfers between devices  617 us (60%)
  blocking collectives  165 us (16%)
  Pallas kernels  121 us (12%)
  local copies, waits for them, and re-layouts  42.6 us (4%)
  matrix products  35.5 us (3%)
  between operations  14.6 us (1%)
  other arithmetic  13.7 us (1%)
    pallas_call x4, Pallas kernels, chunked(): pl.pallas_call(kernel, grid=(steps,), in_specs=[spec(a.shape, r) for a, r...  121 us
    reduce_scatter x2, waiting for transfers between devices, collect(): lax.psum_scatter(values.astype(bf16), 'seq', scatter_dimension=0, tiled=T...  118 us
    all_gather x2, waiting for transfers between devices, dispatch(): lax.all_gather(got.reshape(n_dp * slots, d_model), 'seq', axis=0, tiled=T...  94.5 us
    psum x1, waiting for transfers between devices, on_device(): small = lax.psum(small, 'seq')  69.4 us
    reduce_scatter x1, waiting for transfers between devices, on_device(): lax.psum_scatter(part, 'seq', scatter_dimension=0, tiled=True).astype(f32)  67.9 us
    psum x1, waiting for transfers between devices, on_device(): gsmall = lax.psum(jnp.pad(gsmall, ((0, 0), (0, sp - n_small))), 'seq')  66.4 us
    reduce_scatter x1, waiting for transfers between devices, on_device(): lax.psum_scatter(gpart, 'seq', scatter_dimension=0, tiled=True).astype(f32)  66 us
    all_gather x1, blocking collectives, on_device(): lax.all_gather(jnp.stack([gain_mix, gain_moe]), both, axis=1, tiled=True)  65.7 us
  transfers between devices with their start and end apart: 16, of which 13 were waited for; matrix products, arithmetic and copies ran while one was open for 6% of the time, Pallas kernels for 2%

profile of v1, /device:TPU:0, one launch (start us, length us, event | category | flops | bytes accessed | tf_op | source)
XLA Modules:
  0.0 1019.9 jit_solution(13793568684386330531)
XLA Ops:
  7.2 2.3 reshape.135
  10.5 21.1 %all_to_all.30 = bf16[8,36,768]{2,1,0:T(8,128)(2,1)S(1)} all-to-all(bf16[8,36,768]{2,1,0:T(8,128)(2,1)S(1)} %copy.137), channel_id=1, replica_groups=mesh['dp'=4,'seq'=8] {'seq'}, dimensions={0} | all-to-all | bytes 884736 | tf_op jit(solution)/shard_map/all_to_all | solution.py:294
  32.6 65.7 %all-gather = bf16[32,36,2]{1,2,0:T(2,128)(2,1)S(1)} all-gather(bf16[1,36,2]{1,2,0:T(2,128)(2,1)S(1)} %maximum_bitcast_fusion), channel_id=1, replica_groups=mesh['dp'=4,'seq'=8] {'dp','seq'}, dimensions={0}, use_global_device_ids=true | all-gather | bytes 4752 | tf_op jit(solution)/shard_map/all_gather | solution.py:288
  100.2 7.8 all_gather.24
  109.3 1.5 copy.145.wout
  112.2 35.9 %all-gather.7.cloned.1.call-done.xg = bf16[1024,1152]{1,0:T(8,128)(2,1)} async-done(((bf16[128,1152]{1,0:T(8,128)(2,1)}), bf16[1024,1152]{1,0:T(8,128)(2,1)}) %all-gather.7.cloned.1.call-update) | async-done | bytes 2359312 | tf_op jit(solution)/shard_map/all_gather | solution.py:316
  148.1 8.5 mix_in.1
  158.6 69.4 %all-reduce.12.cloned.1.call-done.small = f32[1024,128]{1,0:T(8,128)} async-done(((f32[1024,128]{1,0:T(8,128)}), f32[1024,128]{1,0:T(8,128)}) %all-reduce.12.cloned.1.call-update) | async-done | bytes 524304 | tf_op jit(solution)/shard_map/psum | solution.py:327
  229.2 2.0 copy.144
  231.2 25.4 %scan_forward.1 = (f32[1024,384]{1,0:T(8,128)}, f32[1024,16,384]{2,1,0:T(8,128)}, f32[1024,384]{1,0:T(8,128)}, bf16[1024,384]{1,0:T(8,128)(2,1)}, bf16[1024,1152]{1,0:T(8,128)(2,1)}) custom-call(f32[1024,128]{1,0:T(8,128)} %all-reduce.12.cloned.1.call-done.small, f32[128,32,8]{2,1,0:T(8,128)} %bitcast.95, bf16[128,384]{1,0:T(8,128)(2,1)} %pad_bitcast_fusion.wdtt, ...), custom_call_target="tpu_custom_call" | custom-call | tf_op jit(solution)/shard_map/scan_forward/pallas_call | solution.py:257
  257.7 67.9 %reduce-scatter.13.cloned.1.call-done = bf16[128,1152]{1,0:T(8,128)(2,1)} async-done(((bf16[1024,1152]{1,0:T(8,128)(2,1)}), bf16[128,1152]{1,0:T(8,128)(2,1)}) %reduce-scatter.13.cloned.1.call-update) | async-done | bytes 294928 | tf_op jit(solution)/shard_map/reduce_scatter | solution.py:338
  328.0 10.2 %all_to_all.31 = bf16[4,40,1152]{2,1,0:T(8,128)(2,1)} all-to-all(bf16[4,40,1152]{2,1,0:T(8,128)(2,1)S(1)} %bitcast.107), channel_id=1, replica_groups=mesh['dp'=4,'seq'=8] {'dp'}, dimensions={0} | all-to-all | bytes 737280 | tf_op jit(solution)/shard_map/all_to_all | solution.py:351
  338.6 10.2 %all_to_all.32 = bf16[4,40,1152]{2,1,0:T(8,128)(2,1)} all-to-all(bf16[4,40,1152]{2,1,0:T(8,128)(2,1)S(1)} %bitcast.108), channel_id=1, replica_groups=mesh['dp'=4,'seq'=8] {'dp'}, dimensions={0} | all-to-all | bytes 737280 | tf_op jit(solution)/shard_map/all_to_all | solution.py:351
  349.1 45.6 %all-gather.11.cloned.1.call-done = bf16[1280,1152]{1,0:T(8,128)(2,1)} async-done(((bf16[160,1152]{1,0:T(8,128)(2,1)}), bf16[1280,1152]{1,0:T(8,128)(2,1)}) %all-gather.11.cloned.1.call-update) | async-done | bytes 2949136 | tf_op jit(solution)/shard_map/all_gather | solution.py:352
  394.7 9.8 multiply_convert_fusion
  404.5 48.9 %all-gather.13.cloned.1.call-done = bf16[1280,1152]{1,0:T(8,128)(2,1)} async-done(((bf16[160,1152]{1,0:T(8,128)(2,1)}), bf16[1280,1152]{1,0:T(8,128)(2,1)}) %all-gather.13.cloned.1.call-update) | async-done | bytes 2949136 | tf_op jit(solution)/shard_map/all_gather | solution.py:352
  453.4 5.3 add_convert_fusion
  459.7 3.4 convolution_convert_fusion
  463.1 71.9 %reduce-scatter.17.cloned.1.call-done = bf16[160,1152]{1,0:T(8,128)(2,1)} async-done(((bf16[1280,1152]{1,0:T(8,128)(2,1)}), bf16[160,1152]{1,0:T(8,128)(2,1)}) %reduce-scatter.17.cloned.1.call-update) | async-done | bytes 368656 | tf_op jit(solution)/shard_map/reduce_scatter | solution.py:355
  535.0 10.6 %all_to_all.33 = bf16[4,40,1152]{2,1,0:T(8,128)(2,1)S(1)} all-to-all(bf16[4,40,1152]{2,1,0:T(8,128)(2,1)} %bitcast.112), channel_id=1, replica_groups=mesh['dp'=4,'seq'=8] {'dp'}, dimensions={0} | all-to-all | bytes 737280 | tf_op jit(solution)/shard_map/all_to_all | solution.py:356
  547.9 49.3 %all-gather.15.cloned.1.call-done.gml = bf16[1024,1152]{1,0:T(8,128)(2,1)} async-done(((bf16[128,1152]{1,0:T(8,128)(2,1)}), bf16[1024,1152]{1,0:T(8,128)(2,1)}) %all-gather.15.cloned.1.call-update) | async-done | bytes 2359312 | tf_op jit(solution)/shard_map/all_gather | solution.py:374
  597.1 70.7 %scan_backward.1 = (f32[1024,128]{1,0:T(8,128)}, f32[128,32,8]{2,1,0:T(8,128)}, f32[1024,384]{1,0:T(8,128)}, bf16[1024,384]{1,0:T(8,128)(2,1)}, f32[384,1152]{1,...) custom-call(bf16[1024,1152]{1,0:T(8,128)(2,1)} %all-gather.15.cloned.1.call-done.gml, ...), custom_call_target="tpu_custom_call" | custom-call | tf_op jit(solution)/shard_map/scan_backward/pallas_call | solution.py:257
  667.9 2.3 copy.148
  671.3 4.6 convolution_convert_fusion.1
  676.2 66.4 %all-reduce.14.cloned.1.call-done.gsmall = f32[1024,128]{1,0:T(8,128)} async-done(((f32[1024,128]{1,0:T(8,128)}), f32[1024,128]{1,0:T(8,128)}) %all-reduce.14.cloned.1.call-update) | async-done | bytes 524304 | tf_op jit(solution)/shard_map/psum | solution.py:387
  742.6 16.3 %mix_out.1 = (bf16[1024,1152]{1,0:T(8,128)(2,1)}, f32[384,128]{1,0:T(8,128)}, f32[1152,768]{1,0:T(8,128)}, f32[8,384]{1,0:T(8,128)}) custom-call(f32[1024,128]{1,0:T(8,128)} %all-reduce.14.cloned.1.call-done.gsmall, bf16[384,128]{1,0:T(8,128)(2,1)} %pad.36.clone.wx, f32[1024,384]{1,0:T(8,128)} %get-tuple-element.36.conv, f32[1024,384]{1,0:T(8,128)} %get-tuple-element.45.x, ...), custom_call_target="tpu_custom_call" | custom-call | tf_op jit(solution)/shard_map/mix_out/pallas_call | solution.py:257
  758.8 2.2 convert.16
  761.1 2.2 copy.159
  763.3 1.4 slice.104
  764.8 1.6 copy.162
  768.8 2.3 slice.129
  771.7 46.5 %reduce-scatter.15.cloned.1.call-done = bf16[160,1152]{1,0:T(8,128)(2,1)} async-done(((bf16[1280,1152]{1,0:T(8,128)(2,1)}), bf16[160,1152]{1,0:T(8,128)(2,1)}) %reduce-scatter.15.cloned.1.call-update) | async-done | bytes 368656 | tf_op jit(solution)/shard_map/reduce_scatter | solution.py:355
  818.2 3.5 all-to-all-start.2
  821.7 4.9 convolution_bitcast_fusion
  826.6 21.3 %reduce-scatter.23.cloned.1.call-done = bf16[288,576]{1,0:T(8,128)(2,1)} async-done(((bf16[1152,576]{1,0:T(8,128)(2,1)}), bf16[288,576]{1,0:T(8,128)(2,1)}) %reduce-scatter.23.cloned.1.call-update) | async-done | bytes 331792 | tf_op jit(solution)/shard_map/reduce_scatter | solution.py:404
  847.9 1.8 reshape.152
  849.8 5.5 all-to-all-start.5
  855.3 4.6 convolution_bitcast_fusion.1
  861.5 9.6 reduce-scatter.21.cloned.1.call-done
  874.1 1.6 slice.108
  875.7 1.4 slice.107
  877.1 1.6 slice_reduce_fusion
  878.6 17.9 %reduce-scatter.25.cloned.1.call-done = bf16[72,1152]{1,0:T(8,128)(2,1)} async-done(((bf16[288,1152]{1,0:T(8,128)(2,1)}), bf16[72,1152]{1,0:T(8,128)(2,1)}) %reduce-scatter.25.cloned.1.call-update) | async-done | bytes 165904
  896.6 1.7 convert_element_type.118
  900.7 2.9 reshape.153
  903.6 66.0 %reduce-scatter.19.cloned.1.call-done = bf16[128,1152]{1,0:T(8,128)(2,1)} async-done(((bf16[1024,1152]{1,0:T(8,128)(2,1)}), bf16[128,1152]{1,0:T(8,128)(2,1)}) %reduce-scatter.19.cloned.1.call-update) | async-done | bytes 294928 | tf_op jit(solution)/shard_map/reduce_scatter | solution.py:396
  970.9 39.7 %all-reduce.7 = f32[2,1152]{1,0:T(2,128)S(1)} all-reduce(f32[2,1152]{1,0:T(2,128)S(1)} %pad_maximum_fusion), channel_id=6, replica_groups=mesh['dp'=4,'seq'=8] {'dp','seq'}, use_global_device_ids=true, to_apply=%region_14.15.clone | all-reduce | flops 2304 | bytes 18432
  1011.2 2.2 fusion.20
  (174 shorter events, 30.0 us)
Async XLA Ops:
  7.2 387.5 %copy-start = (bf16[1,384,1152]{2,1,0:T(8,128)(2,1)S(1)}, bf16[1,384,1152]{2,1,0:T(8,128)(2,1)}, u32[]{:S(2)}) copy-start(bf16[1,384,1152]{2,1,0:T(8,128)(2,1)} %param.28) | copy-start | bytes 2654212
  7.2 105.0 %all-gather.9.cloned.1.call-start = ((), (), s32[]{:S(2)}) async-start(), calls=%async_computation.14 | async-start | bytes 2211840 | tf_op jit(solution)/shard_map/all_gather | solution.py:295
  10.3 22.3 %copy-start.34 = (bf16[36]{0:T(256)(128)(2,1)S(1)}, bf16[36]{0:T(256)(128)(2,1)}, u32[]{:S(2)}) copy-start(bf16[36]{0:T(256)(128)(2,1)} %param.27) | copy-start | bytes 220
  10.3 22.3 %copy-start.35 = (bf16[36]{0:T(256)(128)(2,1)S(1)}, bf16[36]{0:T(256)(128)(2,1)}, u32[]{:S(2)}) copy-start(bf16[36]{0:T(256)(128)(2,1)} %param.18) | copy-start | bytes 220
  10.3 88.2 %copy-start.2 = (bf16[128,1152]{1,0:T(8,128)(2,1)S(1)}, bf16[128,1152]{1,0:T(8,128)(2,1)}, u32[]{:S(2)}) copy-start(bf16[128,1152]{1,0:T(8,128)(2,1)} %param.15) | copy-start | bytes 884740
  10.4 89.1 %copy-start.27 = (bf16[72,4]{0,1:T(4,128)(2,1)S(1)}, bf16[72,4]{0,1:T(4,128)(2,1)}, u32[]{:S(2)}) copy-start(bf16[72,4]{0,1:T(4,128)(2,1)} %param.20) | copy-start | bytes 1732
  10.5 89.2 %copy-start.30 = (bf16[72]{0:T(256)(128)(2,1)S(1)}, bf16[72]{0:T(256)(128)(2,1)}, u32[]{:S(2)}) copy-start(bf16[72]{0:T(256)(128)(2,1)} %param.23) | copy-start | bytes 436
  10.5 89.3 %copy-start.22 = (bf16[72,16]{0,1:T(8,128)(2,1)S(1)}, bf16[72,16]{0,1:T(8,128)(2,1)}, u32[]{:S(2)}) copy-start(bf16[72,16]{0,1:T(8,128)(2,1)} %param.24) | copy-start | bytes 6916
  10.5 89.4 %copy-start.31 = (bf16[72]{0:T(256)(128)(2,1)S(1)}, bf16[72]{0:T(256)(128)(2,1)}, u32[]{:S(2)}) copy-start(bf16[72]{0:T(256)(128)(2,1)} %param.25) | copy-start | bytes 436
  10.5 89.6 %copy-start.10 = (bf16[72,1152]{1,0:T(8,128)(2,1)S(1)}, bf16[72,1152]{1,0:T(8,128)(2,1)}, u32[]{:S(2)}) copy-start(bf16[72,1152]{1,0:T(8,128)(2,1)} %param.26) | copy-start | bytes 497668
  10.5 89.6 %copy-start.14 = (bf16[72,104]{1,0:T(8,128)(2,1)S(1)}, bf16[72,104]{1,0:T(8,128)(2,1)}, u32[]{:S(2)}) copy-start(bf16[72,104]{1,0:T(8,128)(2,1)} %param.21) | copy-start | bytes 44932
  10.5 89.6 %copy-start.15 = (bf16[72,72]{1,0:T(8,128)(2,1)S(1)}, bf16[72,72]{1,0:T(8,128)(2,1)}, u32[]{:S(2)}) copy-start(bf16[72,72]{1,0:T(8,128)(2,1)} %param.22) | copy-start | bytes 31108
  32.5 115.6 %all-gather.7.cloned.1.call-start = ((), (), s32[]{:S(2)}) async-start(), calls=%async_computation.13 | async-start | bytes 2654208 | tf_op jit(solution)/shard_map/all_gather | solution.py:316
  99.5 128.5 %all-reduce.12.cloned.1.call-start = ((), (), s32[]{:S(2)}) async-start(), calls=%async_computation.15 | async-start | bytes 1048576 | tf_op jit(solution)/shard_map/psum | solution.py:327
  156.6 169.0 %reduce-scatter.13.cloned.1.call-start = ((), (), s32[]{:S(2)}) async-start(), calls=%async_computation.16 | async-start | bytes 2654208 | tf_op jit(solution)/shard_map/reduce_scatter | solution.py:338
  256.6 81.7 %copy-start.4 = (bf16[128,1152]{1,0:T(8,128)(2,1)S(1)}, bf16[128,1152]{1,0:T(8,128)(2,1)}, u32[]{:S(2)}) copy-start(bf16[128,1152]{1,0:T(8,128)(2,1)} %param.17) | copy-start | bytes 884740
  256.6 138.1 %all-gather.11.cloned.1.call-start = ((), (), s32[]{:S(2)}) async-start(), calls=%async_computation.17 | async-start | bytes 3317760 | tf_op jit(solution)/shard_map/all_gather | solution.py:352
  257.7 287.9 %copy-start.16 = (s32[128]{0:T(128)}, s32[128]{0:T(128)S(1)}, u32[]{:S(2)}) copy-start(s32[128]{0:T(128)S(1)} %multiply_add_fusion.1) | copy-start | bytes 1540
  326.7 219.3 %copy-start.18 = (f32[128]{0:T(128)}, f32[128]{0:T(128)S(1)}, u32[]{:S(2)}) copy-start(f32[128]{0:T(128)S(1)} %fusion.35) | copy-start | bytes 1540
  338.3 115.1 %all-gather.13.cloned.1.call-start = ((), (), s32[]{:S(2)}) async-start(), calls=%async_computation.19 | async-start | bytes 3317760 | tf_op jit(solution)/shard_map/all_gather | solution.py:352
  348.9 104.5 %copy-start.32 = (bf16[1,384,1152]{2,1,0:T(8,128)(2,1)S(1)}, bf16[1,384,1152]{2,1,0:T(8,128)(2,1)}, u32[]{:S(2)}) copy-start(bf16[1,384,1152]{2,1,0:T(8,128)(2,1)} %param.29) | copy-start | bytes 2654212
  348.9 186.1 %reduce-scatter.17.cloned.1.call-start = ((), (), s32[]{:S(2)}) async-start(), calls=%async_computation.20 | async-start | bytes 3317760 | tf_op jit(solution)/shard_map/reduce_scatter | solution.py:355
  463.0 82.5 %copy-start.3 = (bf16[128,1152]{1,0:T(8,128)(2,1)S(1)}, bf16[128,1152]{1,0:T(8,128)(2,1)}, u32[]{:S(2)}) copy-start(bf16[128,1152]{1,0:T(8,128)(2,1)} %reduce-scatter.13.cloned.1.call-done) | copy-start | bytes 884740
  463.0 134.1 %all-gather.15.cloned.1.call-start = ((), (), s32[]{:S(2)}) async-start(), calls=%async_computation.21 | async-start | bytes 2654208 | tf_op jit(solution)/shard_map/all_gather | solution.py:374
  546.0 121.9 %copy-start.5 = (f32[128,1152]{1,0:T(8,128)}, f32[128,1152]{1,0:T(8,128)S(1)}, u32[]{:S(2)}) copy-start(f32[128,1152]{1,0:T(8,128)S(1)} %get-tuple-element.155) | copy-start | bytes 1769476
  546.0 121.9 %copy-start.25 = (f32[128]{0:T(128)}, f32[128]{0:T(128)S(1)}, u32[]{:S(2)}) copy-start(f32[128]{0:T(128)S(1)} %multiply_multiply_fusion.6) | copy-start | bytes 1540
  547.0 195.6 %all-reduce.14.cloned.1.call-start = ((), (), s32[]{:S(2)}) async-start(), calls=%async_computation.22 | async-start | bytes 1048576 | tf_op jit(solution)/shard_map/psum | solution.py:387
  667.9 3.4 copy-start.33
  671.2 147.0 %reduce-scatter.15.cloned.1.call-start = ((), (), s32[]{:S(2)}) async-start(), calls=%async_computation.18 | async-start | bytes 3317760 | tf_op jit(solution)/shard_map/reduce_scatter | solution.py:355
  675.9 172.0 %reduce-scatter.23.cloned.1.call-start = ((), (), s32[]{:S(2)}) async-start(), calls=%async_computation.25 | async-start | bytes 1843200 | tf_op jit(solution)/shard_map/reduce_scatter | solution.py:404
  764.7 2.5 copy-start.11
  764.7 2.8 copy-start.23
  764.8 2.9 copy-start.8
  764.8 2.9 copy-start.9
  766.5 104.6 %reduce-scatter.21.cloned.1.call-start = ((), (), s32[]{:S(2)}) async-start(), calls=%async_computation.24 | async-start | bytes 368640 | tf_op jit(solution)/shard_map/reduce_scatter | solution.py:411
  768.8 127.8 %reduce-scatter.25.cloned.1.call-start = ((), (), s32[]{:S(2)}) async-start(), calls=%async_computation.26 | async-start | bytes 829440
  771.1 198.5 %reduce-scatter.19.cloned.1.call-start = ((), (), s32[]{:S(2)}) async-start(), calls=%async_computation.23 | async-start | bytes 2654208 | tf_op jit(solution)/shard_map/reduce_scatter | solution.py:396
  818.2 31.5 %all-to-all-start.2 = ((bf16[4,40,1152]{2,1,0:T(8,128)(2,1)}), bf16[4,40,1152]{2,1,0:T(8,128)(2,1)S(1)}, u32[]{:S(2)}, u32[]{:S(2)}) async-start(bf16[4,40,1152]{2,1,0:T(8,128)(2,1)} %bitcast.111), calls=%async_computation.4 | async-start | bytes 737280 | tf_op jit(solution)/shard_map/all_to_all | solution.py:356
  821.7 33.6 %copy-start.37 = (bf16[1280,384]{1,0:T(8,128)(2,1)S(1)}, bf16[1280,384]{1,0:T(8,128)(2,1)}, u32[]{:S(2)}) copy-start(bf16[1280,384]{1,0:T(8,128)(2,1)} %copy-done.36) | copy-start | bytes 2949124
  849.8 48.5 %all-to-all-start.5 = ((bf16[8,36,576]{2,1,0:T(8,128)(2,1)}), bf16[8,36,576]{2,1,0:T(8,128)(2,1)S(1)}, u32[]{:S(2)}, u32[]{:S(2)}) async-start(bf16[8,36,576]{2,1,0:T(8,128)(2,1)} %reshape.152), calls=%async_computation.9 | async-start | bytes 819200 | tf_op jit(solution)/shard_map/all_to_all | solution.py:405
  855.3 5.2 copy-start.17
  899.4 111.7 %copy-start.6 = (f32[128,1152]{1,0:T(8,128)S(1)}, f32[128,1152]{1,0:T(8,128)}, u32[]{:S(2)}) copy-start(f32[128,1152]{1,0:T(8,128)} %copy-done.5) | copy-start | bytes 1769476
  900.7 70.2 %copy-start.13 = (f32[1,1152]{1,0:T(1,128)S(1)}, f32[1,1152]{1,0:T(1,128)}, u32[]{:S(2)}) copy-start(f32[1,1152]{1,0:T(1,128)} %reshape.150) | copy-start | bytes 13828
  900.7 109.9 %copy-start.29 = (f32[128]{0:T(128)S(1)}, f32[128]{0:T(128)}, u32[]{:S(2)}) copy-start(f32[128]{0:T(128)} %copy-done.28) | copy-start | bytes 1540
  900.7 110.5 %copy-start.19 = (f32[128]{0:T(128)S(1)}, f32[128]{0:T(128)}, u32[]{:S(2)}) copy-start(f32[128]{0:T(128)} %copy-done.18) | copy-start | bytes 1540
  900.7 110.5 %copy-start.21 = (f32[128]{0:T(128)S(1)}, f32[128]{0:T(128)}, u32[]{:S(2)}) copy-start(f32[128]{0:T(128)} %copy-done.20) | copy-start | bytes 1540
  900.7 110.5 %copy-start.26 = (f32[128]{0:T(128)S(1)}, f32[128]{0:T(128)}, u32[]{:S(2)}) copy-start(f32[128]{0:T(128)} %copy-done.25) | copy-start | bytes 1540
  900.7 112.7 %copy-start.1 = (bf16[1,384,1152]{2,1,0:T(8,128)(2,1)S(1)}, bf16[1,384,1152]{2,1,0:T(8,128)(2,1)}, u32[]{:S(2)}) copy-start(bf16[1,384,1152]{2,1,0:T(8,128)(2,1)} %param.28) | copy-start | bytes 2654212
  (6 other events, 9.0 us)
Sparse Core Ops, SparseCore 0:
  32.6 19.7 all-gather.8
  99.6 48.4 all-gather.6
  156.8 71.1 all-reduce.11
  256.7 68.8 reduce-scatter.12
  338.4 56.2 all-gather.10
  396.8 56.5 all-gather.12
  463.2 71.7 reduce-scatter.16
  547.1 49.9 all-gather.14
  671.4 71.1 all-reduce.13
  746.0 72.1 reduce-scatter.14
  821.4 26.4 reduce-scatter.22
  850.8 20.2 reduce-scatter.20
  874.2 22.2 reduce-scatter.24
  899.9 69.6 reduce-scatter.18

commit v2 on v1

--- a/solution.py
+++ b/solution.py
@@ -268,6 +268,394 @@
     )(*[a for a, _ in ins])
 
 
+MESH = pl.DeviceIdType.MESH
+
+
+def remote(src, dst, send, recv, **where):
+    return pltpu.make_async_remote_copy(
+        src_ref=src, dst_ref=dst, send_sem=send, recv_sem=recv, device_id=where, device_id_type=MESH
+    )
+
+
+class Line:
+    def __init__(self, n_seq):
+        assert n_seq % 2 == 0
+        self.n = n_seq // 2
+        self.n_seq = n_seq
+        self.me = lax.axis_index("seq")
+        self.o, self.i = self.me // 2, self.me % 2
+
+    def at(self, o, i):
+        return o * 2 + i
+
+    def neighbours(self):
+        return [
+            (None, self.at(self.o, 1 - self.i)),
+            (self.o > 0, self.at(self.o - 1, self.i)),
+            (self.o < self.n - 1, self.at(self.o + 1, self.i)),
+        ]
+
+    def order(self, t):
+        table = [
+            sorted(range(self.n), key=lambda q, o=o: (-abs(q - o), -q))[t] for o in range(self.n)
+        ]
+        place = jnp.int32(0)
+        for o in range(self.n):
+            place = place + jnp.where(self.o == o, table[o], 0)
+        return place
+
+
+def when(condition, action):
+    if condition is None:
+        action()
+    else:
+        pl.when(condition)(action)
+
+
+def greet(peers, extra=()):
+    barrier = pltpu.get_barrier_semaphore()
+    count = jnp.int32(0)
+    for condition, place in peers:
+        when(
+            condition,
+            lambda place=place: pl.semaphore_signal(
+                barrier, inc=1, device_id={"seq": place}, device_id_type=MESH
+            ),
+        )
+        count = count + (1 if condition is None else jnp.where(condition, 1, 0))
+    for place in extra:
+        pl.semaphore_signal(barrier, inc=1, device_id={"dp": place}, device_id_type=MESH)
+        count = count + 1
+    pl.semaphore_wait(barrier, count)
+
+
+def gather_sems(n, pieces):
+    dma = pltpu.SemaphoreType.DMA
+    return [dma((n, pieces)), dma((pieces,)), dma((n, pieces)), dma((n, pieces)), dma((n, pieces))]
+
+
+def gather(line, out, own, pieces, sems, ready=None):
+    zs, zd, zr, ys, yr = sems
+    sent = []
+    o, i, n = line.o, line.i, line.n
+
+    def go(condition, copy):
+        when(condition, lambda: copy.start())
+        sent.append((condition, copy))
+
+    def both(a, b):
+        return b if a is None else jnp.logical_and(a, b)
+
+    def spread(condition, src, p, q, up, down, down_sem):
+        slot = line.at(q, i)
+        if up:
+            go(both(condition, o < n - 1),
+               remote(src, out.at[slot, p], zs.at[q, p], zr.at[q, p], seq=line.at(o + 1, i)))
+        if down:
+            go(both(condition, o > 0),
+               remote(src, out.at[slot, p], down_sem, zr.at[q, p], seq=line.at(o - 1, i)))
+        go(condition, remote(src, out.at[slot, p], ys.at[q, p], yr.at[q, p], seq=line.at(o, 1 - i)))
+
+    for p in pieces:
+        if ready is not None:
+            ready(p)
+        spread(None, own(p), p, o, True, True, zd.at[p])
+    for k in range(1, n):
+        for p in pieces:
+            for q, condition, up in ((o - k, o >= k, True), (o + k, o + k <= n - 1, False)):
+                here = out.at[line.at(q, i), p]
+
+                def arrive(here=here, q=q, p=p):
+                    remote(here, here, zs.at[q, p], zr.at[q, p], seq=line.at(o, 1 - i)).wait_recv()
+
+                when(condition, arrive)
+                spread(condition, here, p, q, up, not up, zs.at[q, p])
+    for q in range(n):
+        for p in pieces:
+            here = out.at[line.at(q, 1 - i), p]
+            remote(here, here, ys.at[q, p], yr.at[q, p], seq=line.at(o, 1 - i)).wait_recv()
+    for condition, copy in sent:
+        when(condition, lambda copy=copy: copy.wait_send())
+
+
+def gather_kernel(n_seq, x, out, lsem, *sems):
+    line = Line(n_seq)
+    greet(line.neighbours())
+    keep = pltpu.make_async_copy(x, out.at[line.me], lsem)
+    keep.start()
+    gather(line, out, lambda p: x.at[p], range(x.shape[0]), sems)
+    keep.wait()
+
+
+def seq_gather(x, n_seq, pieces, number):
+    rows, width = x.shape
+    out = pl.pallas_call(
+        partial(gather_kernel, n_seq),
+        in_specs=[pl.BlockSpec(memory_space=pl.ANY)],
+        out_specs=pl.BlockSpec(memory_space=pl.ANY),
+        out_shape=jax.ShapeDtypeStruct((n_seq, pieces, rows // pieces, width), x.dtype),
+        scratch_shapes=[pltpu.SemaphoreType.DMA] + gather_sems(n_seq // 2, pieces),
+        compiler_params=pltpu.CompilerParams(collective_id=number, has_side_effects=True),
+        name="seq_gather",
+    )(x.reshape(pieces, rows // pieces, width))
+    return out.reshape(n_seq * rows, width)
+
+
+def dispatch_kernel(n_seq, n_dp, x, out, lsem, dps, dpr, *sems):
+    line = Line(n_seq)
+    mine = lax.axis_index("dp")
+    peers = [lax.rem(mine + r, n_dp) for r in range(1, n_dp)]
+    greet(line.neighbours(), peers)
+    copies = []
+    for r, peer in enumerate(peers):
+        copy = remote(x.at[peer], out.at[line.me, mine], dps.at[r], dpr.at[r], dp=peer)
+        copy.start()
+        copies.append(copy)
+    keep = pltpu.make_async_copy(x.at[mine], out.at[line.me, mine], lsem)
+    keep.start()
+
+    def ready(r):
+        if r == 0:
+            keep.wait()
+        else:
+            source = out.at[line.me, lax.rem(mine + n_dp - r, n_dp)]
+            remote(source, source, dps.at[r - 1], dpr.at[r - 1], dp=peers[r - 1]).wait_recv()
+
+    gather_rolled(line, out, mine, n_dp, sems, ready)
+    for copy in copies:
+        copy.wait_send()
+
+
+class Rolled:
+    def __init__(self, out, mine, n_dp):
+        self.out, self.mine, self.n_dp = out, mine, n_dp
+
+    @property
+    def at(self):
+        return self
+
+    def __getitem__(self, key):
+        slot, r = key
+        return self.out.at[slot, lax.rem(self.mine + self.n_dp - r, self.n_dp)]
+
+
+def gather_rolled(line, out, mine, n_dp, sems, ready):
+    view = Rolled(out, mine, n_dp)
+    gather(line, view, lambda r: view.at[line.me, r], range(n_dp), sems, ready)
+
+
+def dispatch_call(x, n_seq, number):
+    n_dp, rows, width = x.shape
+    dma = pltpu.SemaphoreType.DMA
+    return pl.pallas_call(
+        partial(dispatch_kernel, n_seq, n_dp),
+        in_specs=[pl.BlockSpec(memory_space=pl.ANY)],
+        out_specs=pl.BlockSpec(memory_space=pl.ANY),
+        out_shape=jax.ShapeDtypeStruct((n_seq, n_dp, rows, width), x.dtype),
+        scratch_shapes=[dma, dma((n_dp - 1,)), dma((n_dp - 1,))] + gather_sems(n_seq // 2, n_dp),
+        compiler_params=pltpu.CompilerParams(collective_id=number, has_side_effects=True),
+        name="dispatch",
+    )(x)
+
+
+def scatter_scratch(n, pieces, rows, width):
+    dma = pltpu.SemaphoreType.DMA
+    return [
+        pltpu.VMEM((n, pieces, rows, width), bf16),
+        pltpu.VMEM((n, pieces, rows, width), bf16),
+        pltpu.VMEM((n + 1, pieces, rows, width), bf16),
+        dma((n, pieces)), dma((n, pieces)), dma((n, pieces)), dma((n + 1, pieces)),
+    ]
+
+
+def scatter(line, term, pieces, scratch, final):
+    ybuf, zout, zin, ys, yr, zs, zr = scratch
+    o, i, n = line.o, line.i, line.n
+    sent = []
+    orders = [line.order(t) for t in range(n)]
+    for q in orders:
+        for p in pieces:
+            copy = remote(term.at[line.at(q, 1 - i), p], ybuf.at[q, p], ys.at[q, p], yr.at[q, p],
+                          seq=line.at(o, 1 - i))
+            copy.start()
+            sent.append(copy)
+
+    def arrived(k, p):
+        remote(zin.at[k, p], zin.at[k, p], zs.at[0, p], zr.at[k, p], seq=line.at(o, 1 - i)).wait_recv()
+
+    for t, q in enumerate(orders):
+        for p in pieces:
+            remote(ybuf.at[q, p], ybuf.at[q, p], ys.at[q, p], yr.at[q, p],
+                   seq=line.at(o, 1 - i)).wait_recv()
+            value = term[line.at(q, i), p].astype(f32) + ybuf[q, p].astype(f32)
+            if t < n - 1:
+                up = q > o
+                fed = jnp.where(up, o > 0, o < n - 1)
+
+                def with_feed(q=q, p=p, value=value):
+                    arrived(q, p)
+                    zout[q, p] = (value + zin[q, p].astype(f32)).astype(bf16)
+
+                def without(q=q, p=p, value=value):
+                    zout[q, p] = value.astype(bf16)
+
+                pl.when(fed)(with_feed)
+                pl.when(jnp.logical_not(fed))(without)
+                to = jnp.where(up, o + 1, o - 1)
+                slot = jnp.where(jnp.logical_and(q == to, jnp.logical_not(up)), n, q)
+                copy = remote(zout.at[q, p], zin.at[slot, p], zs.at[q, p], zr.at[slot, p],
+                              seq=line.at(to, i))
+                copy.start()
+                sent.append(copy)
+            else:
+                below, above = o > 0, o < n - 1
+                pl.when(below)(lambda p=p: arrived(o, p))
+                pl.when(above)(lambda p=p: arrived(n, p))
+                value = value + jnp.where(below, zin[o, p].astype(f32), 0.0)
+                value = value + jnp.where(above, zin[n, p].astype(f32), 0.0)
+                final(p, value)
+    for copy in sent:
+        copy.wait_send()
+
+
+def scatter_kernel(n_seq, term, out, *scratch):
+    line = Line(n_seq)
+    greet(line.neighbours())
+
+    def final(p, value):
+        out[p] = value
+
+    scatter(line, term, range(term.shape[1]), scratch, final)
+
+
+def seq_scatter(x, n_seq, pieces, number):
+    rows, width = x.shape[0] // n_seq, x.shape[1]
+    part = rows // pieces
+    vmem = pl.BlockSpec(memory_space=pltpu.VMEM)
+    out = pl.pallas_call(
+        partial(scatter_kernel, n_seq),
+        in_specs=[vmem],
+        out_specs=vmem,
+        out_shape=jax.ShapeDtypeStruct((pieces, part, width), f32),
+        scratch_shapes=scatter_scratch(n_seq // 2, pieces, part, width),
+        compiler_params=pltpu.CompilerParams(
+            collective_id=number, has_side_effects=True, vmem_limit_bytes=60 * 1024 * 1024
+        ),
+        name="seq_scatter",
+    )(x.reshape(n_seq, pieces, part, width))
+    return out.reshape(rows, width)
+
+
+def collect_kernel(n_seq, n_dp, term, out, sumbuf, lsem, dps, dpr, *scratch):
+    line = Line(n_seq)
+    mine = lax.axis_index("dp")
+    peers = [lax.rem(mine + r, n_dp) for r in range(1, n_dp)]
+    greet(line.neighbours(), peers)
+    copies = []
+    view = RolledTerm(term, mine, n_dp)
+
+    def final(r, value):
+        sumbuf[r] = value.astype(bf16)
+        if r == 0:
+            copy = pltpu.make_async_copy(sumbuf.at[0], out.at[mine], lsem)
+        else:
+            copy = remote(sumbuf.at[r], out.at[mine], dps.at[r - 1], dpr.at[r - 1], dp=peers[r - 1])
+        copy.start()
+        copies.append(copy)
+
+    scatter(line, view, list(range(1, n_dp)) + [0], scratch, final)
+    for r in range(1, n_dp):
+        here = out.at[lax.rem(mine + n_dp - r, n_dp)]
+        remote(here, here, dps.at[r - 1], dpr.at[r - 1], dp=peers[r - 1]).wait_recv()
+    copies[-1].wait()
+    for copy in copies[:-1]:
+        copy.wait_send()
+
+
+class RolledTerm:
+    def __init__(self, term, mine, n_dp):
+        self.term, self.mine, self.n_dp = term, mine, n_dp
+
+    def index(self, key):
+        return key[0], lax.rem(self.mine + key[1], self.n_dp)
+
+    def __getitem__(self, key):
+        return self.term[self.index(key)]
+
+    @property
+    def at(self):
+        class View:
+            def __getitem__(view, key):
+                return self.term.at[self.index(key)]
+
+        return View()
+
+
+def collect_call(x, n_seq, number):
+    _, n_dp, rows, width = x.shape
+    dma = pltpu.SemaphoreType.DMA
+    vmem = pl.BlockSpec(memory_space=pltpu.VMEM)
+    return pl.pallas_call(
+        partial(collect_kernel, n_seq, n_dp),
+        in_specs=[vmem],
+        out_specs=vmem,
+        out_shape=jax.ShapeDtypeStruct((n_dp, rows, width), bf16),
+        scratch_shapes=[pltpu.VMEM((n_dp, rows, width), bf16), dma, dma((n_dp - 1,)), dma((n_dp - 1,))]
+        + scatter_scratch(n_seq // 2, n_dp, rows, width),
+        compiler_params=pltpu.CompilerParams(
+            collective_id=number, has_side_effects=True, vmem_limit_bytes=60 * 1024 * 1024
+        ),
+        name="collect",
+    )(x)
+
+
+def sum_kernel(n_seq, x, out, inbox, total, lsem, s1, r1, s2, r2):
+    me = lax.axis_index("seq")
+    peers = [lax.rem(me + r, n_seq) for r in range(1, n_seq)]
+    greet([(None, q) for q in peers])
+    copies = []
+    for r, q in enumerate(peers):
+        copy = remote(x.at[q], inbox.at[r], s1.at[r], r1.at[r], seq=q)
+        copy.start()
+        copies.append(copy)
+    value = x[me].astype(f32)
+    for r, q in enumerate(peers):
+        remote(inbox.at[r], inbox.at[r], s1.at[r], r1.at[r], seq=q).wait_recv()
+        value = value + inbox[r].astype(f32)
+    total[...] = value.astype(total.dtype)
+    for r, q in enumerate(peers):
+        copy = remote(total, out.at[me], s2.at[r], r2.at[r], seq=q)
+        copy.start()
+        copies.append(copy)
+    keep = pltpu.make_async_copy(total, out.at[me], lsem)
+    keep.start()
+    for r, q in enumerate(peers):
+        here = out.at[lax.rem(me + n_seq - 1 - r, n_seq)]
+        remote(here, here, s2.at[r], r2.at[r], seq=q).wait_recv()
+    keep.wait()
+    for copy in copies:
+        copy.wait_send()
+
+
+def seq_sum(x, n_seq, number):
+    rows, width = x.shape[0] // n_seq, x.shape[1]
+    dma = pltpu.SemaphoreType.DMA
+    vmem = pl.BlockSpec(memory_space=pltpu.VMEM)
+    out = pl.pallas_call(
+        partial(sum_kernel, n_seq),
+        in_specs=[vmem],
+        out_specs=vmem,
+        out_shape=jax.ShapeDtypeStruct((n_seq, rows, width), x.dtype),
+        scratch_shapes=[pltpu.VMEM((n_seq - 1, rows, width), x.dtype), pltpu.VMEM((rows, width), x.dtype),
+                        dma] + [dma((n_seq - 1,)) for _ in range(4)],
+        compiler_params=pltpu.CompilerParams(
+            collective_id=number, has_side_effects=True, vmem_limit_bytes=60 * 1024 * 1024
+        ),
+        name="seq_sum",
+    )(x.reshape(n_seq, rows, width))
+    return out.reshape(n_seq * rows, width)
+
+
 def on_device(
     tokens, route, cotangent, gain_mix, w_in, conv_w, w_x, w_dt, dt_bias, a_log, d_skip, w_out,
     gain_moe, w_up, w_down,
@@ -313,7 +701,7 @@
     row_values = tokens.astype(f32)
     normed, norm_pullback = jax.vjp(rms_norm, row_values, gmix_all)
     normed_low = normed.astype(bf16)
-    xg = lax.all_gather(normed_low, "seq", axis=0, tiled=True)
+    xg = seq_gather(normed_low, n_seq, 2, 0)
     tb = 128
     steps = tall // tb
     sds = jax.ShapeDtypeStruct
@@ -324,7 +712,7 @@
         [(wide, tb), (wide, tb), (wide, tb), (sds((tall, sp), f32), tb)],
         [pltpu.VMEM((tb + 8, cp), f32)], "mix_in",
     )
-    small = lax.psum(small, "seq")
+    small = seq_sum(small.astype(bf16), n_seq, 1).astype(f32)
     bct = small[:, rank:n_small].reshape(tall // 8, 8, 2 * NS).transpose(0, 2, 1)
     dtp, hs, ssm, gated, part = chunked(
         scan_kernel, steps, False,
@@ -335,7 +723,7 @@
         [pltpu.VMEM((tb, cp), f32), pltpu.VMEM((tb, cp), f32), pltpu.VMEM((NS, cp), f32)],
         "scan_forward",
     )
-    mixer_out = lax.psum_scatter(part, "seq", scatter_dimension=0, tiled=True).astype(f32)
+    mixer_out = seq_scatter(part, n_seq, 2, 2)
     resid = row_values + mixer_out
 
     normed2, norm2_pullback = jax.vjp(rms_norm, resid, gmoe_all)
@@ -346,32 +734,30 @@
     target = choose * slots + slot_index
     pick = (target[None, :] == jnp.arange(experts * slots, dtype=jnp.int32)[:, None]).astype(bf16)
 
-    def dispatch(values):
+    def dispatch(values, number):
         send = mm(pick, values).astype(bf16).reshape(n_dp, slots, d_model)
-        got = lax.all_to_all(send, "dp", 0, 0, tiled=True)
-        return lax.all_gather(got.reshape(n_dp * slots, d_model), "seq", axis=0, tiled=True)
-
-    def collect(values):
-        got = lax.psum_scatter(values.astype(bf16), "seq", scatter_dimension=0, tiled=True)
-        back = lax.all_to_all(got.reshape(n_dp, slots, d_model), "dp", 0, 0, tiled=True)
-        return mm(pick, back.reshape(n_dp * slots, d_model), TN)
+        return dispatch_call(send, n_seq, number).reshape(n_seq * n_dp * slots, d_model)
+
+    def collect(values, number):
+        values = values.astype(bf16).reshape(n_seq, n_dp, slots, d_model)
+        return mm(pick, collect_call(values, n_seq, number).reshape(n_dp * slots, d_model), TN)
 
     up, down = w_up[0], w_down[0]
-    grad_slots = dispatch(cotangent)
+    grad_slots = dispatch(cotangent, 3)
     grad_hidden = mm(grad_slots, down, NT)
-    slot_rows = dispatch(moe_in)
+    slot_rows = dispatch(moe_in, 4)
     pre_act = mm(slot_rows, up, NT)
     hidden_f, gelu_pullback = jax.vjp(partial(jax.nn.gelu, approximate=False), pre_act)
     hidden = hidden_f.astype(bf16)
     grad_pre = gelu_pullback(grad_hidden)[0].astype(bf16)
-    grad_moe_in = collect(mm(grad_pre, up))
-    result = (resid + collect(mm(hidden, down))).astype(bf16)
+    grad_moe_in = collect(mm(grad_pre, up), 5)
+    result = (resid + collect(mm(hidden, down), 6)).astype(bf16)
     grad_down = mm(hidden, grad_slots, TN)
     grad_up = mm(grad_pre, slot_rows, TN)
 
     grad_resid, grad_gmoe = norm2_pullback(grad_moe_in)
     grad_resid = grad_resid + cotangent.astype(f32)
-    gml = lax.all_gather(grad_resid.astype(bf16), "seq", axis=0, tiled=True)
+    gml = seq_gather(grad_resid.astype(bf16), n_seq, 2, 7)
     grad_rank, gbct, gu, gz, gwout, gwdt, ga, gvecs = chunked(
         back_kernel, steps, True,
         [(gml, tb), (wout_m, 0), (gated, tb), (conv, tb), (z, tb), (ssm, tb), (dtp, tb), (hs, tb),
@@ -384,7 +770,7 @@
     )
     grad_bc = gbct.transpose(0, 2, 1).reshape(tall, 2 * NS)
     gsmall = jnp.concatenate([grad_rank[:, :rank], grad_bc], axis=1)
-    gsmall = lax.psum(jnp.pad(gsmall, ((0, 0), (0, sp - n_small))), "seq")
+    gsmall = seq_sum(jnp.pad(gsmall, ((0, 0), (0, sp - n_small))).astype(bf16), n_seq, 8)
     gpart, gwx, gw, gcw = chunked(
         out_kernel, steps, True,
         [(gsmall, tb), (wx_m, 0), (conv, tb), (x, tb), (gu, tb), (gz, tb), (xg, tb), (w_mine, 0),
@@ -393,7 +779,7 @@
          (sds((d_model, 2 * cp), f32), 0), (sds((8, cp), f32), 0)],
         [pltpu.VMEM((tb + 8, cp), f32)], "mix_out",
     )
-    grad_normed = lax.psum_scatter(gpart, "seq", scatter_dimension=0, tiled=True).astype(f32)
+    grad_normed = seq_scatter(gpart, n_seq, 2, 9)
     grad_row_norm, grad_gmix = norm_pullback(grad_normed)
     grad_tokens = grad_row_norm + grad_resid
 

time: 1020 us -> 667 us (0.65)
  waiting for transfers between devices: 617 us -> 1.22 us
  Pallas kernels: 121 us -> 431 us
  blocking collectives: 165 us -> 115 us
    pallas_call x0 -> x10, Pallas kernels: none -> 310 us  [the longest x2 78 us: collect_call(): pl.pallas_call(partial(collect_kernel, n_seq, n_dp), in_specs=[vmem], out...]
    reduce_scatter x4 -> x0, waiting for transfers between devices: 252 us -> none  [the longest x2 118 us: collect(): lax.psum_scatter(values.astype(bf16), 'seq', scatter_dimension=0, tiled=T...]
    all_gather x4 -> x0, waiting for transfers between devices: 180 us -> none  [the longest x2 94.5 us: dispatch(): lax.all_gather(got.reshape(n_dp * slots, d_model), 'seq', axis=0, tiled=T...]
    psum x2 -> x0, waiting for transfers between devices: 136 us -> none  [the longest x1 69.4 us: on_device(): small = lax.psum(small, 'seq')]
    all_to_all x4 -> x0, blocking collectives: 52.1 us -> none  [the longest x1 21.1 us: on_device(): lax.all_to_all(w_cols.reshape(n_seq, rows_in, 2 * cp), 'seq', 0, 0, tiled...]
    reduce_scatter x1, waiting for transfers between devices: 21.3 us -> 0.01 us  [on_device(): gw = lax.psum_scatter(gw, 'dp', scatter_dimension=0, tiled=True)]
    unnamed x15 -> x5, waiting for transfers between devices: 18.7 us -> 1.21 us
  transfers between devices with their start and end apart: 16 -> 6, of which waited for: 13 -> 1; matrix products, arithmetic and copies ran while one was open for 6% -> 7% of each run, Pallas kernels for 2% -> 20%
where the time goes in v2:
time: 667 us; the launch traced here: 666 us
  Pallas kernels  431 us (65%)
  blocking collectives  115 us (17%)
  local copies, waits for them, and re-layouts  40.9 us (6%)
  matrix products  33 us (5%)
  other arithmetic  17.3 us (3%)
  between operations  14.5 us (2%)
  starting transfers between devices  12.8 us (2%)
    pallas_call x4, Pallas kernels, chunked(): pl.pallas_call(kernel, grid=(steps,), in_specs=[spec(a.shape, r) for a, r...  121 us
    pallas_call x2, Pallas kernels, collect_call(): pl.pallas_call(partial(collect_kernel, n_seq, n_dp), in_specs=[vmem], out...  78 us
    pallas_call x2, Pallas kernels, dispatch_call(): pl.pallas_call(partial(dispatch_kernel, n_seq, n_dp), in_specs=[pl.BlockS...  77.7 us
    all_gather x1, blocking collectives, on_device(): lax.all_gather(jnp.stack([gain_mix, gain_moe]), both, axis=1, tiled=True)  68 us
    pallas_call x2, Pallas kernels, seq_scatter(): pl.pallas_call(partial(scatter_kernel, n_seq), in_specs=[vmem], out_specs...  64 us
    pallas_call x2, Pallas kernels, seq_gather(): pl.pallas_call(partial(gather_kernel, n_seq), in_specs=[pl.BlockSpec(memo...  54 us
    unnamed x1, blocking collectives  38.1 us
    pallas_call x2, Pallas kernels, seq_sum(): pl.pallas_call(partial(sum_kernel, n_seq), in_specs=[vmem], out_specs=vme...  36.3 us
  transfers between devices with their start and end apart: 6, of which 1 were waited for; matrix products, arithmetic and copies ran while one was open for 7% of the time, Pallas kernels for 20%

profile of v2, /device:TPU:0, one launch (start us, length us, event | category | flops | bytes accessed | tf_op | source)
XLA Modules:
  0.0 665.5 jit_solution(8836636516137258913)
XLA Ops:
  7.2 2.3 reshape.174
  11.2 7.4 %all-to-all-start = ((bf16[8,36,768]{2,1,0:T(8,128)(2,1)}), bf16[8,36,768]{2,1,0:T(8,128)(2,1)S(1)}, u32[]{:S(2)}, u32[]{:S(2)}) async-start(bf16[8,36,768]{2,1,0:T(8,128)(2,1)} %copy.136), calls=%async_computation | async-start | bytes 983040 | tf_op jit(solution)/shard_map/all_to_all | solution.py:682
  19.3 8.7 %all_gather.11 = bf16[288,1350]{1,0:T(8,128)(2,1)S(1)} all-gather(bf16[72,1350]{1,0:T(8,128)(2,1)S(1)} %concatenate.13), channel_id=1, replica_groups=mesh['dp'=4,'seq'=8] {'dp'}, dimensions={0}, use_global_device_ids=true | all-gather | bytes 972000 | tf_op jit(solution)/shard_map/all_gather | solution.py:687
  28.1 1.2 copy.141
  29.3 68.0 %all-gather = bf16[32,36,2]{1,2,0:T(2,128)(2,1)S(1)} all-gather(bf16[1,36,2]{1,2,0:T(2,128)(2,1)S(1)} %maximum_bitcast_fusion), channel_id=1, replica_groups=mesh['dp'=4,'seq'=8] {'dp','seq'}, dimensions={0}, use_global_device_ids=true | all-gather | bytes 4752 | tf_op jit(solution)/shard_map/all_gather | solution.py:676
  99.3 2.3 copy.144.wout
  104.3 24.5 %seq_gather.2 = bf16[8,2,64,1152]{3,2,1,0:T(8,128)(2,1)} custom-call(bf16[2,64,1152]{2,1,0:T(8,128)(2,1)} %bitcast.139), custom_call_target="tpu_custom_call" | custom-call | tf_op jit(solution)/shard_map/seq_gather/pallas_call | solution.py:392
  130.3 38.6 %dispatch.3 = bf16[8,4,40,1152]{3,2,1,0:T(8,128)(2,1)} custom-call(bf16[4,40,1152]{2,1,0:T(8,128)(2,1)} %bitcast.137), custom_call_target="tpu_custom_call" | custom-call | tf_op jit(solution)/shard_map/dispatch/pallas_call | solution.py:450
  171.3 8.5 %mix_in.1 = (f32[1024,384]{1,0:T(8,128)}, f32[1024,384]{1,0:T(8,128)}, f32[1024,384]{1,0:T(8,128)}, f32[1024,128]{1,0:T(8,128)}) custom-call(bf16[1024,1152]{1,0:T(8,128)(2,1)} %bitcast.117, bf16[1152,768]{1,0:T(8,128)(2,1)} %all-gather.3.cloned.1.call-done.w, f32[8,384]{1,0:T(8,128)} %pad_convert_fusion.1.cw, bf16[384,128]{1,0:T(8,128)(2,1)} %pad.37.clone.wx), custom_call_target="tpu_custom_call" | custom-call | tf_op jit(solution)/shard_map/mix_in/pallas_call | solution.py:257
  179.8 1.8 convert_element_type.101
  181.6 17.7 %seq_sum.2 = bf16[8,128,128]{2,1,0:T(8,128)(2,1)} custom-call(bf16[8,128,128]{2,1,0:T(8,128)(2,1)} %bitcast.143), custom_call_target="tpu_custom_call" | custom-call | tf_op jit(solution)/shard_map/seq_sum/pallas_call | solution.py:644
  200.5 2.0 copy.143
  202.5 25.4 %scan_forward.1 = (f32[1024,384]{1,0:T(8,128)}, f32[1024,16,384]{2,1,0:T(8,128)}, f32[1024,384]{1,0:T(8,128)}, bf16[1024,384]{1,0:T(8,128)(2,1)}, bf16[1024,1152]{1,0:T(8,128)(2,1)}) custom-call(f32[1024,128]{1,0:T(8,128)} %copy-done.2, f32[128,32,8]{2,1,0:T(8,128)} %bitcast.119, bf16[128,384]{1,0:T(8,128)(2,1)} %pad_bitcast_fusion.wdtt, ...), custom_call_target="tpu_custom_call" | custom-call | tf_op jit(solution)/shard_map/scan_forward/pallas_call | solution.py:257
  227.9 30.7 %seq_scatter.2 = f32[2,64,1152]{2,1,0:T(8,128)} custom-call(bf16[8,2,64,1152]{3,2,1,0:T(8,128)(2,1)} %bitcast.132), custom_call_target="tpu_custom_call" | custom-call | tf_op jit(solution)/shard_map/seq_scatter/pallas_call | solution.py:535
  258.5 1.2 multiply_reduce_fusion.2
  260.9 39.2 %dispatch.2 = bf16[8,4,40,1152]{3,2,1,0:T(8,128)(2,1)} custom-call(bf16[4,40,1152]{2,1,0:T(8,128)(2,1)} %bitcast.138), custom_call_target="tpu_custom_call" | custom-call | tf_op jit(solution)/shard_map/dispatch/pallas_call | solution.py:450
  300.1 8.2 %multiply_convert_fusion = (bf16[1280,384]{1,0:T(8,128)(2,1)}, f32[1280,384]{1,0:T(8,128)S(1)}, f32[1280,384]{1,0:T(8,128)S(1)}) fusion(bf16[1280,1152]{1,0:T(8,128)(2,1)} %bitcast.127, bf16[1,384,1152]{2,1,0:T(8,128)(2,1)S(1)} %copy-done), kind=kOutput, calls=%fused_computation.11 | convolution fusion | flops 1164410880 | bytes 8749056 | tf_op jit(solution)/shard_map/dot_general | solution.py:23
  308.3 2.4 add_convert_fusion
  310.7 3.4 convolution_convert_fusion
  314.0 39.5 %collect.3 = bf16[4,40,1152]{2,1,0:T(8,128)(2,1)} custom-call(bf16[8,4,40,1152]{3,2,1,0:T(8,128)(2,1)} %bitcast.129), custom_call_target="tpu_custom_call" | custom-call | tf_op jit(solution)/shard_map/collect/pallas_call | solution.py:598
  353.5 1.4 multiply_reduce_fusion
  355.9 29.5 %seq_gather.3 = bf16[8,2,64,1152]{3,2,1,0:T(8,128)(2,1)} custom-call(bf16[2,64,1152]{2,1,0:T(8,128)(2,1)} %bitcast.140), custom_call_target="tpu_custom_call" | custom-call | tf_op jit(solution)/shard_map/seq_gather/pallas_call | solution.py:392
  385.4 70.7 %scan_backward.1 = (f32[1024,128]{1,0:T(8,128)}, f32[128,32,8]{2,1,0:T(8,128)}, f32[1024,384]{1,0:T(8,128)}, bf16[1024,384]{1,0:T(8,128)(2,1)}, f32[384,1152]{1,...) custom-call(bf16[1024,1152]{1,0:T(8,128)(2,1)} %bitcast.121, bf16[384,1152]{1,0:T(8,128)(2,1)} %copy.144.wout, ...), custom_call_target="tpu_custom_call" | custom-call | tf_op jit(solution)/shard_map/scan_backward/pallas_call | solution.py:257
  457.3 1.8 convert_bitcast_fusion
  460.4 18.6 %seq_sum.3 = bf16[8,128,128]{2,1,0:T(8,128)(2,1)} custom-call(bf16[8,128,128]{2,1,0:T(8,128)(2,1)} %bitcast.142), custom_call_target="tpu_custom_call" | custom-call | tf_op jit(solution)/shard_map/seq_sum/pallas_call | solution.py:644
  478.9 16.3 %mix_out.1 = (bf16[1024,1152]{1,0:T(8,128)(2,1)}, f32[384,128]{1,0:T(8,128)}, f32[1152,768]{1,0:T(8,128)}, f32[8,384]{1,0:T(8,128)}) custom-call(bf16[1024,128]{1,0:T(8,128)(2,1)} %bitcast.144, bf16[384,128]{1,0:T(8,128)(2,1)} %pad.37.clone.wx, f32[1024,384]{1,0:T(8,128)} %get-tuple-element.36.conv, f32[1024,384]{1,0:T(8,128)} %get-tuple-element.45.x, ...), custom_call_target="tpu_custom_call" | custom-call | tf_op jit(solution)/shard_map/mix_out/pallas_call | solution.py:257
  495.2 2.2 convert.30
  497.4 2.2 copy.158
  499.6 1.4 slice.106
  501.1 1.6 copy.161
  502.8 4.9 convolution_convert_fusion.1
  507.7 38.6 %collect.2 = bf16[4,40,1152]{2,1,0:T(8,128)(2,1)} custom-call(bf16[8,4,40,1152]{3,2,1,0:T(8,128)(2,1)} %bitcast.130), custom_call_target="tpu_custom_call" | custom-call | tf_op jit(solution)/shard_map/collect/pallas_call | solution.py:598
  547.3 33.4 %seq_scatter.3 = f32[2,64,1152]{2,1,0:T(8,128)} custom-call(bf16[8,2,64,1152]{3,2,1,0:T(8,128)(2,1)} %bitcast.131), custom_call_target="tpu_custom_call" | custom-call | tf_op jit(solution)/shard_map/seq_scatter/pallas_call | solution.py:535
  580.7 1.3 fusion.18
  584.4 2.2 slice.132
  586.7 38.1 %all-reduce.7 = f32[2,1152]{1,0:T(2,128)S(1)} all-reduce(f32[2,1152]{1,0:T(2,128)S(1)} %pad_maximum_fusion), channel_id=2, replica_groups=mesh['dp'=4,'seq'=8] {'dp','seq'}, use_global_device_ids=true, to_apply=%region_8.9.clone | all-reduce | flops 2304 | bytes 18432
  624.8 4.9 convolution_bitcast_fusion
  629.8 1.1 fusion.20
  631.0 1.8 reshape.200
  632.8 5.2 all-to-all-start.1
  638.6 4.8 convolution_bitcast_fusion.1
  646.4 1.6 slice.110
  648.0 1.4 slice.109
  649.4 1.6 slice_reduce_fusion
  650.9 1.1 reduce-scatter.13.cloned.1.call-done
  652.1 1.7 convert_element_type.122
  654.9 1.3 copy.152
  656.2 2.8 reshape.202
  (150 shorter events, 24.7 us)
Async XLA Ops:
  7.2 292.9 %copy-start = (bf16[1,384,1152]{2,1,0:T(8,128)(2,1)S(1)}, bf16[1,384,1152]{2,1,0:T(8,128)(2,1)}, u32[]{:S(2)}) copy-start(bf16[1,384,1152]{2,1,0:T(8,128)(2,1)} %param.28) | copy-start | bytes 2654212
  9.8 8.9 %copy-start.27 = (bf16[72,4]{0,1:T(4,128)(2,1)S(1)}, bf16[72,4]{0,1:T(4,128)(2,1)}, u32[]{:S(2)}) copy-start(bf16[72,4]{0,1:T(4,128)(2,1)} %param.20) | copy-start | bytes 1732
  9.9 9.0 %copy-start.30 = (bf16[72]{0:T(256)(128)(2,1)S(1)}, bf16[72]{0:T(256)(128)(2,1)}, u32[]{:S(2)}) copy-start(bf16[72]{0:T(256)(128)(2,1)} %param.23) | copy-start | bytes 436
  9.9 9.1 %copy-start.22 = (bf16[72,16]{0,1:T(8,128)(2,1)S(1)}, bf16[72,16]{0,1:T(8,128)(2,1)}, u32[]{:S(2)}) copy-start(bf16[72,16]{0,1:T(8,128)(2,1)} %param.24) | copy-start | bytes 6916
  9.9 9.2 %copy-start.31 = (bf16[72]{0:T(256)(128)(2,1)S(1)}, bf16[72]{0:T(256)(128)(2,1)}, u32[]{:S(2)}) copy-start(bf16[72]{0:T(256)(128)(2,1)} %param.25) | copy-start | bytes 436
  9.9 9.3 %copy-start.11 = (bf16[72,1152]{1,0:T(8,128)(2,1)S(1)}, bf16[72,1152]{1,0:T(8,128)(2,1)}, u32[]{:S(2)}) copy-start(bf16[72,1152]{1,0:T(8,128)(2,1)} %param.26) | copy-start | bytes 497668
  9.9 9.3 %copy-start.14 = (bf16[72,104]{1,0:T(8,128)(2,1)S(1)}, bf16[72,104]{1,0:T(8,128)(2,1)}, u32[]{:S(2)}) copy-start(bf16[72,104]{1,0:T(8,128)(2,1)} %param.21) | copy-start | bytes 44932
  9.9 9.3 %copy-start.15 = (bf16[72,72]{1,0:T(8,128)(2,1)S(1)}, bf16[72,72]{1,0:T(8,128)(2,1)}, u32[]{:S(2)}) copy-start(bf16[72,72]{1,0:T(8,128)(2,1)} %param.22) | copy-start | bytes 31108
  11.2 18.0 %copy-start.33 = (bf16[36]{0:T(256)(128)(2,1)S(1)}, bf16[36]{0:T(256)(128)(2,1)}, u32[]{:S(2)}) copy-start(bf16[36]{0:T(256)(128)(2,1)} %param.27) | copy-start | bytes 220
  11.2 18.0 %copy-start.34 = (bf16[36]{0:T(256)(128)(2,1)S(1)}, bf16[36]{0:T(256)(128)(2,1)}, u32[]{:S(2)}) copy-start(bf16[36]{0:T(256)(128)(2,1)} %param.18) | copy-start | bytes 220
  11.2 87.0 %all-to-all-start = ((bf16[8,36,768]{2,1,0:T(8,128)(2,1)}), bf16[8,36,768]{2,1,0:T(8,128)(2,1)S(1)}, u32[]{:S(2)}, u32[]{:S(2)}) async-start(bf16[8,36,768]{2,1,0:T(8,128)(2,1)} %copy.136), calls=%async_computation | async-start | bytes 983040 | tf_op jit(solution)/shard_map/all_to_all | solution.py:682
  18.7 152.7 %all-gather.3.cloned.1.call-start = ((), (), s32[]{:S(2)}) async-start(), calls=%async_computation.5 | async-start | bytes 2211840 | tf_op jit(solution)/shard_map/all_gather | solution.py:683
  99.1 531.9 %reduce-scatter.11.cloned.1.call-start = ((), (), s32[]{:S(2)}) async-start(), calls=%async_computation.7 | async-start | bytes 1843200 | tf_op jit(solution)/shard_map/reduce_scatter | solution.py:790
  99.3 4.0 copy-start.3
  102.4 26.4 %copy-start.24 = (s32[128,1]{0,1:T(1,128)S(1)}, s32[128,1]{0,1:T(1,128)}, u32[]{:S(2)}) copy-start(s32[128,1]{0,1:T(1,128)} %param.16) | copy-start | bytes 1540
  103.2 26.0 %copy-start.6 = (bf16[128,1152]{1,0:T(8,128)(2,1)S(1)}, bf16[128,1152]{1,0:T(8,128)(2,1)}, u32[]{:S(2)}) copy-start(bf16[128,1152]{1,0:T(8,128)(2,1)} %param.17) | copy-start | bytes 884740
  103.4 25.3 %copy-start.28 = (f32[128]{0:T(128)}, f32[128]{0:T(128)S(1)}, u32[]{:S(2)}) copy-start(f32[128]{0:T(128)S(1)} %fusion.21) | copy-start | bytes 1540
  103.5 26.8 %copy-start.20 = (f32[128]{0:T(128)}, f32[128]{0:T(128)S(1)}, u32[]{:S(2)}) copy-start(f32[128]{0:T(128)S(1)} %fusion.37) | copy-start | bytes 1540
  129.3 224.2 %copy-start.16 = (s32[128]{0:T(128)}, s32[128]{0:T(128)S(1)}, u32[]{:S(2)}) copy-start(s32[128]{0:T(128)S(1)} %multiply_add_fusion.1) | copy-start | bytes 1540
  200.3 2.2 copy-start.2
  259.8 95.2 %copy-start.18 = (f32[128]{0:T(128)}, f32[128]{0:T(128)S(1)}, u32[]{:S(2)}) copy-start(f32[128]{0:T(128)S(1)} %fusion.38) | copy-start | bytes 1540
  300.1 8.2 %copy-start.5 = (bf16[8,4,40,1152]{3,2,1,0:T(8,128)(2,1)S(1)}, bf16[8,4,40,1152]{3,2,1,0:T(8,128)(2,1)}, u32[]{:S(2)}) copy-start(bf16[8,4,40,1152]{3,2,1,0:T(8,128)(2,1)} %dispatch.3) | copy-start | bytes 8847364
  300.1 8.2 %copy-start.32 = (bf16[1,384,1152]{2,1,0:T(8,128)(2,1)S(1)}, bf16[1,384,1152]{2,1,0:T(8,128)(2,1)}, u32[]{:S(2)}) copy-start(bf16[1,384,1152]{2,1,0:T(8,128)(2,1)} %param.29) | copy-start | bytes 2654212
  310.7 3.4 copy-start.35
  354.9 30.5 %copy-start.25 = (f32[128]{0:T(128)}, f32[128]{0:T(128)S(1)}, u32[]{:S(2)}) copy-start(f32[128]{0:T(128)S(1)} %multiply_multiply_fusion.6) | copy-start | bytes 1540
  502.7 140.6 %reduce-scatter.9.cloned.1.call-start = ((), (), s32[]{:S(2)}) async-start(), calls=%async_computation.6 | async-start | bytes 368640 | tf_op jit(solution)/shard_map/reduce_scatter | solution.py:797
  507.7 39.3 %copy-start.12 = (bf16[384,16]{0,1:T(8,128)(2,1)S(1)}, bf16[384,16]{0,1:T(8,128)(2,1)}, u32[]{:S(2)}) copy-start(bf16[384,16]{0,1:T(8,128)(2,1)} %get-tuple-element.153) | copy-start | bytes 36868
  507.7 39.3 %copy-start.13 = (f32[16,384]{1,0:T(8,128)S(1)}, f32[16,384]{1,0:T(8,128)}, u32[]{:S(2)}) copy-start(f32[16,384]{1,0:T(8,128)} %get-tuple-element.53) | copy-start | bytes 73732
  546.3 34.4 %copy-start.21 = (f32[128]{0:T(128)S(1)}, f32[128]{0:T(128)}, u32[]{:S(2)}) copy-start(f32[128]{0:T(128)} %copy-done.20) | copy-start | bytes 1540
  547.3 34.8 %copy-start.23 = (f32[8,384]{1,0:T(8,128)S(1)}, f32[8,384]{1,0:T(8,128)}, u32[]{:S(2)}) copy-start(f32[8,384]{1,0:T(8,128)} %get-tuple-element.52) | copy-start | bytes 36868
  547.3 34.9 %copy-start.9 = (f32[384,128]{1,0:T(8,128)S(1)}, f32[384,128]{1,0:T(8,128)}, u32[]{:S(2)}) copy-start(f32[384,128]{1,0:T(8,128)} %get-tuple-element.51) | copy-start | bytes 589828
  547.3 34.9 %copy-start.10 = (f32[384,128]{1,0:T(8,128)S(1)}, f32[384,128]{1,0:T(8,128)}, u32[]{:S(2)}) copy-start(f32[384,128]{1,0:T(8,128)} %get-tuple-element.50) | copy-start | bytes 589828
  580.7 2.6 copy-start.8
  580.7 2.6 copy-start.17
  582.0 2.4 copy-start.29
  584.4 67.7 %reduce-scatter.13.cloned.1.call-start = ((), (), s32[]{:S(2)}) async-start(), calls=%async_computation.8 | async-start | bytes 829440
  624.8 5.0 copy-start.4
  624.8 5.0 copy-start.7
  624.8 5.0 copy-start.19
  624.8 5.0 copy-start.26
  632.8 20.9 %all-to-all-start.1 = ((bf16[8,36,576]{2,1,0:T(8,128)(2,1)}), bf16[8,36,576]{2,1,0:T(8,128)(2,1)S(1)}, u32[]{:S(2)}, u32[]{:S(2)}) async-start(bf16[8,36,576]{2,1,0:T(8,128)(2,1)} %reshape.200), calls=%async_computation.1 | async-start | bytes 819200 | tf_op jit(solution)/shard_map/all_to_all | solution.py:791
  654.9 4.1 copy-start.1
Sparse Core Ops, SparseCore 0:
  99.2 17.9 all-gather.2
  502.9 25.7 reduce-scatter.10
  584.5 17.7 reduce-scatter.8
  629.9 22.1 reduce-scatter.12

commit v3 on v2

v3 whole, which is shorter than its diff:
```python
from functools import partial

import jax
import jax.numpy as jnp
from jax import lax
from jax.experimental import pallas as pl
from jax.experimental.pallas import tpu as pltpu
from jax.sharding import PartitionSpec as P

NS = 16
LN2 = 0.6931471805599453
LOG2E = 1.4426950408889634
eps = 1e-05
f32 = jnp.float32
bf16 = jnp.bfloat16

NN = (((1,), (0,)), ((), ()))
NT = (((1,), (1,)), ((), ()))
TN = (((0,), (0,)), ((), ()))


def mm(left, right, dims=NN):
    return lax.dot_general(left, right, dims, preferred_element_type=f32)


def up128(count):
    return -(-count // 128) * 128


def rms_norm(values, gain_vec):
    return values * lax.rsqrt(jnp.mean(values * values, axis=-1, keepdims=True) + eps) * gain_vec


def sigmoid(v):
    return 1.0 / (1.0 + jnp.exp(-v))


def softplus(v):
    return jnp.maximum(v, 0.0) + jnp.log1p(jnp.exp(-jnp.abs(v)))


def tree_step(first, second, by):
    row = lax.broadcasted_iota(jnp.int32, first.shape, 0)
    clear = (row & by) == 0
    return jnp.where(clear, first, second) + pltpu.roll(jnp.where(clear, second, first), by, 0)


def tree_push(stack, value, falling=False):
    level = 1
    while stack and stack[-1][0] == level:
        other = stack.pop()[1]
        value = tree_step(value, other, level) if falling else tree_step(other, value, level)
        level *= 2
    stack.append((level, value))


def turned(misc):
    return misc[...].astype(f32).T


def in_kernel(tok, gain, w, wx, misc, x_out, z_out, conv_out, small_out, norm_out, buf, mt):
    rows, cp = x_out.shape

    @pl.when(pl.program_id(0) == 0)
    def _():
        buf[0:8, :] = jnp.zeros((8, cp), f32)
        mt[...] = turned(misc)

    @pl.when(pl.program_id(0) > 0)
    def _():
        buf[0:8, :] = buf[rows : rows + 8, :]

    normed = rms_norm(tok[...].astype(f32), gain[0:1, :]).astype(bf16)
    norm_out[...] = normed
    prod = mm(normed, w[...])
    x_part = prod[:, :cp]
    x_out[...] = x_part
    z_out[...] = prod[:, cp:]
    buf[8 : 8 + rows, :] = x_part
    conv = x_part * mt[3:4, :]
    for k in range(3):
        conv = conv + buf[5 + k : 5 + k + rows, :] * mt[k : k + 1, :]
    conv_out[...] = conv
    small_out[...] = mm((conv * sigmoid(conv)).astype(bf16), wx[...]).astype(bf16)


def stage_step(k, n, steps):
    return steps - 1 - (n - 1 - k) * max(1, (steps - 2) // max(1, n - 1))


def scan_kernel(
    n_seq, steps, small, bct, wdt, misc, conv, z, wout, cot_own,
    dtp_out, h_out, ssm_out, gated_out, part_out, cot_all,
    delta_s, du_s, state, mt, a2, csem, *gsems,
):
    rows, cp = conv.shape
    line = Line(n_seq)
    step = pl.program_id(0)
    slots_of = Gather(
        line, lambda q, p: cot_all.at[q, p], lambda p: cot_own.at[p], cot_own.shape[0], gsems
    )
    own = pltpu.make_async_copy(cot_own, cot_all.at[line.me], csem)

    @pl.when(step == 0)
    def _():
        greet(line.neighbours())
        own.start()
        slots_of.stage(0)

    for k in range(1, line.n):
        pl.when(step == stage_step(k, line.n, steps))(lambda k=k: slots_of.stage(k))

    @pl.when(pl.program_id(0) == 0)
    def _():
        state[...] = jnp.zeros_like(state)
        mt[...] = turned(misc)
        a2[...] = -jnp.exp(mt[16:32, :]) * LOG2E

    dtp = mm(small[...], wdt[...], NT) + mt[8:9, :]
    dtp_out[...] = dtp
    delta = softplus(dtp)
    cv = conv[...]
    u = cv * sigmoid(cv)
    delta_s[...] = delta
    du_s[...] = delta * u

    def group(g, h):
        base = pl.multiple_of(g * 8, 8)
        bc = bct[g]
        stack = []
        for t in range(8):
            d = jnp.broadcast_to(delta_s[pl.ds(base + t, 1), :], (NS, cp))
            du = jnp.broadcast_to(du_s[pl.ds(base + t, 1), :], (NS, cp))
            h = jnp.exp2(d * a2[...]) * h + du * bc[:NS, t : t + 1]
            h_out[base + t] = h
            prod = h * bc[NS:, t : t + 1]
            tree_push(stack, prod[:8] + prod[8:])
        ssm_out[pl.ds(base, 8), :] = stack[0][1]
        return h

    state[...] = lax.fori_loop(0, rows // 8, group, state[...])
    zv = z[...]
    gated = (ssm_out[...] + mt[9:10, :] * u) * (zv * sigmoid(zv))
    low = gated.astype(bf16)
    gated_out[...] = low
    part_out[...] = mm(low, wout[...]).astype(part_out.dtype)

    @pl.when(step == steps - 1)
    def _():
        slots_of.finish()
        own.wait()


def back_kernel(
    n_seq, steps, gml, wout, gated, conv, z, ssm, dtp, hs, hlast, bct, small, wdt, misc,
    term, rank_out, gbct_out, gu_out, gz_out, gwout_out, gwdt, gmisc, sums_out,
    delta_s, du_s, gs_s, r1_s, r2_s, lam_s, mt, a2, gwout, ga, *scratch,
):
    rows, cp = conv.shape
    step = pl.program_id(0)
    last = steps - 1
    line = Line(n_seq)
    work = Collect(line, term, sums_out, scratch)

    @pl.when(step == 0)
    def _():
        greet(line.neighbours(), work.peers)
        work.open()

    for t in range(line.n):
        pl.when(step == t + 1)(lambda t=t: work.stage(t))

    @pl.when(step == 0)
    def _():
        lam_s[...] = jnp.zeros_like(lam_s)
        gwout[...] = jnp.zeros_like(gwout)
        gwdt[...] = jnp.zeros_like(gwdt)
        ga[...] = jnp.zeros_like(ga)
        gmisc[...] = jnp.zeros_like(gmisc)
        mt[...] = turned(misc)
        a2[...] = -jnp.exp(mt[16:32, :]) * LOG2E

    grad_mixed = gml[...]
    gg = mm(grad_mixed, wout[...], NT)
    gwout[...] += mm(gated[...], grad_mixed, TN)
    zv = z[...]
    sz = sigmoid(zv)
    cv = conv[...]
    u = cv * sigmoid(cv)
    skip = mt[9:10, :]
    gz_out[...] = (gg * (ssm[...] + skip * u) * (sz * (1.0 + zv * (1.0 - sz)))).astype(bf16)
    gs = gg * (zv * sz)
    delta = softplus(dtp[...])
    gs_s[...] = gs
    delta_s[...] = delta
    du_s[...] = delta * u
    lane = lax.broadcasted_iota(jnp.int32, (NS, 128), 1)
    keep_first = jnp.where(step == last, 0.0, 1.0)
    tiles = cp // 128

    def lane_fold(v):
        total = v[:, :128]
        for i in range(1, tiles):
            total = total + v[:, i * 128 : (i + 1) * 128]
        return jnp.sum(total, axis=1, keepdims=True)

    def group(k, carry):
        lamd, acc = carry
        g = rows // 8 - 1 - k
        base = pl.multiple_of(g * 8, 8)
        bc = bct[g]
        stack1, stack2 = [], []
        gb = jnp.zeros((NS, 128), f32)
        gc = jnp.zeros((NS, 128), f32)
        h = hs[base + 7]
        for t in range(7, -1, -1):
            d = jnp.broadcast_to(delta_s[pl.ds(base + t, 1), :], (NS, cp))
            du = jnp.broadcast_to(du_s[pl.ds(base + t, 1), :], (NS, cp))
            g_s = jnp.broadcast_to(gs_s[pl.ds(base + t, 1), :], (NS, cp))
            if t > 0:
                before = hs[base + t - 1]
            else:
                inside = hs[jnp.maximum(base - 1, 0)]
                before = jnp.where(g == 0, hlast[0] * keep_first, inside)
            lam = lamd + g_s * bc[NS:, t : t + 1]
            gc = jnp.where(lane == t, lane_fold(g_s * h), gc)
            gb = jnp.where(lane == t, lane_fold(lam * du), gb)
            lamd = jnp.exp2(d * a2[...]) * lam
            w = lamd * before
            acc = acc + w * d
            wa = w * a2[...]
            lb = lam * bc[:NS, t : t + 1]
            tree_push(stack1, wa[:8] + wa[8:], True)
            tree_push(stack2, lb[:8] + lb[8:], True)
            h = before
        r1_s[pl.ds(base, 8), :] = stack1[0][1]
        r2_s[pl.ds(base, 8), :] = stack2[0][1]
        gbct_out[g, :NS, :] = gb[:, :8]
        gbct_out[g, NS:, :] = gc[:, :8]
        return lamd, acc

    lamd, acc = lax.fori_loop(0, rows // 8, group, (lam_s[...], jnp.zeros((NS, cp), f32)))
    lam_s[...] = lamd
    ga[...] += acc
    r2 = r2_s[...]
    gu_out[...] = skip * gs + delta * r2
    gdelta = r1_s[...] * LN2 + u * r2
    gdtp = gdelta * sigmoid(dtp[...])
    gmisc[8:9, :] += jnp.sum(gdtp, axis=0, keepdims=True)
    gmisc[9:10, :] += jnp.sum(gs * u, axis=0, keepdims=True)
    low = gdtp.astype(bf16)
    gwdt[...] += mm(low, small[...], TN)
    rank_out[...] = mm(low, wdt[...])

    @pl.when(step == last)
    def _():
        gmisc[16:32, :] = ga[...] * (a2[...] * LN2)
        parts, cpd, _ = gwout_out.shape
        for p in range(parts):
            gwout_out[p] = gwout[p * cpd : (p + 1) * cpd, :].astype(bf16)
        work.finish()


def out_kernel(
    gsmall, wx, misc, conv, x, gu, gz, norm, w, gwdt, gmisc, part_out, gw_out, pack_out,
    buf, mt, gwx, gw, gm,
):
    rows, cp = conv.shape

    @pl.when(pl.program_id(0) == 0)
    def _():
        buf[rows : rows + 8, :] = jnp.zeros((8, cp), f32)
        gwx[...] = jnp.zeros_like(gwx)
        gw[...] = jnp.zeros_like(gw)
        gm[...] = jnp.zeros_like(gm)
        gm[8:32, :] = gmisc[8:32, :]
        mt[...] = turned(misc)

    @pl.when(pl.program_id(0) > 0)
    def _():
        buf[rows : rows + 8, :] = buf[0:8, :]

    gsl = gsmall[...]
    cv = conv[...]
    s = sigmoid(cv)
    gwx[...] += mm((cv * s).astype(bf16), gsl, TN)
    gconv = (gu[...] + mm(gsl, wx[...], NT)) * (s * (1.0 + cv * (1.0 - s)))
    buf[0:rows, :] = gconv
    xv = x[...]
    gx = gconv * mt[3:4, :]
    gm[3:4, :] += jnp.sum(gconv * xv, axis=0, keepdims=True)
    for k in range(3):
        moved = buf[3 - k : 3 - k + rows, :]
        gx = gx + moved * mt[k : k + 1, :]
        gm[k : k + 1, :] += jnp.sum(moved * xv, axis=0, keepdims=True)
    gp = jnp.concatenate([gx.astype(bf16), gz[...]], axis=1)
    part_out[...] = mm(gp, w[...], NT).astype(part_out.dtype)
    gw[...] += mm(norm[...], gp, TN)

    @pl.when(pl.program_id(0) == pl.num_programs(0) - 1)
    def _():
        parts, blocks, high, _ = gw_out.shape
        for b in range(parts * blocks):
            gw_out[b // blocks, b % blocks] = gw[b * high : (b + 1) * high, :].astype(bf16)
        flat = gm[...].T
        cpd = pack_out.shape[1]
        for p in range(parts):
            own = slice(p * cpd, (p + 1) * cpd)
            pack_out[p, :, 0:128] = gwx[own, :]
            pack_out[p, :, 128:256] = gwdt[own, :]
            pack_out[p, :, 256:384] = flat[own, :]


def chunked(kernel, steps, backward, ins, outs, scratch, name, number=None):
    def at(i):
        return steps - 1 - i if backward else i

    def spec(shape, rows):
        tail = (0,) * (len(shape) - 1)
        if rows is None:
            return pl.BlockSpec(memory_space=pl.ANY)
        if isinstance(rows, tuple):
            (block, column), = rows
            return pl.BlockSpec(block, lambda i: (0, column))
        if rows == 0:
            return pl.BlockSpec(shape, lambda i: (0,) + tail)
        if rows < 0:
            return pl.BlockSpec((1,) + shape[1:], lambda i: (jnp.maximum(at(i) * -rows - 1, 0),) + tail)
        return pl.BlockSpec((rows,) + shape[1:], lambda i: (at(i),) + tail)

    return pl.pallas_call(
        kernel,
        grid=(steps,),
        in_specs=[spec(a.shape, r) for a, r in ins],
        out_specs=[spec(s.shape, r) for s, r in outs],
        out_shape=[s for s, _ in outs],
        scratch_shapes=scratch,
        name=name,
        compiler_params=pltpu.CompilerParams(
            dimension_semantics=("arbitrary",), vmem_limit_bytes=60 * 1024 * 1024,
            collective_id=number, has_side_effects=number is not None,
        ),
    )(*[a for a, _ in ins])


MESH = pl.DeviceIdType.MESH


def remote(src, dst, send, recv, **where):
    return pltpu.make_async_remote_copy(
        src_ref=src, dst_ref=dst, send_sem=send, recv_sem=recv, device_id=where, device_id_type=MESH
    )


class Line:
    def __init__(self, n_seq):
        assert n_seq % 2 == 0
        self.n = n_seq // 2
        self.n_seq = n_seq
        self.me = lax.axis_index("seq")
        self.o, self.i = self.me // 2, self.me % 2

    def at(self, o, i):
        return o * 2 + i

    def neighbours(self):
        return [
            (None, self.at(self.o, 1 - self.i)),
            (self.o > 0, self.at(self.o - 1, self.i)),
            (self.o < self.n - 1, self.at(self.o + 1, self.i)),
        ]

    def order(self, t):
        table = [
            sorted(range(self.n), key=lambda q, o=o: (-abs(q - o), -q))[t] for o in range(self.n)
        ]
        place = jnp.int32(0)
        for o in range(self.n):
            place = place + jnp.where(self.o == o, table[o], 0)
        return place


def when(condition, action):
    if condition is None:
        action()
    else:
        pl.when(condition)(action)


def greet(peers, extra=()):
    barrier = pltpu.get_barrier_semaphore()
    count = jnp.int32(0)
    for condition, place in peers:
        when(
            condition,
            lambda place=place: pl.semaphore_signal(
                barrier, inc=1, device_id={"seq": place}, device_id_type=MESH
            ),
        )
        count = count + (1 if condition is None else jnp.where(condition, 1, 0))
    for place in extra:
        pl.semaphore_signal(barrier, inc=1, device_id={"dp": place}, device_id_type=MESH)
        count = count + 1
    pl.semaphore_wait(barrier, count)


def gather_sems(n, pieces):
    dma = pltpu.SemaphoreType.DMA
    return [dma((n, pieces)), dma((pieces,)), dma((n, pieces)), dma((n, pieces)), dma((n, pieces))]


class Gather:
    def __init__(self, line, at, own, pieces, sems):
        self.line, self.at, self.own, self.pieces, self.sems = line, at, own, pieces, sems

    def copy(self, src, q, p, send, recv, place):
        return remote(src, self.at(self.line.at(q, self.line.i), p), send, recv, seq=place)

    def up(self, src, q, p):
        zs, _, zr, _, _ = self.sems
        return self.copy(src, q, p, zs.at[q, p], zr.at[q, p], self.line.at(self.line.o + 1, self.line.i))

    def down(self, src, q, p, own):
        zs, zd, zr, _, _ = self.sems
        send = zd.at[p] if own else zs.at[q, p]
        return self.copy(src, q, p, send, zr.at[q, p], self.line.at(self.line.o - 1, self.line.i))

    def over(self, src, q, p):
        _, _, _, ys, yr = self.sems
        return self.copy(src, q, p, ys.at[q, p], yr.at[q, p], self.line.at(self.line.o, 1 - self.line.i))

    def each(self, k, act, arrive=None):
        line, o, n = self.line, self.line.o, self.line.n
        for p in range(self.pieces):
            if k == 0:
                src = self.own(p)
                if arrive is not None:
                    arrive(p)
                pl.when(o < n - 1)(lambda src=src, p=p: act(self.up(src, o, p)))
                pl.when(o > 0)(lambda src=src, p=p: act(self.down(src, o, p, True)))
                act(self.over(src, o, p))
                continue

            def below(p=p):
                q = o - k
                src = self.at(line.at(q, line.i), p)
                if arrive is not None:
                    arrive(self.up(src, q, p))
                pl.when(o < n - 1)(lambda: act(self.up(src, q, p)))
                act(self.over(src, q, p))

            def above(p=p):
                q = o + k
                src = self.at(line.at(q, line.i), p)
                if arrive is not None:
                    arrive(self.up(src, q, p))
                pl.when(o > 0)(lambda: act(self.down(src, q, p, False)))
                act(self.over(src, q, p))

            pl.when(o >= k)(below)
            pl.when(o + k <= n - 1)(above)

    def stage(self, k, ready=None):
        arrive = ready if k == 0 else (lambda copy: copy.wait_recv())
        self.each(k, lambda copy: copy.start(), arrive)

    def finish(self):
        line = self.line
        for q in range(line.n):
            for p in range(self.pieces):
                here = self.at(line.at(q, 1 - line.i), p)
                self.over(here, q, p).wait_recv()
        for k in range(line.n):
            self.each(k, lambda copy: copy.wait_send())

    def run(self, ready=None):
        for k in range(self.line.n):
            self.stage(k, ready)
        self.finish()


def gather_kernel(n_seq, x, out, lsem, *sems):
    line = Line(n_seq)
    greet(line.neighbours())
    keep = pltpu.make_async_copy(x, out.at[line.me], lsem)
    keep.start()
    Gather(line, lambda q, p: out.at[q, p], lambda p: x.at[p], x.shape[0], sems).run()
    keep.wait()


def seq_gather(x, n_seq, pieces, number):
    rows, width = x.shape
    out = pl.pallas_call(
        partial(gather_kernel, n_seq),
        in_specs=[pl.BlockSpec(memory_space=pl.ANY)],
        out_specs=pl.BlockSpec(memory_space=pl.ANY),
        out_shape=jax.ShapeDtypeStruct((n_seq, pieces, rows // pieces, width), x.dtype),
        scratch_shapes=[pltpu.SemaphoreType.DMA] + gather_sems(n_seq // 2, pieces),
        compiler_params=pltpu.CompilerParams(collective_id=number, has_side_effects=True),
        name="seq_gather",
    )(x.reshape(pieces, rows // pieces, width))
    return out.reshape(n_seq * rows, width)


def dispatch_kernel(n_seq, n_dp, x, out, lsem, dps, dpr, *sems):
    line = Line(n_seq)
    mine = lax.axis_index("dp")
    peers = [lax.rem(mine + r, n_dp) for r in range(1, n_dp)]
    greet(line.neighbours(), peers)
    copies = []
    for r, peer in enumerate(peers):
        copy = remote(x.at[peer], out.at[line.me, mine], dps.at[r], dpr.at[r], dp=peer)
        copy.start()
        copies.append(copy)
    keep = pltpu.make_async_copy(x.at[mine], out.at[line.me, mine], lsem)
    keep.start()

    def ready(r):
        if r == 0:
            keep.wait()
        else:
            source = out.at[line.me, lax.rem(mine + n_dp - r, n_dp)]
            remote(source, source, dps.at[r - 1], dpr.at[r - 1], dp=peers[r - 1]).wait_recv()

    at = rolled(out, mine, n_dp)
    Gather(line, at, lambda r: at(line.me, r), n_dp, sems).run(ready)
    for copy in copies:
        copy.wait_send()


def rolled(out, mine, n_dp):
    return lambda q, r: out.at[q, lax.rem(mine + n_dp - r, n_dp)]


def dispatch_call(x, n_seq, number):
    n_dp, rows, width = x.shape
    dma = pltpu.SemaphoreType.DMA
    return pl.pallas_call(
        partial(dispatch_kernel, n_seq, n_dp),
        in_specs=[pl.BlockSpec(memory_space=pl.ANY)],
        out_specs=pl.BlockSpec(memory_space=pl.ANY),
        out_shape=jax.ShapeDtypeStruct((n_seq, n_dp, rows, width), x.dtype),
        scratch_shapes=[dma, dma((n_dp - 1,)), dma((n_dp - 1,))] + gather_sems(n_seq // 2, n_dp),
        compiler_params=pltpu.CompilerParams(collective_id=number, has_side_effects=True),
        name="dispatch",
    )(x)


def scatter_scratch(n, pieces, rows, width):
    dma = pltpu.SemaphoreType.DMA
    return [
        pltpu.VMEM((n, pieces, rows, width), bf16),
        pltpu.VMEM((n, pieces, rows, width), bf16),
        pltpu.VMEM((n + 1, pieces, rows, width), bf16),
        dma((n, pieces)), dma((n, pieces)), dma((n, pieces)), dma((n + 1, pieces)),
    ]


class Scatter:
    def __init__(self, line, at, pieces, scratch, final):
        self.line, self.at, self.pieces, self.final = line, at, pieces, final
        self.ybuf, self.zout, self.zin, self.ys, self.yr, self.zs, self.zr = scratch

    def over(self, t, p):
        q, line = self.line.order(t), self.line
        return remote(self.at(line.at(q, 1 - line.i), p), self.ybuf.at[q, p], self.ys.at[q, p],
                      self.yr.at[q, p], seq=line.at(line.o, 1 - line.i))

    def along(self, t, p):
        q, line = self.line.order(t), self.line
        up = q > line.o
        to = jnp.where(up, line.o + 1, line.o - 1)
        slot = jnp.where(jnp.logical_and(q == to, jnp.logical_not(up)), line.n, q)
        return remote(self.zout.at[q, p], self.zin.at[slot, p], self.zs.at[q, p], self.zr.at[slot, p],
                      seq=line.at(to, line.i))

    def arrived(self, k, p):
        here, line = self.zin.at[k, p], self.line
        remote(here, here, self.zs.at[0, p], self.zr.at[k, p],
               seq=line.at(line.o, 1 - line.i)).wait_recv()

    def open(self):
        for t in range(self.line.n):
            for p in self.pieces:
                self.over(t, p).start()

    def stage(self, t):
        line = self.line
        o, n = line.o, line.n
        q = line.order(t)
        for p in self.pieces:
            self.over(t, p).wait_recv()
            value = self.at(line.at(q, line.i), p)[...].astype(f32) + self.ybuf[q, p].astype(f32)
            if t < n - 1:
                fed = jnp.where(q > o, o > 0, o < n - 1)

                def with_feed(value=value, p=p):
                    self.arrived(q, p)
                    self.zout[q, p] = (value + self.zin[q, p].astype(f32)).astype(bf16)

                def without(value=value, p=p):
                    self.zout[q, p] = value.astype(bf16)

                pl.when(fed)(with_feed)
                pl.when(jnp.logical_not(fed))(without)
                self.along(t, p).start()
            else:
                below, above = o > 0, o < n - 1
                pl.when(below)(lambda p=p: self.arrived(o, p))
                pl.when(above)(lambda p=p: self.arrived(n, p))
                value = value + jnp.where(below, self.zin[o, p].astype(f32), 0.0)
                value = value + jnp.where(above, self.zin[n, p].astype(f32), 0.0)
                self.final(p, value)

    def finish(self):
        for t in range(self.line.n):
            for p in self.pieces:
                self.over(t, p).wait_send()
                if t < self.line.n - 1:
                    self.along(t, p).wait_send()

    def run(self):
        self.open()
        for t in range(self.line.n):
            self.stage(t)
        self.finish()


def scatter_kernel(n_seq, term, out, *scratch):
    line = Line(n_seq)
    greet(line.neighbours())

    def final(p, value):
        out[p] = value

    Scatter(line, lambda q, p: term.at[q, p], range(term.shape[1]), scratch, final).run()


def seq_scatter(x, n_seq, pieces, number):
    rows, width = x.shape[0] // n_seq, x.shape[1]
    part = rows // pieces
    vmem = pl.BlockSpec(memory_space=pltpu.VMEM)
    out = pl.pallas_call(
        partial(scatter_kernel, n_seq),
        in_specs=[vmem],
        out_specs=vmem,
        out_shape=jax.ShapeDtypeStruct((pieces, part, width), f32),
        scratch_shapes=scatter_scratch(n_seq // 2, pieces, part, width),
        compiler_params=pltpu.CompilerParams(
            collective_id=number, has_side_effects=True, vmem_limit_bytes=60 * 1024 * 1024
        ),
        name="seq_scatter",
    )(x.reshape(n_seq, pieces, part, width))
    return out.reshape(rows, width)


class Collect:
    def __init__(self, line, term, out, scratch):
        self.line, self.term, self.out = line, term, out
        self.sumbuf, self.lsem, self.dps, self.dpr = scratch[:4]
        self.n_dp = term.shape[1]
        self.mine = lax.axis_index("dp")
        self.peers = [lax.rem(self.mine + r, self.n_dp) for r in range(1, self.n_dp)]

        def at(q, r):
            return term.at[q, lax.rem(self.mine + r, self.n_dp)]

        def final(r, value):
            self.sumbuf[r] = value.astype(bf16)
            self.back(r).start()

        pieces = list(range(1, self.n_dp)) + [0]
        self.scatter = Scatter(line, at, pieces, scratch[4:], final)
        self.open, self.stage = self.scatter.open, self.scatter.stage

    def back(self, r):
        if r == 0:
            return pltpu.make_async_copy(self.sumbuf.at[0], self.out.at[self.mine], self.lsem)
        return remote(self.sumbuf.at[r], self.out.at[self.mine], self.dps.at[r - 1], self.dpr.at[r - 1],
                      dp=self.peers[r - 1])

    def finish(self):
        self.scatter.finish()
        for r in range(1, self.n_dp):
            here = self.out.at[lax.rem(self.mine + self.n_dp - r, self.n_dp)]
            remote(here, here, self.dps.at[r - 1], self.dpr.at[r - 1],
                   dp=self.peers[r - 1]).wait_recv()
            self.back(r).wait_send()
        self.back(0).wait()


def collect_scratch(n_seq, n_dp, rows, width):
    dma = pltpu.SemaphoreType.DMA
    return [pltpu.VMEM((n_dp, rows, width), bf16), dma, dma((n_dp - 1,)), dma((n_dp - 1,))] + (
        scatter_scratch(n_seq // 2, n_dp, rows, width)
    )


def collect_kernel(n_seq, term, out, *scratch):
    line = Line(n_seq)
    work = Collect(line, term, out, scratch)
    greet(line.neighbours(), work.peers)
    work.open()
    for t in range(line.n):
        work.stage(t)
    work.finish()


def collect_call(x, n_seq, number):
    _, n_dp, rows, width = x.shape
    vmem = pl.BlockSpec(memory_space=pltpu.VMEM)
    return pl.pallas_call(
        partial(collect_kernel, n_seq),
        in_specs=[vmem],
        out_specs=vmem,
        out_shape=jax.ShapeDtypeStruct((n_dp, rows, width), bf16),
        scratch_shapes=collect_scratch(n_seq, n_dp, rows, width),
        compiler_params=pltpu.CompilerParams(
            collective_id=number, has_side_effects=True, vmem_limit_bytes=60 * 1024 * 1024
        ),
        name="collect",
    )(x)


def sum_kernel(n_seq, x, out, inbox, total, lsem, s1, r1, s2, r2):
    me = lax.axis_index("seq")
    peers = [lax.rem(me + r, n_seq) for r in range(1, n_seq)]
    greet([(None, q) for q in peers])
    copies = []
    for r, q in enumerate(peers):
        copy = remote(x.at[q], inbox.at[r], s1.at[r], r1.at[r], seq=q)
        copy.start()
        copies.append(copy)
    value = x[me].astype(f32)
    for r, q in enumerate(peers):
        remote(inbox.at[r], inbox.at[r], s1.at[r], r1.at[r], seq=q).wait_recv()
        value = value + inbox[r].astype(f32)
    total[...] = value.astype(total.dtype)
    for r, q in enumerate(peers):
        copy = remote(total, out.at[me], s2.at[r], r2.at[r], seq=q)
        copy.start()
        copies.append(copy)
    keep = pltpu.make_async_copy(total, out.at[me], lsem)
    keep.start()
    for r, q in enumerate(peers):
        here = out.at[lax.rem(me + n_seq - 1 - r, n_seq)]
        remote(here, here, s2.at[r], r2.at[r], seq=q).wait_recv()
    keep.wait()
    for copy in copies:
        copy.wait_send()


def seq_sum(x, n_seq, number):
    rows, width = x.shape[0] // n_seq, x.shape[1]
    dma = pltpu.SemaphoreType.DMA
    vmem = pl.BlockSpec(memory_space=pltpu.VMEM)
    out = pl.pallas_call(
        partial(sum_kernel, n_seq),
        in_specs=[vmem],
        out_specs=vmem,
        out_shape=jax.ShapeDtypeStruct((n_seq, rows, width), x.dtype),
        scratch_shapes=[pltpu.VMEM((n_seq - 1, rows, width), x.dtype), pltpu.VMEM((rows, width), x.dtype),
                        dma] + [dma((n_seq - 1,)) for _ in range(4)],
        compiler_params=pltpu.CompilerParams(
            collective_id=number, has_side_effects=True, vmem_limit_bytes=60 * 1024 * 1024
        ),
        name="seq_sum",
    )(x.reshape(n_seq, rows, width))
    return out.reshape(n_seq * rows, width)


def all_peers(n_seq):
    me = lax.axis_index("seq")
    return [lax.rem(me + r, n_seq) for r in range(1, n_seq)]


def dp_peers():
    mine = lax.axis_index("dp")
    other = mine + 1 - 2 * lax.rem(mine, 2)
    return mine, other, lax.rem(mine + 2, 4), lax.rem(other + 2, 4)


class Spread:
    def __init__(self, out, sems):
        self.out, (self.s, self.r) = out, sems
        self.mine, self.core, self.far, self.rest = dp_peers()
        self.sent = []

    def push(self, src, place, k, peer):
        copy = remote(src, self.out.at[place], self.s.at[k], self.r.at[k], dp=peer)
        copy.start()
        self.sent.append(copy)

    def wait(self, place, k):
        here = self.out.at[place]
        remote(here, here, self.s.at[k], self.r.at[k], dp=self.core).wait_recv()

    def start(self, src):
        self.push(src, self.mine, 1, self.far)
        self.push(src, self.mine, 0, self.core)

    def forward(self):
        self.wait(self.far, 1)
        self.push(self.out.at[self.far], self.far, 2, self.core)

    def finish(self):
        self.wait(self.core, 0)
        self.wait(self.rest, 2)
        for copy in self.sent:
            copy.wait_send()


def start_kernel(
    n_seq, tok, w_in, wout, side, gains, route, cot,
    xg, w_all, wout_all, side_all, gain_all, cot_own, pick_out,
    wst, gbox, zero_w, zero_s, cst, lsem, tsem, csem, cds, cdr, *sems,
):
    gsems, (a2s, a2r, gs2, gr2), dsems = sems[:5], sems[5:9], sems[9:]
    line = Line(n_seq)
    me = line.me
    peers = all_peers(n_seq)
    mine, core, far, rest = dp_peers()
    greet([(None, q) for q in peers], [core, far, rest])
    keep = pltpu.make_async_copy(tok, xg.at[me], tsem)
    keep.start()
    tokens_of = Gather(line, lambda q, p: xg.at[q, p], lambda p: tok.at[p], tok.shape[0], gsems)
    tokens_of.stage(0)
    locals_ = []

    def local(src, dst, k):
        copy = pltpu.make_async_copy(src, dst, lsem.at[k])
        copy.start()
        locals_.append(copy)

    gain_dp = Spread(gbox, dsems[0:2])
    gbox[mine] = gains[...]
    gain_dp.start(gains)
    w_dp = Spread(w_all, dsems[2:4])
    wout_dp = Spread(wout_all, dsems[4:6])
    side_dp = Spread(side_all, dsems[6:8])
    side_dp.start(side)
    wout_dp.start(wout)
    local(wout, wout_all.at[mine], 0)
    local(side, side_all.at[mine], 1)
    zero_w[...] = jnp.zeros_like(zero_w)
    zero_s[...] = jnp.zeros_like(zero_s)

    here = route.shape[0]
    n_dp, slots, _ = cot_own.shape
    expert = lax.broadcasted_iota(jnp.int32, (here, n_dp), 1)
    onehot = jnp.where(route[...] == expert, 1.0, 0.0)
    earlier = lax.broadcasted_iota(jnp.int32, (here, here), 1) < lax.broadcasted_iota(
        jnp.int32, (here, here), 0
    )
    before = mm(jnp.where(earlier, 1.0, 0.0).astype(bf16), onehot.astype(bf16))
    index = jnp.sum(before * onehot, axis=1, keepdims=True)
    target = route[...] * slots + index.astype(jnp.int32)
    slot = lax.broadcasted_iota(jnp.int32, (here, n_dp * slots), 1)
    pick = jnp.where(target == slot, 1.0, 0.0).astype(bf16)
    pick_out[...] = pick
    for e in range(n_dp):
        cst[e] = mm(pick[:, e * slots : (e + 1) * slots], cot[...], TN).astype(bf16)
    copies = []
    for k, peer in enumerate((core, far, rest)):
        copy = remote(cst.at[peer], cot_own.at[mine], cds.at[k], cdr.at[k], dp=peer)
        copy.start()
        copies.append(copy)
    keep_cot = pltpu.make_async_copy(cst.at[mine], cot_own.at[mine], csem)
    keep_cot.start()

    high, wide = w_in.shape
    cpd = wide // (2 * 4 * n_seq)
    half = wst.shape[2] // 2
    values = w_in[...].astype(f32)
    for q in range(n_seq):
        for side_of in range(2):
            first = side_of * 4 * n_seq
            parts = [
                values[:, (first + p * n_seq + q) * cpd : (first + p * n_seq + q + 1) * cpd]
                for p in range(4)
            ]
            if half > 4 * cpd:
                parts.append(jnp.zeros((high, half - 4 * cpd), f32))
            wst[q, :, side_of * half : (side_of + 1) * half] = jnp.concatenate(
                parts, axis=1
            ).astype(bf16)
    for r, q in enumerate(peers):
        copy = remote(wst.at[q], w_all.at[mine, me], a2s.at[r], a2r.at[r], seq=q)
        copy.start()
        copies.append(copy)
    local(wst.at[me], w_all.at[mine, me], 2)
    extra = wout_all.shape[0] - 4
    for k in range(extra):
        local(zero_w, wout_all.at[4 + k], 3 + 2 * k)
        local(zero_s, side_all.at[4 + k], 4 + 2 * k)
    gain_dp.forward()
    gain_dp.finish()
    for r, q in enumerate(peers):
        copy = remote(gbox, gain_all.at[me], gs2.at[r], gr2.at[r], seq=q)
        copy.start()
        copies.append(copy)
    gain_all[me] = gbox[...]
    tokens_of.stage(1)
    for r, q in enumerate(peers):
        here = w_all.at[mine, lax.rem(me + n_seq - 1 - r, n_seq)]
        remote(here, here, a2s.at[r], a2r.at[r], seq=q).wait_recv()
    for copy in locals_:
        copy.wait()
    w_dp.start(w_all.at[mine])
    if line.n > 2:
        tokens_of.stage(2)
    side_dp.forward()
    wout_dp.forward()
    for k in range(3, line.n):
        tokens_of.stage(k)
    w_dp.forward()
    tokens_of.finish()
    side_dp.finish()
    wout_dp.finish()
    for r, q in enumerate(peers):
        here = gain_all.at[lax.rem(me + n_seq - 1 - r, n_seq)]
        remote(here, here, gs2.at[r], gr2.at[r], seq=q).wait_recv()
    for k, peer in enumerate((core, far, rest)):
        remote(cot_own.at[peer], cot_own.at[peer], cds.at[k], cdr.at[k], dp=peer).wait_recv()
    keep_cot.wait()
    keep.wait()
    w_dp.finish()
    for copy in copies:
        copy.wait_send()


def start_call(tokens, w_in, w_out, side, gains, route, cot, slots, n_seq, cp, number):
    here, d_model = tokens.shape
    high, _ = w_in.shape
    cpd, n_side = side.shape
    extra = -(-cp // cpd) - 4
    dma = pltpu.SemaphoreType.DMA
    anyw, vmem = pl.BlockSpec(memory_space=pl.ANY), pl.BlockSpec(memory_space=pltpu.VMEM)
    sds = jax.ShapeDtypeStruct
    return pl.pallas_call(
        partial(start_kernel, n_seq),
        in_specs=[anyw, vmem, anyw, anyw, vmem, vmem, vmem],
        out_specs=[anyw, anyw, anyw, anyw, vmem, anyw, vmem],
        out_shape=[
            sds((n_seq, 2, here // 2, d_model), bf16),
            sds((4, n_seq, high, 2 * cp), bf16),
            sds((4 + extra, cpd, d_model), bf16),
            sds((4 + extra, cpd, n_side), bf16),
            sds((n_seq, 4, 8, 128), f32),
            sds((4, slots, d_model), bf16),
            sds((here, 4 * slots), bf16),
        ],
        scratch_shapes=[
            pltpu.VMEM((n_seq, high, 2 * cp), bf16), pltpu.VMEM((4, 8, 128), f32),
            pltpu.VMEM((cpd, d_model), bf16), pltpu.VMEM((cpd, n_side), bf16),
            pltpu.VMEM((4, slots, d_model), bf16),
            dma((3 + 2 * extra,)), dma, dma, dma((3,)), dma((3,)),
        ] + gather_sems(n_seq // 2, 2) + [dma((n_seq - 1,)) for _ in range(4)]
        + [dma((3,)) for _ in range(8)],
        compiler_params=pltpu.CompilerParams(
            collective_id=number, has_side_effects=True, vmem_limit_bytes=60 * 1024 * 1024
        ),
        name="startup",
    )(tokens.reshape(2, here // 2, d_model), w_in, w_out, side, gains, route, cot)


class Fold:
    def __init__(self, arr, box, send, sems):
        self.arr, self.box, self.send, (self.s, self.r) = arr, box, send, sems
        self.mine, self.core, self.far, self.rest = dp_peers()
        self.sent = []

    def push(self, src, k, peer):
        copy = remote(src, self.box.at[k], self.s.at[k], self.r.at[k], dp=peer)
        copy.start()
        self.sent.append(copy)

    def wait(self, k):
        remote(self.box.at[k], self.box.at[k], self.s.at[k], self.r.at[k], dp=self.core).wait_recv()

    def start(self):
        self.push(self.arr.at[self.rest], 1, self.core)
        self.push(self.arr.at[self.core], 0, self.core)

    def middle(self):
        self.wait(1)
        value = self.arr[self.far].astype(f32) + self.box[1].astype(f32)
        self.send[...] = value.astype(self.send.dtype)
        self.push(self.send, 2, self.far)

    def final(self):
        self.wait(0)
        self.wait(2)
        value = self.arr[self.mine].astype(f32) + self.box[0].astype(f32)
        return value + self.box[2].astype(f32)

    def done(self):
        for copy in self.sent:
            copy.wait_send()


def finish_kernel(
    n_seq, term, gwout, gw, pack, tok, gres, gains, ggmoe,
    gtok_out, gwout_out, pack_out, gwin_out, gain_out,
    gn, wsum, wbox, gst, gb1, gsum, gb2, o_box, o_send, w_box, w_send, p_box, p_send, lsem, *sems,
):
    scratch, (a2s, a2r, g1s, g1r, g2s, g2r), dsems = sems[:7], sems[7:13], sems[13:]
    line = Line(n_seq)
    me = line.me
    peers = all_peers(n_seq)
    mine, core, far, rest = dp_peers()
    dps = [core, far, rest]
    greet([(None, q) for q in peers], dps)
    f_w = Fold(gw, w_box, w_send, dsems[0:2])
    f_o = Fold(gwout, o_box, o_send, dsems[2:4])
    f_p = Fold(pack, p_box, p_send, dsems[4:6])
    for fold in (f_w, f_o, f_p):
        fold.start()

    def final(p, value):
        gn[p] = value

    sums = Scatter(line, lambda q, p: term.at[q, p], range(term.shape[1]), scratch, final)
    sums.open()
    for fold in (f_w, f_o, f_p):
        fold.middle()
    sums.stage(0)
    wsum[...] = f_w.final().astype(bf16)
    copies = []
    for r, q in enumerate(peers):
        copy = remote(wsum.at[q], wbox.at[me], a2s.at[r], a2r.at[r], seq=q)
        copy.start()
        copies.append(copy)
    keep = pltpu.make_async_copy(wsum.at[me], wbox.at[me], lsem)
    keep.start()
    if line.n > 1:
        sums.stage(1)
    gwout_out[...] = f_o.final()
    pack_out[...] = f_p.final()
    for t in range(2, line.n):
        sums.stage(t)
    sums.finish()

    v = tok[...].astype(f32)
    r_ = lax.rsqrt(jnp.mean(v * v, axis=-1, keepdims=True) + eps)
    gy = jnp.concatenate([gn[p] for p in range(gn.shape[0])], axis=0)
    gst[0:1, :] = jnp.sum(gy * (v * r_), axis=0, keepdims=True)
    gst[1:2, :] = ggmoe[...]
    gsends = []
    for k, peer in enumerate(dps):
        copy = remote(gst, gb1.at[k], g1s.at[k], g1r.at[k], dp=peer)
        copy.start()
        gsends.append(copy)
    gyg = gy * gains[0:1, :]
    inner = jnp.mean(gyg * v, axis=-1, keepdims=True)
    gtok_out[...] = gyg * r_ - v * (r_ * r_ * r_ * inner) + gres[...]
    total = gst[...]
    for k in range(3):
        remote(gb1.at[k], gb1.at[k], g1s.at[k], g1r.at[k], dp=core).wait_recv()
        total = total + gb1[k]
    gsum[...] = total
    for r, q in enumerate(peers):
        copy = remote(gsum, gb2.at[r], g2s.at[r], g2r.at[r], seq=q)
        copy.start()
        gsends.append(copy)

    keep.wait()
    for r, q in enumerate(peers):
        here = wbox.at[lax.rem(me + n_seq - 1 - r, n_seq)]
        remote(here, here, a2s.at[r], a2r.at[r], seq=q).wait_recv()
    wide = gwin_out.shape[1]
    cpd = wide // (2 * 4 * n_seq)
    half = wbox.shape[2] // 2
    for q in range(n_seq):
        block = wbox[q].astype(f32)
        for side_of in range(2):
            for p in range(4):
                at = (side_of * 4 * n_seq + p * n_seq + q) * cpd
                src = side_of * half + p * cpd
                gwin_out[:, at : at + cpd] = block[:, src : src + cpd]
    for r, q in enumerate(peers):
        remote(gb2.at[r], gb2.at[r], g2s.at[r], g2r.at[r], seq=q).wait_recv()
        total = total + gb2[r]
    gain_out[...] = total
    for fold in (f_w, f_o, f_p):
        fold.done()
    for copy in copies + gsends:
        copy.wait_send()


def finish_call(gpart, gwout, gw, pack, tokens, gres, gains, ggmoe, n_seq, number):
    here, d_model = tokens.shape
    _, _, high, wide = gw.shape
    _, cpd, n_side = pack.shape
    dma = pltpu.SemaphoreType.DMA
    vmem = pl.BlockSpec(memory_space=pltpu.VMEM)
    sds = jax.ShapeDtypeStruct
    mem = pltpu.VMEM
    return pl.pallas_call(
        partial(finish_kernel, n_seq),
        in_specs=[vmem] * 8,
        out_specs=[vmem] * 5,
        out_shape=[
            sds((here, d_model), f32), sds((cpd, d_model), f32), sds((cpd, n_side), f32),
            sds((high, 2 * 4 * n_seq * cpd), f32), sds((2, d_model), f32),
        ],
        scratch_shapes=[
            mem((2, here // 2, d_model), f32), mem((n_seq, high, wide), bf16), mem((n_seq, high, wide), bf16),
            mem((2, d_model), f32), mem((3, 2, d_model), f32), mem((2, d_model), f32),
            mem((n_seq - 1, 2, d_model), f32),
            mem((3, cpd, d_model), bf16), mem((cpd, d_model), bf16),
            mem((3, n_seq, high, wide), bf16), mem((n_seq, high, wide), bf16),
            mem((3, cpd, n_side), f32), mem((cpd, n_side), f32), dma,
        ] + scatter_scratch(n_seq // 2, 2, here // 2, d_model)
        + [dma((n_seq - 1,)), dma((n_seq - 1,)), dma((3,)), dma((3,)), dma((n_seq - 1,)), dma((n_seq - 1,))]
        + [dma((3,)) for _ in range(6)],
        compiler_params=pltpu.CompilerParams(
            collective_id=number, has_side_effects=True, vmem_limit_bytes=62 * 1024 * 1024
        ),
        name="finish",
    )(gpart.reshape(n_seq, 2, here // 2, d_model), gwout, gw, pack, tokens, gres, gains, ggmoe)


def on_device(
    tokens, route, cotangent, gain_mix, w_in, conv_w, w_x, w_dt, dt_bias, a_log, d_skip, w_out,
    gain_moe, w_up, w_down,
):
    n_seq, n_dp = lax.axis_size("seq"), lax.axis_size("dp")
    here, d_model = tokens.shape
    cpd = conv_w.shape[0]
    chans = cpd * n_dp
    cp = up128(chans)
    rank = w_dt.shape[1]
    n_small = w_x.shape[1]
    sp = up128(n_small)
    tall = here * n_seq
    rows_in = w_in.shape[0]
    experts, slots = n_dp, 40

    gap = jnp.zeros((cpd, 128), bf16)
    side = jnp.concatenate(
        [w_x, gap[:, n_small:], w_dt, gap[:, rank:], conv_w, gap[:, 4:8], dt_bias[:, None],
         d_skip[:, None], gap[:, 10:16], a_log, gap[:, 32:]], axis=1,
    )
    gains_in = jnp.pad(jnp.stack([gain_mix, gain_moe]).astype(f32), ((0, 6), (0, 128 - gain_mix.shape[0])))
    xg, w_all, wout_all, side_all, gain_all, cot_own, pick = start_call(
        tokens, w_in, w_out, side, gains_in, route, cotangent, slots, n_seq, cp, 0
    )
    toks = xg.reshape(tall, d_model)
    w_mine = w_all.reshape(n_dp * n_seq * rows_in, 2 * cp)
    wout_m = wout_all.reshape(-1, d_model)
    side_m = side_all.reshape(-1, 384)
    gains = gain_all[:, :, :2, : gain_mix.shape[0]].transpose(2, 1, 0, 3).reshape(2, d_model)
    wout_spec = (((cp, d_model), 0),)
    wx_spec, wdt_spec, misc_spec = [(((cp, 128), k),) for k in range(3)]

    row_values = tokens.astype(f32)
    tb = 128
    steps = tall // tb
    sds = jax.ShapeDtypeStruct
    wide = sds((tall, cp), f32)
    vec = pltpu.VMEM((tb, cp), f32)
    turned_misc = pltpu.VMEM((128, cp), f32)
    by_state = pltpu.VMEM((NS, cp), f32)
    x, z, conv, small, normed = chunked(
        in_kernel, steps, False,
        [(toks, tb), (gains, 0), (w_mine, 0), (side_m, wx_spec), (side_m, misc_spec)],
        [(wide, tb), (wide, tb), (wide, tb), (sds((tall, sp), bf16), tb), (sds((tall, d_model), bf16), tb)],
        [pltpu.VMEM((tb + 8, cp), f32), turned_misc], "mix_in",
    )
    small = seq_sum(small, n_seq, 1)
    bct = small[:, rank:n_small].astype(f32).reshape(tall // 8, 8, 2 * NS).transpose(0, 2, 1)
    dtp, hs, ssm, gated, part, grad_slots = chunked(
        partial(scan_kernel, n_seq, steps), steps, False,
        [(small, tb), (bct, tb // 8), (side_m, wdt_spec), (side_m, misc_spec), (conv, tb), (z, tb),
         (wout_m, wout_spec), (cot_own, None)],
        [(wide, tb), (sds((tall, NS, cp), f32), tb), (wide, tb), (sds((tall, cp), bf16), tb),
         (sds((tall, d_model), bf16), tb), (sds((n_seq, n_dp, slots, d_model), bf16), None)],
        [vec, vec, by_state, turned_misc, by_state, pltpu.SemaphoreType.DMA]
        + gather_sems(n_seq // 2, n_dp),
        "scan_forward", 3,
    )
    grad_slots = grad_slots.reshape(n_seq * n_dp * slots, d_model)
    mixer_out = seq_scatter(part, n_seq, 2, 2)
    resid = row_values + mixer_out

    normed2, norm2_pullback = jax.vjp(rms_norm, resid, gains[1])
    moe_in = normed2.astype(bf16)
    def dispatch(values, number):
        send = mm(pick, values, TN).astype(bf16).reshape(n_dp, slots, d_model)
        return dispatch_call(send, n_seq, number).reshape(n_seq * n_dp * slots, d_model)

    def returned(sums):
        return mm(pick, sums.reshape(n_dp * slots, d_model))

    shape4 = (n_seq, n_dp, slots, d_model)
    up, down = w_up[0], w_down[0]
    grad_hidden = mm(grad_slots, down, NT)
    slot_rows = dispatch(moe_in, 4)
    pre_act = mm(slot_rows, up, NT)
    hidden_f, gelu_pullback = jax.vjp(partial(jax.nn.gelu, approximate=False), pre_act)
    hidden = hidden_f.astype(bf16)
    grad_pre = gelu_pullback(grad_hidden)[0].astype(bf16)
    grad_moe_in = returned(collect_call(mm(grad_pre, up).astype(bf16).reshape(shape4), n_seq, 5))
    expert_terms = mm(hidden, down).astype(bf16).reshape(shape4)
    grad_down = mm(hidden, grad_slots, TN)
    grad_up = mm(grad_pre, slot_rows, TN)

    grad_resid, grad_gmoe = norm2_pullback(grad_moe_in)
    grad_resid = grad_resid + cotangent.astype(f32)
    gml = seq_gather(grad_resid.astype(bf16), n_seq, 2, 7)
    grad_rank, gbct, gu, gz, gwout, gwdt, gmisc, expert_out = chunked(
        partial(back_kernel, n_seq, steps), steps, True,
        [(gml, tb), (wout_m, wout_spec), (gated, tb), (conv, tb), (z, tb), (ssm, tb), (dtp, tb), (hs, tb),
         (hs, -tb), (bct, tb // 8), (small, tb), (side_m, wdt_spec), (side_m, misc_spec),
         (expert_terms, 0)],
        [(sds((tall, sp), f32), tb), (sds((tall // 8, 2 * NS, 8), f32), tb // 8), (wide, tb),
         (sds((tall, cp), bf16), tb), (sds((n_dp, cpd, d_model), bf16), 0), (sds((cp, sp), f32), 0),
         (sds((32, cp), f32), 0), (sds((n_dp, slots, d_model), bf16), None)],
        [vec] * 5 + [by_state, turned_misc, by_state, pltpu.VMEM((cp, d_model), f32), by_state]
        + collect_scratch(n_seq, n_dp, slots, d_model),
        "scan_backward", 6,
    )
    result = (resid + returned(expert_out)).astype(bf16)
    grad_bc = gbct.transpose(0, 2, 1).reshape(tall, 2 * NS)
    gsmall = jnp.concatenate([grad_rank[:, :rank], grad_bc], axis=1)
    gsmall = seq_sum(jnp.pad(gsmall, ((0, 0), (0, sp - n_small))).astype(bf16), n_seq, 8)
    gpart, gw, gpack = chunked(
        out_kernel, steps, True,
        [(gsmall, tb), (side_m, wx_spec), (side_m, misc_spec), (conv, tb), (x, tb), (gu, tb), (gz, tb),
         (normed, tb), (w_mine, 0), (gwdt, 0), (gmisc, 0)],
        [(sds((tall, d_model), bf16), tb), (sds((n_dp, n_seq, rows_in, 2 * cp), bf16), 0),
         (sds((n_dp, cpd, 384), f32), 0)],
        [pltpu.VMEM((tb + 8, cp), f32), turned_misc, pltpu.VMEM((cp, sp), f32),
         pltpu.VMEM((d_model, 2 * cp), f32), turned_misc], "mix_out",
    )
    grad_tokens, grad_wout, gpack, grad_win, ggains = finish_call(
        gpart, gwout, gw, gpack, tokens, grad_resid, gains, grad_gmoe[None], n_seq, 9
    )
    own = gain_mix.shape[0]
    ggains = lax.dynamic_slice(
        ggains, (0, (lax.axis_index("dp") * n_seq + lax.axis_index("seq")) * own), (2, own)
    )
    return (
        result, grad_tokens, ggains[0], grad_win, gpack[:, 256:260], gpack[:, :n_small],
        gpack[:, 128 : 128 + rank], gpack[:, 264], gpack[:, 272 : 272 + NS], gpack[:, 265],
        grad_wout, ggains[1], grad_up[None], grad_down[None],
    )


def solution(mesh):
    row2, row1 = P(("dp", "seq"), None), P(("dp", "seq"))
    mats = P("dp", "seq", None)
    return jax.shard_map(
        on_device,
        mesh=mesh,
        in_specs=(
            row2, row2, row2, row1, row2, row2, row2, row2, row1, row2, row1, row2, row1, mats, mats
        ),
        out_specs=(
            row2, row2, row1, row2, row2, row2, row2, row1, row2, row1, row2, row1, mats, mats
        ),
        check_vma=False,
    )
```

time: 667 us -> 481 us (0.72)
  blocking collectives: 115 us -> 0 us
  Pallas kernels: 431 us -> 417 us
  between operations: 14.5 us -> 0.95 us
  local copies, waits for them, and re-layouts: 40.9 us -> 27.6 us
  starting transfers between devices: 12.8 us -> 0 us
  other arithmetic: 17.3 us -> 7.5 us
    all_gather x2 -> x0, blocking collectives: 76.7 us -> none  [the longest x1 68 us: on_device(): lax.all_gather(jnp.stack([gain_mix, gain_moe]), both, axis=1, tiled=True)]
    pallas_call x2 -> x3, Pallas kernels: 78 us -> 133 us  [the longest x1 49 us: finish_call(): pl.pallas_call(partial(finish_kernel, n_seq), in_specs=[vmem] * 8, out_sp...]
    unnamed x1 -> x0, blocking collectives: 38.1 us -> none
    pallas_call x2 -> x1, Pallas kernels: 77.7 us -> 41.6 us  [dispatch_call(): pl.pallas_call(partial(dispatch_kernel, n_seq, n_dp), in_specs=[pl.BlockS...]
    pallas_call x2 -> x1, Pallas kernels: 64 us -> 30.3 us  [seq_scatter(): pl.pallas_call(partial(scatter_kernel, n_seq), in_specs=[vmem], out_specs...]
    pallas_call x4, Pallas kernels: 121 us -> 148 us  [chunked(): pl.pallas_call(kernel, grid=(steps,), in_specs=[spec(a.shape, r) for a, r...]
    pallas_call x2 -> x1, Pallas kernels: 54 us -> 29.4 us  [seq_gather(): pl.pallas_call(partial(gather_kernel, n_seq), in_specs=[pl.BlockSpec(memo...]
    all_to_all x2 -> x0, starting transfers between devices: 12.7 us -> none  [the longest x1 7.44 us: on_device(): lax.all_to_all(w_cols.reshape(n_seq, rows_in, 2 * cp), 'seq', 0, 0, tiled...]
  transfers between devices with their start and end apart: 6 -> 0, of which waited for: 1 -> 0; matrix products, arithmetic and copies ran while one was open for 7% -> 0% of each run, Pallas kernels for 20% -> 0%
where the time goes in v3:
time: 481 us; the launch traced here: 480 us
  Pallas kernels  417 us (87%)
  local copies, waits for them, and re-layouts  27.6 us (6%)
  matrix products  26.5 us (6%)
  other arithmetic  7.5 us (2%)
    pallas_call x4, Pallas kernels, chunked(): pl.pallas_call(kernel, grid=(steps,), in_specs=[spec(a.shape, r) for a, r...  148 us
    pallas_call x1, Pallas kernels, finish_call(): pl.pallas_call(partial(finish_kernel, n_seq), in_specs=[vmem] * 8, out_sp...  49 us
    pallas_call x1, Pallas kernels, start_call(): pl.pallas_call(partial(start_kernel, n_seq), in_specs=[anyw, vmem, anyw,...  45.6 us
    pallas_call x1, Pallas kernels, dispatch_call(): pl.pallas_call(partial(dispatch_kernel, n_seq, n_dp), in_specs=[pl.BlockS...  41.6 us
    pallas_call x1, Pallas kernels, collect_call(): pl.pallas_call(partial(collect_kernel, n_seq), in_specs=[vmem], out_specs...  38.3 us
    pallas_call x2, Pallas kernels, seq_sum(): pl.pallas_call(partial(sum_kernel, n_seq), in_specs=[vmem], out_specs=vme...  34.9 us
    pallas_call x1, Pallas kernels, seq_scatter(): pl.pallas_call(partial(scatter_kernel, n_seq), in_specs=[vmem], out_specs...  30.3 us
    pallas_call x1, Pallas kernels, seq_gather(): pl.pallas_call(partial(gather_kernel, n_seq), in_specs=[pl.BlockSpec(memo...  29.4 us

profile of v3, /device:TPU:0, one launch (start us, length us, event | category | flops | bytes accessed | tf_op | source)
XLA Modules:
  0.0 479.5 jit_solution(8489909131993919569)
XLA Ops:
  0.7 1.4 fusion.28.gains
  2.0 0.8 copy.38
  2.8 0.8 copy.39
  3.6 0.8 copy.41
  4.4 0.8 copy.40
  5.2 1.5 concatenate.7.side
  6.7 1.4 copy.42.route
  8.1 45.6 %startup.1 = (bf16[8,2,64,1152]{3,2,1,0:T(8,128)(2,1)}, bf16[4,8,36,768]{3,2,1,0:T(8,128)(2,1)}, bf16[6,72,1152]{2,1,0:T(8,128)(2,1)}, bf16[6,72,384]{2,1,0:T(8,...) custom-call(bf16[2,64,1152]{2,1,0:T(8,128)(2,1)} %bitcast.96, ...), custom_call_target="tpu_custom_call" | custom-call | tf_op jit(solution)/shard_map/startup/pallas_call | solution.py:940
  53.6 0.9 slice_bitcast_fusion.1
  54.6 0.7 reshape.127.gain.gains
  55.4 3.7 reshape.128.w
  59.1 9.4 %mix_in.1 = (f32[1024,384]{1,0:T(8,128)}, f32[1024,384]{1,0:T(8,128)}, f32[1024,384]{1,0:T(8,128)}, bf16[1024,128]{1,0:T(8,128)(2,1)}, bf16[1024,1152]{1,0:T(8,128)(2,1)}) custom-call(bf16[1024,1152]{1,0:T(8,128)(2,1)} %bitcast.99, f32[2,1152]{1,0:T(2,128)} %reshape.127.gain.gains, bf16[1152,768]{1,0:T(8,128)(2,1)} %reshape.128.w, ...), custom_call_target="tpu_custom_call" | custom-call | tf_op jit(solution)/shard_map/mix_in/pallas_call | solution.py:331
  68.5 18.0 %seq_sum.2 = bf16[8,128,128]{2,1,0:T(8,128)(2,1)} custom-call(bf16[8,128,128]{2,1,0:T(8,128)(2,1)} %bitcast.107), custom_call_target="tpu_custom_call" | custom-call | tf_op jit(solution)/shard_map/seq_sum/pallas_call | solution.py:757
  86.4 1.1 fusion.21
  87.5 1.9 copy.44
  89.4 36.7 %scan_forward.1 = (f32[1024,384]{1,0:T(8,128)}, f32[1024,16,384]{2,1,0:T(8,128)}, f32[1024,384]{1,0:T(8,128)}, bf16[1024,384]{1,0:T(8,128)(2,1)}, bf16[1024,1152...) custom-call(bf16[1024,128]{1,0:T(8,128)(2,1)} %bitcast.88, f32[128,32,8]{2,1,0:T(8,128)} %bitcast.84, ...), custom_call_target="tpu_custom_call" | custom-call | tf_op jit(solution)/shard_map/scan_forward/pallas_call | solution.py:331
  126.2 30.3 %seq_scatter.1 = f32[2,64,1152]{2,1,0:T(8,128)} custom-call(bf16[8,2,64,1152]{3,2,1,0:T(8,128)(2,1)} %bitcast.98), custom_call_target="tpu_custom_call" | custom-call | tf_op jit(solution)/shard_map/seq_scatter/pallas_call | solution.py:643
  156.5 1.2 multiply_reduce_fusion.2
  157.8 1.1 convolution_convert_fusion.2
  158.8 41.6 %dispatch.1 = bf16[8,4,40,1152]{3,2,1,0:T(8,128)(2,1)} custom-call(bf16[4,40,1152]{2,1,0:T(8,128)(2,1)} %bitcast.100), custom_call_target="tpu_custom_call" | custom-call | tf_op jit(solution)/shard_map/dispatch/pallas_call | solution.py:538
  200.4 7.5 %multiply_convert_fusion = (bf16[1280,384]{1,0:T(8,128)(2,1)S(1)}, f32[1280,384]{1,0:T(8,128)S(1)}, f32[1280,384]{1,0:T(8,128)S(1)}) fusion(bf16[1280,1152]{1,0:T(8,128)(2,1)} %bitcast.93, bf16[1,384,1152]{2,1,0:T(8,128)(2,1)S(1)} %copy-done), kind=kOutput, calls=%fused_computation.9 | convolution fusion | flops 1164410880 | bytes 8749056 | tf_op jit(solution)/shard_map/dot_general | solution.py:23
  208.0 2.4 add_convert_fusion
  210.4 2.7 convolution_bitcast_fusion
  213.1 2.7 convolution_bitcast_fusion.1
  215.8 3.4 convolution_convert_fusion.1
  219.2 38.3 %collect.1 = bf16[4,40,1152]{2,1,0:T(8,128)(2,1)} custom-call(bf16[8,4,40,1152]{3,2,1,0:T(8,128)(2,1)} %bitcast.95), custom_call_target="tpu_custom_call" | custom-call | tf_op jit(solution)/shard_map/collect/pallas_call | solution.py:712
  257.5 1.3 multiply_reduce_fusion
  259.5 1.1 fusion.31
  260.6 3.5 convolution_convert_fusion
  264.0 29.4 %seq_gather.1 = bf16[8,2,64,1152]{3,2,1,0:T(8,128)(2,1)} custom-call(bf16[2,64,1152]{2,1,0:T(8,128)(2,1)} %bitcast.102), custom_call_target="tpu_custom_call" | custom-call | tf_op jit(solution)/shard_map/seq_gather/pallas_call | solution.py:493
  293.4 85.3 %scan_backward.1 = (f32[1024,128]{1,0:T(8,128)}, f32[128,32,8]{2,1,0:T(8,128)}, f32[1024,384]{1,0:T(8,128)}, bf16[1024,384]{1,0:T(8,128)(2,1)}, bf16[4,72,1152]{...) custom-call(bf16[1024,1152]{1,0:T(8,128)(2,1)} %bitcast.86, ...), custom_call_target="tpu_custom_call" | custom-call | tf_op jit(solution)/shard_map/scan_backward/pallas_call | solution.py:331
  378.7 1.9 fusion
  380.7 1.1 slice.82
  381.8 1.8 convert_bitcast_fusion
  384.0 0.9 fusion.20
  384.8 16.9 %seq_sum.3 = bf16[8,128,128]{2,1,0:T(8,128)(2,1)} custom-call(bf16[8,128,128]{2,1,0:T(8,128)(2,1)} %bitcast.105), custom_call_target="tpu_custom_call" | custom-call | tf_op jit(solution)/shard_map/seq_sum/pallas_call | solution.py:757
  401.7 16.6 %mix_out.1 = (bf16[1024,1152]{1,0:T(8,128)(2,1)}, bf16[4,8,36,768]{3,2,1,0:T(8,128)(2,1)}, f32[4,72,384]{2,1,0:T(8,128)}) custom-call(bf16[1024,128]{1,0:T(8,128)(2,1)} %bitcast.104, bf16[432,384]{1,0:T(8,128)(2,1)} %bitcast.82, bf16[432,384]{1,0:T(8,128)(2,1)} %bitcast.83, f32[1024,384]{1,0:T(8,128)} %get-tuple-element.53.conv, ...), custom_call_target="tpu_custom_call" | custom-call | tf_op jit(solution)/shard_map/mix_out/pallas_call | solution.py:331
  418.4 49.0 %finish.1 = (f32[128,1152]{1,0:T(8,128)}, f32[72,1152]{1,0:T(8,128)}, f32[72,384]{1,0:T(8,128)}, f32[36,4608]{1,0:T(8,128)}, f32[2,1152]{1,0:T(2,128)}) custom-call(bf16[8,2,64,1152]{3,2,1,0:T(8,128)(2,1)} %bitcast.97, bf16[4,72,1152]{2,1,0:T(8,128)(2,1)} %get-tuple-element.74.gwout, bf16[4,8,36,768]{3,2,1,0:T(8,128)(2,1)} %get-tuple-element.75.gw, ...), custom_call_target="tpu_custom_call" | custom-call | tf_op jit(solution)/shard_map/finish/pallas_call | solution.py:1099
  467.4 0.8 constant_dynamic-slice_fusion
  468.7 1.6 slice_reduce_fusion
  470.3 0.8 slice.67
  471.1 0.7 copy.48
  471.8 1.4 slice.65
  473.2 1.4 slice.64
  474.6 0.8 slice.63
  476.0 1.9 copy.52
  477.9 0.9 copy.53
  478.8 0.7 copy.54
  (35 shorter events, 2.4 us)
Async XLA Ops:
  0.6 199.7 %copy-start = (bf16[1,384,1152]{2,1,0:T(8,128)(2,1)S(1)}, bf16[1,384,1152]{2,1,0:T(8,128)(2,1)}, u32[]{:S(2)}) copy-start(bf16[1,384,1152]{2,1,0:T(8,128)(2,1)} %param.28) | copy-start | bytes 2654212
  126.2 30.3 %copy-start.3 = (bf16[128,1152]{1,0:T(8,128)(2,1)S(1)}, bf16[128,1152]{1,0:T(8,128)(2,1)}, u32[]{:S(2)}) copy-start(bf16[128,1152]{1,0:T(8,128)(2,1)} %tok.1) | copy-start | bytes 884740
  126.2 31.6 %copy-start.6 = (bf16[128,160]{1,0:T(8,128)(2,1)S(1)}, bf16[128,160]{1,0:T(8,128)(2,1)}, u32[]{:S(2)}) copy-start(bf16[128,160]{1,0:T(8,128)(2,1)} %get-tuple-element.58) | copy-start | bytes 122884
  200.4 7.5 %copy-start.8 = (bf16[8,4,40,1152]{3,2,1,0:T(8,128)(2,1)S(1)}, bf16[8,4,40,1152]{3,2,1,0:T(8,128)(2,1)}, u32[]{:S(2)}) copy-start(bf16[8,4,40,1152]{3,2,1,0:T(8,128)(2,1)} %get-tuple-element.59) | copy-start | bytes 8847364
  200.4 7.5 %copy-start.9 = (bf16[1,384,1152]{2,1,0:T(8,128)(2,1)S(1)}, bf16[1,384,1152]{2,1,0:T(8,128)(2,1)}, u32[]{:S(2)}) copy-start(bf16[1,384,1152]{2,1,0:T(8,128)(2,1)} %param.29) | copy-start | bytes 2654212
  210.4 2.7 copy-start.2
  219.2 40.3 %copy-start.4 = (bf16[128,1152]{1,0:T(8,128)(2,1)S(1)}, bf16[128,1152]{1,0:T(8,128)(2,1)}, u32[]{:S(2)}) copy-start(bf16[128,1152]{1,0:T(8,128)(2,1)} %cot.1) | copy-start | bytes 884740
  418.4 61.1 %copy-start.1 = (bf16[1,384,1152]{2,1,0:T(8,128)(2,1)S(1)}, bf16[1,384,1152]{2,1,0:T(8,128)(2,1)}, u32[]{:S(2)}) copy-start(bf16[1,384,1152]{2,1,0:T(8,128)(2,1)} %param.28) | copy-start | bytes 2654212
  467.4 10.6 %copy-start.5 = (f32[36,4608]{1,0:T(8,128)S(1)}, f32[36,4608]{1,0:T(8,128)}, u32[]{:S(2)}) copy-start(f32[36,4608]{1,0:T(8,128)} %get-tuple-element.141) | copy-start | bytes 1990660
  467.4 11.4 %copy-start.7 = (f32[72,1152]{1,0:T(8,128)S(1)}, f32[72,1152]{1,0:T(8,128)}, u32[]{:S(2)}) copy-start(f32[72,1152]{1,0:T(8,128)} %get-tuple-element.148) | copy-start | bytes 995332

commit v4 on v3

--- a/solution.py
+++ b/solution.py
@@ -8,6 +8,7 @@
 from jax.sharding import PartitionSpec as P
 
 NS = 16
+B_AT, C_AT = 80, 96
 LN2 = 0.6931471805599453
 LOG2E = 1.4426950408889634
 eps = 1e-05
@@ -58,8 +59,32 @@
     return misc[...].astype(f32).T
 
 
-def in_kernel(tok, gain, w, wx, misc, x_out, z_out, conv_out, small_out, norm_out, buf, mt):
+def in_kernel(
+    n_seq, steps, tok, gain, w, wx, misc, cot_own, x_out, z_out, conv_out, norm_out, small_all, cot_all,
+    buf, mt, csem, *scratch,
+):
     rows, cp = x_out.shape
+    line = Line(n_seq)
+    sums = Sum(line, scratch[7:], small_all)
+    half = cot_own.shape[0] // 2
+    slots_of = Gather(
+        line, lambda q, p: cot_all.at[q, p], lambda p: cot_own.at[p], range(half), scratch[:7]
+    )
+    own = pltpu.make_async_copy(cot_own, cot_all.at[line.me], csem)
+
+    @pl.when(pl.program_id(0) == 0)
+    def _():
+        greet([(None, q) for q in all_peers(n_seq)])
+        own.start()
+        slots_of.stage(0)
+
+    late = []
+    for k in range(1, line.n):
+        at = k * steps // (line.n - 1) + 1
+        if at < steps:
+            pl.when(pl.program_id(0) == at)(lambda k=k: slots_of.stage(k))
+        else:
+            late.append(k)
 
     @pl.when(pl.program_id(0) == 0)
     def _():
@@ -81,55 +106,76 @@
     for k in range(3):
         conv = conv + buf[5 + k : 5 + k + rows, :] * mt[k : k + 1, :]
     conv_out[...] = conv
-    small_out[...] = mm((conv * sigmoid(conv)).astype(bf16), wx[...]).astype(bf16)
+    sums.put(pl.program_id(0), mm((conv * sigmoid(conv)).astype(bf16), wx[...]))
+
+    @pl.when(pl.program_id(0) == steps - 1)
+    def _():
+        sums.finish()
+        for k in late:
+            slots_of.stage(k)
+        slots_of.finish()
+        own.wait()
 
 
 def stage_step(k, n, steps):
     return steps - 1 - (n - 1 - k) * max(1, (steps - 2) // max(1, n - 1))
 
 
+def state_maps(small, st):
+    st[...] = small[...].astype(f32).T[B_AT : B_AT + 2 * NS, :]
+
+
+def maps_of(st, g):
+    lanes = st.shape[1]
+    return pltpu.roll(st[...], lax.rem(lanes - 8 * g, lanes), 1)
+
+
 def scan_kernel(
-    n_seq, steps, small, bct, wdt, misc, conv, z, wout, cot_own,
-    dtp_out, h_out, ssm_out, gated_out, part_out, cot_all,
-    delta_s, du_s, state, mt, a2, csem, *gsems,
+    n_seq, steps, small, wdt, misc, conv, z, wout, cot_own, cot_half,
+    dtp_out, delta_out, u_out, h_out, ssm_out, gated_out, mixed, cot_all,
+    du_s, state, mt, a2, st, *sems,
 ):
     rows, cp = conv.shape
     line = Line(n_seq)
     step = pl.program_id(0)
     slots_of = Gather(
-        line, lambda q, p: cot_all.at[q, p], lambda p: cot_own.at[p], cot_own.shape[0], gsems
+        line, lambda q, p: cot_all.at[q, p], lambda p: cot_own.at[p],
+        range(cot_own.shape[0] // 2, cot_own.shape[0]), sems[:7],
     )
-    own = pltpu.make_async_copy(cot_own, cot_all.at[line.me], csem)
+
+    def final(p, value):
+        high = value.shape[0]
+        mixed[p * high : (p + 1) * high, :] = value
+
+    stream = Made(line, sems[7:], final)
 
     @pl.when(step == 0)
     def _():
         greet(line.neighbours())
-        own.start()
         slots_of.stage(0)
-
-    for k in range(1, line.n):
-        pl.when(step == stage_step(k, line.n, steps))(lambda k=k: slots_of.stage(k))
-
-    @pl.when(pl.program_id(0) == 0)
-    def _():
         state[...] = jnp.zeros_like(state)
         mt[...] = turned(misc)
         a2[...] = -jnp.exp(mt[16:32, :]) * LOG2E
+
+    for k in range(1, line.n):
+        pl.when(step == k * steps // line.n)(lambda k=k: slots_of.stage(k))
 
     dtp = mm(small[...], wdt[...], NT) + mt[8:9, :]
     dtp_out[...] = dtp
     delta = softplus(dtp)
     cv = conv[...]
     u = cv * sigmoid(cv)
-    delta_s[...] = delta
+    u_out[...] = u
+    delta_out[...] = delta
     du_s[...] = delta * u
+    state_maps(small, st)
 
     def group(g, h):
         base = pl.multiple_of(g * 8, 8)
-        bc = bct[g]
+        bc = maps_of(st, g)
         stack = []
         for t in range(8):
-            d = jnp.broadcast_to(delta_s[pl.ds(base + t, 1), :], (NS, cp))
+            d = jnp.broadcast_to(delta_out[pl.ds(base + t, 1), :], (NS, cp))
             du = jnp.broadcast_to(du_s[pl.ds(base + t, 1), :], (NS, cp))
             h = jnp.exp2(d * a2[...]) * h + du * bc[:NS, t : t + 1]
             h_out[base + t] = h
@@ -138,84 +184,80 @@
         ssm_out[pl.ds(base, 8), :] = stack[0][1]
         return h
 
-    state[...] = lax.fori_loop(0, rows // 8, group, state[...])
+    state[...] = lax.fori_loop(0, rows // 8, group, state[...], unroll=2)
     zv = z[...]
     gated = (ssm_out[...] + mt[9:10, :] * u) * (zv * sigmoid(zv))
     low = gated.astype(bf16)
     gated_out[...] = low
-    part_out[...] = mm(low, wout[...]).astype(part_out.dtype)
+    stream.put(step, mm(low, wout[...]))
 
     @pl.when(step == steps - 1)
     def _():
+        for t in range(line.n):
+            stream.stage(t)
+        stream.finish()
         slots_of.finish()
-        own.wait()
+
+
+def cut_rows(src, out):
+    parts, blocks, high, _ = out.shape
+    for b in range(parts * blocks):
+        out[b // blocks, b % blocks] = src[b * high : (b + 1) * high, :].astype(out.dtype)
 
 
 def back_kernel(
-    n_seq, steps, gml, wout, gated, conv, z, ssm, dtp, hs, hlast, bct, small, wdt, misc,
-    term, rank_out, gbct_out, gu_out, gz_out, gwout_out, gwdt, gmisc, sums_out,
-    delta_s, du_s, gs_s, r1_s, r2_s, lam_s, mt, a2, gwout, ga, *scratch,
+    n_seq, steps, gml, wout, gated, u_ref, z, ssm, delta_ref, dtp, hs, hlast, small, wdt, misc, term,
+    norm, gu_out, gz_out, gwout_out, gwdt, gmisc, gwz_out, sums_out, small_all,
+    du_s, gs_s, r1_s, r2_s, lam_s, mt, a2, st, lams, gwout, ga, gwz, *scratch,
 ):
-    rows, cp = conv.shape
+    rows, cp = u_ref.shape
     step = pl.program_id(0)
     last = steps - 1
     line = Line(n_seq)
-    work = Collect(line, term, sums_out, scratch)
+    work = Collect(line, term, sums_out, scratch[:-8])
+    sums = Sum(line, scratch[-8:], small_all)
 
     @pl.when(step == 0)
     def _():
-        greet(line.neighbours(), work.peers)
+        greet([(None, q) for q in all_peers(n_seq)], work.peers)
         work.open()
-
-    for t in range(line.n):
-        pl.when(step == t + 1)(lambda t=t: work.stage(t))
-
-    @pl.when(step == 0)
-    def _():
         lam_s[...] = jnp.zeros_like(lam_s)
         gwout[...] = jnp.zeros_like(gwout)
+        gwz[...] = jnp.zeros_like(gwz)
         gwdt[...] = jnp.zeros_like(gwdt)
         ga[...] = jnp.zeros_like(ga)
         gmisc[...] = jnp.zeros_like(gmisc)
         mt[...] = turned(misc)
         a2[...] = -jnp.exp(mt[16:32, :]) * LOG2E
 
+    for t in range(line.n):
+        at = 2 + t * (steps - 4) // max(1, line.n - 1)
+        pl.when(step == at)(lambda t=t: work.stage(t))
+
     grad_mixed = gml[...]
     gg = mm(grad_mixed, wout[...], NT)
     gwout[...] += mm(gated[...], grad_mixed, TN)
     zv = z[...]
     sz = sigmoid(zv)
-    cv = conv[...]
-    u = cv * sigmoid(cv)
+    u = u_ref[...]
     skip = mt[9:10, :]
-    gz_out[...] = (gg * (ssm[...] + skip * u) * (sz * (1.0 + zv * (1.0 - sz)))).astype(bf16)
+    gz = (gg * (ssm[...] + skip * u) * (sz * (1.0 + zv * (1.0 - sz)))).astype(bf16)
+    gz_out[...] = gz
+    gwz[...] += mm(norm[...], gz, TN)
     gs = gg * (zv * sz)
-    delta = softplus(dtp[...])
     gs_s[...] = gs
-    delta_s[...] = delta
-    du_s[...] = delta * u
-    lane = lax.broadcasted_iota(jnp.int32, (NS, 128), 1)
+    du_s[...] = delta_ref[...] * u
+    state_maps(small, st)
     keep_first = jnp.where(step == last, 0.0, 1.0)
-    tiles = cp // 128
-
-    def lane_fold(v):
-        total = v[:, :128]
-        for i in range(1, tiles):
-            total = total + v[:, i * 128 : (i + 1) * 128]
-        return jnp.sum(total, axis=1, keepdims=True)
 
     def group(k, carry):
         lamd, acc = carry
         g = rows // 8 - 1 - k
         base = pl.multiple_of(g * 8, 8)
-        bc = bct[g]
+        bc = maps_of(st, g)
         stack1, stack2 = [], []
-        gb = jnp.zeros((NS, 128), f32)
-        gc = jnp.zeros((NS, 128), f32)
-        h = hs[base + 7]
         for t in range(7, -1, -1):
-            d = jnp.broadcast_to(delta_s[pl.ds(base + t, 1), :], (NS, cp))
-            du = jnp.broadcast_to(du_s[pl.ds(base + t, 1), :], (NS, cp))
+            d = jnp.broadcast_to(delta_ref[pl.ds(base + t, 1), :], (NS, cp))
             g_s = jnp.broadcast_to(gs_s[pl.ds(base + t, 1), :], (NS, cp))
             if t > 0:
                 before = hs[base + t - 1]
@@ -223,8 +265,7 @@
                 inside = hs[jnp.maximum(base - 1, 0)]
                 before = jnp.where(g == 0, hlast[0] * keep_first, inside)
             lam = lamd + g_s * bc[NS:, t : t + 1]
-            gc = jnp.where(lane == t, lane_fold(g_s * h), gc)
-            gb = jnp.where(lane == t, lane_fold(lam * du), gb)
+            lams[base + t] = lam.astype(bf16)
             lamd = jnp.exp2(d * a2[...]) * lam
             w = lamd * before
             acc = acc + w * d
@@ -232,25 +273,41 @@
             lb = lam * bc[:NS, t : t + 1]
             tree_push(stack1, wa[:8] + wa[8:], True)
             tree_push(stack2, lb[:8] + lb[8:], True)
-            h = before
         r1_s[pl.ds(base, 8), :] = stack1[0][1]
         r2_s[pl.ds(base, 8), :] = stack2[0][1]
-        gbct_out[g, :NS, :] = gb[:, :8]
-        gbct_out[g, NS:, :] = gc[:, :8]
         return lamd, acc
 
-    lamd, acc = lax.fori_loop(0, rows // 8, group, (lam_s[...], jnp.zeros((NS, cp), f32)))
+    lamd, acc = lax.fori_loop(0, rows // 8, group, (lam_s[...], jnp.zeros((NS, cp), f32)), unroll=2)
     lam_s[...] = lamd
     ga[...] += acc
     r2 = r2_s[...]
-    gu_out[...] = skip * gs + delta * r2
+    gu_out[...] = skip * gs + delta_ref[...] * r2
     gdelta = r1_s[...] * LN2 + u * r2
     gdtp = gdelta * sigmoid(dtp[...])
     gmisc[8:9, :] += jnp.sum(gdtp, axis=0, keepdims=True)
     gmisc[9:10, :] += jnp.sum(gs * u, axis=0, keepdims=True)
     low = gdtp.astype(bf16)
     gwdt[...] += mm(low, small[...], TN)
-    rank_out[...] = mm(low, wdt[...])
+
+    lane = lax.broadcasted_iota(jnp.int32, (8, 128), 1)
+    same = lax.broadcasted_iota(jnp.int32, (8, 128), 0) == lane // NS
+
+    def of_channels(values, states):
+        prod = jnp.where(same, mm(values.astype(bf16), states, NT), 0.0)
+        for by in (64, 32, 16):
+            prod = prod + pltpu.roll(prod, by, 1)
+        return prod
+
+    parts = []
+    for g in range(rows // 8):
+        own8 = slice(g * 8, g * 8 + 8)
+        gb = of_channels(du_s[own8, :], lams[own8].reshape(8 * NS, cp))
+        gc = of_channels(gs_s[own8, :], hs[own8].reshape(8 * NS, cp).astype(bf16))
+        parts.append(jnp.where(lane < C_AT, gb, gc))
+    grad_bc = jnp.concatenate(parts, axis=0)
+    wide = lax.broadcasted_iota(jnp.int32, (rows, 128), 1)
+    grad_bc = jnp.where(jnp.logical_and(wide >= B_AT, wide < C_AT + NS), grad_bc, 0.0)
+    sums.put(steps - 1 - step, mm(low, wdt[...]) + grad_bc)
 
     @pl.when(step == last)
     def _():
@@ -258,14 +315,25 @@
         parts, cpd, _ = gwout_out.shape
         for p in range(parts):
             gwout_out[p] = gwout[p * cpd : (p + 1) * cpd, :].astype(bf16)
+        cut_rows(gwz, gwz_out)
+        sums.finish()
         work.finish()
 
 
 def out_kernel(
-    gsmall, wx, misc, conv, x, gu, gz, norm, w, gwdt, gmisc, part_out, gw_out, pack_out,
-    buf, mt, gwx, gw, gm,
+    n_seq, steps, gsmall, wx, misc, conv, x, gu, gz, norm, w, gwdt, gmisc, gwout, gwz, tok, gres, gains, ggmoe,
+    gtok_out, gwout_out, pack_sum, gwin_out, gain_out,
+    buf, mt, gwx, gw, gm, gw_out, pack_out, *scratch,
 ):
     rows, cp = conv.shape
+    step = pl.program_id(0)
+    final = Finish(
+        n_seq, gwout, gwz, gw_out, pack_out, tok, gres, gains, ggmoe,
+        gtok_out, gwout_out, pack_sum, gwin_out, gain_out, *scratch,
+    )
+    pl.when(step == 0)(final.open)
+    pl.when(step == 2)(final.early_middle)
+    pl.when(step == steps - 2)(final.early_final)
 
     @pl.when(pl.program_id(0) == 0)
     def _():
@@ -293,25 +361,26 @@
         moved = buf[3 - k : 3 - k + rows, :]
         gx = gx + moved * mt[k : k + 1, :]
         gm[k : k + 1, :] += jnp.sum(moved * xv, axis=0, keepdims=True)
-    gp = jnp.concatenate([gx.astype(bf16), gz[...]], axis=1)
-    part_out[...] = mm(gp, w[...], NT).astype(part_out.dtype)
-    gw[...] += mm(norm[...], gp, TN)
+    gx = gx.astype(bf16)
+    gp = jnp.concatenate([gx, gz[...]], axis=1)
+    final.stream.put(steps - 1 - step, mm(gp, w[...], NT))
+    gw[...] += mm(norm[...], gx, TN)
 
     @pl.when(pl.program_id(0) == pl.num_programs(0) - 1)
     def _():
-        parts, blocks, high, _ = gw_out.shape
-        for b in range(parts * blocks):
-            gw_out[b // blocks, b % blocks] = gw[b * high : (b + 1) * high, :].astype(bf16)
+        cut_rows(gw, gw_out)
+        final.f_w.start()
         flat = gm[...].T
-        cpd = pack_out.shape[1]
+        parts, cpd, _ = pack_out.shape
         for p in range(parts):
             own = slice(p * cpd, (p + 1) * cpd)
             pack_out[p, :, 0:128] = gwx[own, :]
             pack_out[p, :, 128:256] = gwdt[own, :]
             pack_out[p, :, 256:384] = flat[own, :]
-
-
-def chunked(kernel, steps, backward, ins, outs, scratch, name, number=None):
+        final.close()
+
+
+def chunked(kernel, steps, backward, ins, outs, scratch, name, number=None, alias=None):
     def at(i):
         return steps - 1 - i if backward else i
 
@@ -336,6 +405,7 @@
         out_shape=[s for s, _ in outs],
         scratch_shapes=scratch,
         name=name,
+        input_output_aliases=alias or {},
         compiler_params=pltpu.CompilerParams(
             dimension_semantics=("arbitrary",), vmem_limit_bytes=60 * 1024 * 1024,
             collective_id=number, has_side_effects=number is not None,
@@ -406,7 +476,10 @@
 
 def gather_sems(n, pieces):
     dma = pltpu.SemaphoreType.DMA
-    return [dma((n, pieces)), dma((pieces,)), dma((n, pieces)), dma((n, pieces)), dma((n, pieces))]
+    return [
+        dma((n, pieces)), dma((pieces,)), dma((n, pieces)), dma((n, pieces)), dma((n, pieces)),
+        dma((2, pieces)), dma((pieces,)),
+    ]
 
 
 class Gather:
@@ -417,21 +490,31 @@
         return remote(src, self.at(self.line.at(q, self.line.i), p), send, recv, seq=place)
 
     def up(self, src, q, p):
-        zs, _, zr, _, _ = self.sems
+        zs, _, zr = self.sems[:3]
         return self.copy(src, q, p, zs.at[q, p], zr.at[q, p], self.line.at(self.line.o + 1, self.line.i))
 
     def down(self, src, q, p, own):
-        zs, zd, zr, _, _ = self.sems
+        zs, zd, zr = self.sems[:3]
         send = zd.at[p] if own else zs.at[q, p]
         return self.copy(src, q, p, send, zr.at[q, p], self.line.at(self.line.o - 1, self.line.i))
 
     def over(self, src, q, p):
-        _, _, _, ys, yr = self.sems
+        ys, yr = self.sems[3:5]
         return self.copy(src, q, p, ys.at[q, p], yr.at[q, p], self.line.at(self.line.o, 1 - self.line.i))
+
+    def late(self, p):
+        pieces = list(self.pieces)
+        return self.line.n > 2 and pieces.index(p) >= (len(pieces) + 1) // 2
+
+    def extra(self, end, p):
+        line = self.line
+        far, to = (line.n - 1, 0) if end == 0 else (0, line.n - 1)
+        here = self.at(line.at(far, 1 - line.i), p)
+        return remote(here, here, self.sems[5].at[end, p], self.sems[6].at[p], seq=line.at(to, line.i))
 
     def each(self, k, act, arrive=None):
         line, o, n = self.line, self.line.o, self.line.n
-        for p in range(self.pieces):
+        for p in self.pieces:
             if k == 0:
                 src = self.own(p)
                 if arrive is not None:
@@ -446,19 +529,24 @@
                 src = self.at(line.at(q, line.i), p)
                 if arrive is not None:
                     arrive(self.up(src, q, p))
-                pl.when(o < n - 1)(lambda: act(self.up(src, q, p)))
-                act(self.over(src, q, p))
+                if k < n - 1:
+                    pl.when(o < n - 1)(lambda: act(self.up(src, q, p)))
+                if k < n - 1 or not self.late(p):
+                    act(self.over(src, q, p))
 
             def above(p=p):
                 q = o + k
                 src = self.at(line.at(q, line.i), p)
                 if arrive is not None:
                     arrive(self.up(src, q, p))
-                pl.when(o > 0)(lambda: act(self.down(src, q, p, False)))
-                act(self.over(src, q, p))
-
-            pl.when(o >= k)(below)
-            pl.when(o + k <= n - 1)(above)
+                if k < n - 1:
+                    pl.when(o > 0)(lambda: act(self.down(src, q, p, False)))
+                if k < n - 1 or not self.late(p):
+                    act(self.over(src, q, p))
+
+            if arrive is not None or k < n - 1 or not self.late(p):
+                pl.when(o >= k)(below)
+                pl.when(o + k <= n - 1)(above)
 
     def stage(self, k, ready=None):
         arrive = ready if k == 0 else (lambda copy: copy.wait_recv())
@@ -466,11 +554,33 @@
 
     def finish(self):
         line = self.line
-        for q in range(line.n):
-            for p in range(self.pieces):
-                here = self.at(line.at(q, 1 - line.i), p)
-                self.over(here, q, p).wait_recv()
-        for k in range(line.n):
+        o, n = line.o, line.n
+        ends = ((0, n - 1, 1, 0), (1, 0, n - 2, n - 1))
+        held = [p for p in self.pieces if self.late(p)]
+
+        def over_in(q, p):
+            self.over(self.at(line.at(q, 1 - line.i), p), q, p).wait_recv()
+
+        for end, far, beside, _ in ends:
+            for p in held:
+                @pl.when(o == beside)
+                def _(end=end, far=far, p=p):
+                    over_in(far, p)
+                    self.extra(end, p).start()
+
+        for q in range(n):
+            for p in self.pieces:
+                if p in held and q in (0, n - 1):
+                    end, _, beside, at = ends[0 if q == n - 1 else 1]
+                    done = jnp.logical_or(o == beside, o == at)
+                    pl.when(jnp.logical_not(done))(lambda q=q, p=p: over_in(q, p))
+                    pl.when(o == at)(lambda end=end, p=p: self.extra(end, p).wait_recv())
+                else:
+                    over_in(q, p)
+        for end, _, beside, _ in ends:
+            for p in held:
+                pl.when(o == beside)(lambda end=end, p=p: self.extra(end, p).wait_send())
+        for k in range(n):
             self.each(k, lambda copy: copy.wait_send())
 
     def run(self, ready=None):
@@ -484,7 +594,7 @@
     greet(line.neighbours())
     keep = pltpu.make_async_copy(x, out.at[line.me], lsem)
     keep.start()
-    Gather(line, lambda q, p: out.at[q, p], lambda p: x.at[p], x.shape[0], sems).run()
+    Gather(line, lambda q, p: out.at[q, p], lambda p: x.at[p], range(x.shape[0]), sems).run()
     keep.wait()
 
 
@@ -523,7 +633,7 @@
             remote(source, source, dps.at[r - 1], dpr.at[r - 1], dp=peers[r - 1]).wait_recv()
 
     at = rolled(out, mine, n_dp)
-    Gather(line, at, lambda r: at(line.me, r), n_dp, sems).run(ready)
+    Gather(line, at, lambda r: at(line.me, r), range(n_dp), sems).run(ready)
     for copy in copies:
         copy.wait_send()
 
@@ -722,51 +832,74 @@
     )(x)
 
 
-def sum_kernel(n_seq, x, out, inbox, total, lsem, s1, r1, s2, r2):
-    me = lax.axis_index("seq")
-    peers = [lax.rem(me + r, n_seq) for r in range(1, n_seq)]
-    greet([(None, q) for q in peers])
-    copies = []
-    for r, q in enumerate(peers):
-        copy = remote(x.at[q], inbox.at[r], s1.at[r], r1.at[r], seq=q)
-        copy.start()
-        copies.append(copy)
-    value = x[me].astype(f32)
-    for r, q in enumerate(peers):
-        remote(inbox.at[r], inbox.at[r], s1.at[r], r1.at[r], seq=q).wait_recv()
-        value = value + inbox[r].astype(f32)
-    total[...] = value.astype(total.dtype)
-    for r, q in enumerate(peers):
-        copy = remote(total, out.at[me], s2.at[r], r2.at[r], seq=q)
-        copy.start()
-        copies.append(copy)
-    keep = pltpu.make_async_copy(total, out.at[me], lsem)
-    keep.start()
-    for r, q in enumerate(peers):
-        here = out.at[lax.rem(me + n_seq - 1 - r, n_seq)]
-        remote(here, here, s2.at[r], r2.at[r], seq=q).wait_recv()
-    keep.wait()
-    for copy in copies:
-        copy.wait_send()
-
-
-def seq_sum(x, n_seq, number):
-    rows, width = x.shape[0] // n_seq, x.shape[1]
+def made_scratch(n, pieces, rows, width):
+    return [pltpu.VMEM((2 * n, pieces, rows, width), bf16)] + scatter_scratch(n, pieces, rows, width)
+
+
+class Made(Scatter):
+    def __init__(self, line, scratch, final):
+        self.made = scratch[0]
+        pieces = self.made.shape[1]
+        super().__init__(line, lambda q, p: self.made.at[q, p], range(pieces), scratch[1:], final)
+
+    def put(self, b, value):
+        line, rows = self.line, self.made.shape[2]
+        for p in self.pieces:
+            self.made[b, p] = value[p * rows : (p + 1) * rows, :].astype(bf16)
+
+        @pl.when(b % 2 != line.i)
+        def _():
+            for p in self.pieces:
+                remote(self.made.at[b, p], self.ybuf.at[b // 2, p], self.ys.at[b // 2, p],
+                       self.yr.at[b // 2, p], seq=line.at(line.o, 1 - line.i)).start()
+
+
+def sum_scratch(n_seq, rows, width):
     dma = pltpu.SemaphoreType.DMA
-    vmem = pl.BlockSpec(memory_space=pltpu.VMEM)
-    out = pl.pallas_call(
-        partial(sum_kernel, n_seq),
-        in_specs=[vmem],
-        out_specs=vmem,
-        out_shape=jax.ShapeDtypeStruct((n_seq, rows, width), x.dtype),
-        scratch_shapes=[pltpu.VMEM((n_seq - 1, rows, width), x.dtype), pltpu.VMEM((rows, width), x.dtype),
-                        dma] + [dma((n_seq - 1,)) for _ in range(4)],
-        compiler_params=pltpu.CompilerParams(
-            collective_id=number, has_side_effects=True, vmem_limit_bytes=60 * 1024 * 1024
-        ),
-        name="seq_sum",
-    )(x.reshape(n_seq, rows, width))
-    return out.reshape(n_seq * rows, width)
+    mem = pltpu.VMEM
+    return [
+        mem((n_seq, rows, width), bf16), mem((n_seq, rows, width), bf16), mem((rows, width), bf16),
+        dma, dma((n_seq,)), dma((n_seq,)), dma((n_seq,)), dma((n_seq,)),
+    ]
+
+
+class Sum:
+    def __init__(self, line, scratch, out):
+        self.line, self.out = line, out
+        self.made, self.inbox, self.total, self.own, self.s1, self.r1, self.s2, self.r2 = scratch
+
+    def send(self, b):
+        me = self.line.me
+        return remote(self.made.at[b], self.inbox.at[me], self.s1.at[b], self.r1.at[me], seq=b)
+
+    def spread(self, q):
+        me = self.line.me
+        return remote(self.total, self.out.at[me], self.s2.at[q], self.r2.at[me], seq=q)
+
+    def put(self, b, value):
+        self.made[b] = value.astype(bf16)
+        pl.when(b != self.line.me)(lambda: self.send(b).start())
+
+    def finish(self):
+        me = self.line.me
+        peers = all_peers(self.line.n_seq)
+        value = self.made[me].astype(f32)
+        for q in peers:
+            here = self.inbox.at[q]
+            remote(here, here, self.s1.at[q], self.r1.at[q], seq=q).wait_recv()
+            value = value + self.inbox[q].astype(f32)
+        self.total[...] = value.astype(bf16)
+        for q in peers:
+            self.spread(q).start()
+        own = pltpu.make_async_copy(self.total, self.out.at[me], self.own)
+        own.start()
+        for q in peers:
+            here = self.out.at[q]
+            remote(here, here, self.s2.at[q], self.r2.at[q], seq=q).wait_recv()
+        own.wait()
+        for q in peers:
+            self.send(q).wait_send()
+            self.spread(q).wait_send()
 
 
 def all_peers(n_seq):
@@ -815,7 +948,7 @@
     xg, w_all, wout_all, side_all, gain_all, cot_own, pick_out,
     wst, gbox, zero_w, zero_s, cst, lsem, tsem, csem, cds, cdr, *sems,
 ):
-    gsems, (a2s, a2r, gs2, gr2), dsems = sems[:5], sems[5:9], sems[9:]
+    gsems, (a2s, a2r, gs2, gr2), dsems = sems[:7], sems[7:11], sems[11:]
     line = Line(n_seq)
     me = line.me
     peers = all_peers(n_seq)
@@ -823,7 +956,7 @@
     greet([(None, q) for q in peers], [core, far, rest])
     keep = pltpu.make_async_copy(tok, xg.at[me], tsem)
     keep.start()
-    tokens_of = Gather(line, lambda q, p: xg.at[q, p], lambda p: tok.at[p], tok.shape[0], gsems)
+    tokens_of = Gather(line, lambda q, p: xg.at[q, p], lambda p: tok.at[p], range(tok.shape[0]), gsems)
     tokens_of.stage(0)
     locals_ = []
 
@@ -968,157 +1101,171 @@
     def __init__(self, arr, box, send, sems):
         self.arr, self.box, self.send, (self.s, self.r) = arr, box, send, sems
         self.mine, self.core, self.far, self.rest = dp_peers()
-        self.sent = []
-
-    def push(self, src, k, peer):
-        copy = remote(src, self.box.at[k], self.s.at[k], self.r.at[k], dp=peer)
-        copy.start()
-        self.sent.append(copy)
-
-    def wait(self, k):
-        remote(self.box.at[k], self.box.at[k], self.s.at[k], self.r.at[k], dp=self.core).wait_recv()
+
+    def copy(self, k):
+        src = [lambda: self.arr.at[self.core], lambda: self.arr.at[self.rest], lambda: self.send][k]()
+        peer = self.far if k == 2 else self.core
+        return remote(src, self.box.at[k], self.s.at[k], self.r.at[k], dp=peer)
 
     def start(self):
-        self.push(self.arr.at[self.rest], 1, self.core)
-        self.push(self.arr.at[self.core], 0, self.core)
+        self.copy(1).start()
+        self.copy(0).start()
 
     def middle(self):
-        self.wait(1)
+        self.copy(1).wait_recv()
         value = self.arr[self.far].astype(f32) + self.box[1].astype(f32)
         self.send[...] = value.astype(self.send.dtype)
-        self.push(self.send, 2, self.far)
+        self.copy(2).start()
 
     def final(self):
-        self.wait(0)
-        self.wait(2)
+        self.copy(0).wait_recv()
+        self.copy(2).wait_recv()
         value = self.arr[self.mine].astype(f32) + self.box[0].astype(f32)
         return value + self.box[2].astype(f32)
 
     def done(self):
-        for copy in self.sent:
+        for k in range(3):
+            self.copy(k).wait_send()
+
+
+class Finish:
+    def __init__(
+        self, n_seq, gwout, gwz, gw, pack, tok, gres, gains, ggmoe,
+        gtok_out, gwout_out, pack_out, gwin_out, gain_out,
+        gn, wsum, wbox, gst, gb1, gsum, gb2, o_box, o_send, w_box, w_send, z_box, z_send, p_box, p_send,
+        lsem, *sems,
+    ):
+        self.line = Line(n_seq)
+        self.tok, self.gres, self.gains, self.ggmoe = tok, gres, gains, ggmoe
+        self.gtok_out, self.gwout_out, self.pack_out = gtok_out, gwout_out, pack_out
+        self.gwin_out, self.gain_out = gwin_out, gain_out
+        self.gn, self.wsum, self.wbox, self.gst, self.gb1 = gn, wsum, wbox, gst, gb1
+        self.gsum, self.gb2, self.lsem = gsum, gb2, lsem
+        self.sems, dsems = sems[8:14], sems[14:]
+
+        def final(p, value):
+            high = value.shape[0]
+            gn[p * high : (p + 1) * high, :] = value
+
+        self.stream = Made(self.line, sems[:8], final)
+        self.f_w = Fold(gw, w_box, w_send, dsems[0:2])
+        self.f_z = Fold(gwz, z_box, z_send, dsems[6:8])
+        self.f_o = Fold(gwout, o_box, o_send, dsems[2:4])
+        self.f_p = Fold(pack, p_box, p_send, dsems[4:6])
+
+    def open(self):
+        mine, core, far, rest = dp_peers()
+        greet([(None, q) for q in all_peers(self.line.n_seq)], [core, far, rest])
+        self.f_z.start()
+        self.f_o.start()
+
+    def early_middle(self):
+        self.f_z.middle()
+        self.f_o.middle()
+
+    def block(self, half, q, r):
+        a2s, a2r = self.sems[:2]
+        return remote(self.wsum.at[half, q], self.wbox.at[half, self.line.me], a2s.at[half, r],
+                      a2r.at[half, r], seq=q)
+
+    def keep(self, half):
+        me = self.line.me
+        return pltpu.make_async_copy(self.wsum.at[half, me], self.wbox.at[half, me], self.lsem.at[half])
+
+    def exchange(self, half, value):
+        self.wsum[half] = value.astype(bf16)
+        for r, q in enumerate(all_peers(self.line.n_seq)):
+            self.block(half, q, r).start()
+        self.keep(half).start()
+
+    def early_final(self):
+        self.exchange(1, self.f_z.final())
+        self.gwout_out[...] = self.f_o.final()
+
+    def close(self):
+        line, f_w, f_o, f_p, stream = self.line, self.f_w, self.f_o, self.f_p, self.stream
+        a2s, a2r, g1s, g1r, g2s, g2r = self.sems
+        n_seq, me = line.n_seq, line.me
+        peers = all_peers(n_seq)
+        mine, core, far, rest = dp_peers()
+        dps = [core, far, rest]
+        f_p.start()
+        stream.stage(0)
+        f_w.middle()
+        f_p.middle()
+        for t in range(1, line.n - 1):
+            stream.stage(t)
+        self.exchange(0, f_w.final())
+        copies = []
+        self.pack_out[...] = f_p.final()
+        if line.n > 2:
+            stream.stage(line.n - 1)
+
+        v = self.tok[...].astype(f32)
+        r_ = lax.rsqrt(jnp.mean(v * v, axis=-1, keepdims=True) + eps)
+        gy = self.gn[...]
+        gst, gb1, gb2 = self.gst, self.gb1, self.gb2
+        gst[0:1, :] = jnp.sum(gy * (v * r_), axis=0, keepdims=True)
+        gst[1:2, :] = self.ggmoe[...]
+        for k, peer in enumerate(dps):
+            copy = remote(gst, gb1.at[k], g1s.at[k], g1r.at[k], dp=peer)
+            copy.start()
+            copies.append(copy)
+        gyg = gy * self.gains[0:1, :]
+        inner = jnp.mean(gyg * v, axis=-1, keepdims=True)
+        self.gtok_out[...] = gyg * r_ - v * (r_ * r_ * r_ * inner) + self.gres[...]
+        total = gst[...]
+        for k in range(3):
+            remote(gb1.at[k], gb1.at[k], g1s.at[k], g1r.at[k], dp=core).wait_recv()
+            total = total + gb1[k]
+        self.gsum[...] = total
+        for r, q in enumerate(peers):
+            copy = remote(self.gsum, gb2.at[r], g2s.at[r], g2r.at[r], seq=q)
+            copy.start()
+            copies.append(copy)
+
+        for half in range(2):
+            self.keep(half).wait()
+            for r, q in enumerate(peers):
+                here = self.wbox.at[half, lax.rem(me + n_seq - 1 - r, n_seq)]
+                remote(here, here, a2s.at[half, r], a2r.at[half, r], seq=q).wait_recv()
+        wide = self.gwin_out.shape[1]
+        cpd = wide // (2 * 4 * n_seq)
+        for q in range(n_seq):
+            for half in range(2):
+                block = self.wbox[half, q].astype(f32)
+                for p in range(4):
+                    at = (half * 4 * n_seq + p * n_seq + q) * cpd
+                    self.gwin_out[:, at : at + cpd] = block[:, p * cpd : (p + 1) * cpd]
+        for r, q in enumerate(peers):
+            remote(gb2.at[r], gb2.at[r], g2s.at[r], g2r.at[r], seq=q).wait_recv()
+            total = total + gb2[r]
+        self.gain_out[...] = total
+        stream.finish()
+        for fold in (f_w, self.f_z, f_o, f_p):
+            fold.done()
+        for half in range(2):
+            for r, q in enumerate(peers):
+                self.block(half, q, r).wait_send()
+        for copy in copies:
             copy.wait_send()
 
 
-def finish_kernel(
-    n_seq, term, gwout, gw, pack, tok, gres, gains, ggmoe,
-    gtok_out, gwout_out, pack_out, gwin_out, gain_out,
-    gn, wsum, wbox, gst, gb1, gsum, gb2, o_box, o_send, w_box, w_send, p_box, p_send, lsem, *sems,
-):
-    scratch, (a2s, a2r, g1s, g1r, g2s, g2r), dsems = sems[:7], sems[7:13], sems[13:]
-    line = Line(n_seq)
-    me = line.me
-    peers = all_peers(n_seq)
-    mine, core, far, rest = dp_peers()
-    dps = [core, far, rest]
-    greet([(None, q) for q in peers], dps)
-    f_w = Fold(gw, w_box, w_send, dsems[0:2])
-    f_o = Fold(gwout, o_box, o_send, dsems[2:4])
-    f_p = Fold(pack, p_box, p_send, dsems[4:6])
-    for fold in (f_w, f_o, f_p):
-        fold.start()
-
-    def final(p, value):
-        gn[p] = value
-
-    sums = Scatter(line, lambda q, p: term.at[q, p], range(term.shape[1]), scratch, final)
-    sums.open()
-    for fold in (f_w, f_o, f_p):
-        fold.middle()
-    sums.stage(0)
-    wsum[...] = f_w.final().astype(bf16)
-    copies = []
-    for r, q in enumerate(peers):
-        copy = remote(wsum.at[q], wbox.at[me], a2s.at[r], a2r.at[r], seq=q)
-        copy.start()
-        copies.append(copy)
-    keep = pltpu.make_async_copy(wsum.at[me], wbox.at[me], lsem)
-    keep.start()
-    if line.n > 1:
-        sums.stage(1)
-    gwout_out[...] = f_o.final()
-    pack_out[...] = f_p.final()
-    for t in range(2, line.n):
-        sums.stage(t)
-    sums.finish()
-
-    v = tok[...].astype(f32)
-    r_ = lax.rsqrt(jnp.mean(v * v, axis=-1, keepdims=True) + eps)
-    gy = jnp.concatenate([gn[p] for p in range(gn.shape[0])], axis=0)
-    gst[0:1, :] = jnp.sum(gy * (v * r_), axis=0, keepdims=True)
-    gst[1:2, :] = ggmoe[...]
-    gsends = []
-    for k, peer in enumerate(dps):
-        copy = remote(gst, gb1.at[k], g1s.at[k], g1r.at[k], dp=peer)
-        copy.start()
-        gsends.append(copy)
-    gyg = gy * gains[0:1, :]
-    inner = jnp.mean(gyg * v, axis=-1, keepdims=True)
-    gtok_out[...] = gyg * r_ - v * (r_ * r_ * r_ * inner) + gres[...]
-    total = gst[...]
-    for k in range(3):
-        remote(gb1.at[k], gb1.at[k], g1s.at[k], g1r.at[k], dp=core).wait_recv()
-        total = total + gb1[k]
-    gsum[...] = total
-    for r, q in enumerate(peers):
-        copy = remote(gsum, gb2.at[r], g2s.at[r], g2r.at[r], seq=q)
-        copy.start()
-        gsends.append(copy)
-
-    keep.wait()
-    for r, q in enumerate(peers):
-        here = wbox.at[lax.rem(me + n_seq - 1 - r, n_seq)]
-        remote(here, here, a2s.at[r], a2r.at[r], seq=q).wait_recv()
-    wide = gwin_out.shape[1]
-    cpd = wide // (2 * 4 * n_seq)
-    half = wbox.shape[2] // 2
-    for q in range(n_seq):
-        block = wbox[q].astype(f32)
-        for side_of in range(2):
-            for p in range(4):
-                at = (side_of * 4 * n_seq + p * n_seq + q) * cpd
-                src = side_of * half + p * cpd
-                gwin_out[:, at : at + cpd] = block[:, src : src + cpd]
-    for r, q in enumerate(peers):
-        remote(gb2.at[r], gb2.at[r], g2s.at[r], g2r.at[r], seq=q).wait_recv()
-        total = total + gb2[r]
-    gain_out[...] = total
-    for fold in (f_w, f_o, f_p):
-        fold.done()
-    for copy in copies + gsends:
-        copy.wait_send()
-
-
-def finish_call(gpart, gwout, gw, pack, tokens, gres, gains, ggmoe, n_seq, number):
-    here, d_model = tokens.shape
-    _, _, high, wide = gw.shape
-    _, cpd, n_side = pack.shape
+def finish_scratch(n_seq, here, d_model, high, wide, cpd, n_side):
     dma = pltpu.SemaphoreType.DMA
-    vmem = pl.BlockSpec(memory_space=pltpu.VMEM)
-    sds = jax.ShapeDtypeStruct
     mem = pltpu.VMEM
-    return pl.pallas_call(
-        partial(finish_kernel, n_seq),
-        in_specs=[vmem] * 8,
-        out_specs=[vmem] * 5,
-        out_shape=[
-            sds((here, d_model), f32), sds((cpd, d_model), f32), sds((cpd, n_side), f32),
-            sds((high, 2 * 4 * n_seq * cpd), f32), sds((2, d_model), f32),
-        ],
-        scratch_shapes=[
-            mem((2, here // 2, d_model), f32), mem((n_seq, high, wide), bf16), mem((n_seq, high, wide), bf16),
-            mem((2, d_model), f32), mem((3, 2, d_model), f32), mem((2, d_model), f32),
-            mem((n_seq - 1, 2, d_model), f32),
-            mem((3, cpd, d_model), bf16), mem((cpd, d_model), bf16),
-            mem((3, n_seq, high, wide), bf16), mem((n_seq, high, wide), bf16),
-            mem((3, cpd, n_side), f32), mem((cpd, n_side), f32), dma,
-        ] + scatter_scratch(n_seq // 2, 2, here // 2, d_model)
-        + [dma((n_seq - 1,)), dma((n_seq - 1,)), dma((3,)), dma((3,)), dma((n_seq - 1,)), dma((n_seq - 1,))]
-        + [dma((3,)) for _ in range(6)],
-        compiler_params=pltpu.CompilerParams(
-            collective_id=number, has_side_effects=True, vmem_limit_bytes=62 * 1024 * 1024
-        ),
-        name="finish",
-    )(gpart.reshape(n_seq, 2, here // 2, d_model), gwout, gw, pack, tokens, gres, gains, ggmoe)
+    many = dma((n_seq - 1,))
+    return [
+        mem((here, d_model), f32), mem((2, n_seq, high, wide), bf16), mem((2, n_seq, high, wide), bf16),
+        mem((2, d_model), f32), mem((3, 2, d_model), f32), mem((2, d_model), f32),
+        mem((n_seq - 1, 2, d_model), f32),
+        mem((3, cpd, d_model), bf16), mem((cpd, d_model), bf16),
+        mem((3, n_seq, high, wide), bf16), mem((n_seq, high, wide), bf16),
+        mem((3, n_seq, high, wide), bf16), mem((n_seq, high, wide), bf16),
+        mem((3, cpd, n_side), f32), mem((cpd, n_side), f32), dma((2,)),
+    ] + made_scratch(n_seq // 2, 2, here // 2, d_model) + [
+        dma((2, n_seq - 1)), dma((2, n_seq - 1)), dma((3,)), dma((3,)), many, many
+    ] + [dma((3,)) for _ in range(8)]
 
 
 def on_device(
@@ -1139,7 +1286,7 @@
 
     gap = jnp.zeros((cpd, 128), bf16)
     side = jnp.concatenate(
-        [w_x, gap[:, n_small:], w_dt, gap[:, rank:], conv_w, gap[:, 4:8], dt_bias[:, None],
+        [w_x[:, :rank], gap[:, rank:B_AT], w_x[:, rank:], gap[:, C_AT + NS :], w_dt, gap[:, rank:], conv_w, gap[:, 4:8], dt_bias[:, None],
          d_skip[:, None], gap[:, 10:16], a_log, gap[:, 32:]], axis=1,
     )
     gains_in = jnp.pad(jnp.stack([gain_mix, gain_moe]).astype(f32), ((0, 6), (0, 128 - gain_mix.shape[0])))
@@ -1162,26 +1309,28 @@
     vec = pltpu.VMEM((tb, cp), f32)
     turned_misc = pltpu.VMEM((128, cp), f32)
     by_state = pltpu.VMEM((NS, cp), f32)
-    x, z, conv, small, normed = chunked(
-        in_kernel, steps, False,
-        [(toks, tb), (gains, 0), (w_mine, 0), (side_m, wx_spec), (side_m, misc_spec)],
-        [(wide, tb), (wide, tb), (wide, tb), (sds((tall, sp), bf16), tb), (sds((tall, d_model), bf16), tb)],
-        [pltpu.VMEM((tb + 8, cp), f32), turned_misc], "mix_in",
+    x, z, conv, normed, small, grad_slots = chunked(
+        partial(in_kernel, n_seq, steps), steps, False,
+        [(toks, tb), (gains, 0), (w_mine, 0), (side_m, wx_spec), (side_m, misc_spec),
+         (cot_own, None)],
+        [(wide, tb), (wide, tb), (wide, tb), (sds((tall, d_model), bf16), tb),
+         (sds((n_seq, tb, sp), bf16), None), (sds((n_seq, n_dp, slots, d_model), bf16), None)],
+        [pltpu.VMEM((tb + 8, cp), f32), turned_misc, pltpu.SemaphoreType.DMA]
+        + gather_sems(n_seq // 2, n_dp) + sum_scratch(n_seq, tb, sp), "mix_in", 1,
     )
-    small = seq_sum(small, n_seq, 1)
-    bct = small[:, rank:n_small].astype(f32).reshape(tall // 8, 8, 2 * NS).transpose(0, 2, 1)
-    dtp, hs, ssm, gated, part, grad_slots = chunked(
+    small = small.reshape(tall, sp)
+    dtp, delta, u_all, hs, ssm, gated, mixer_out, grad_slots = chunked(
         partial(scan_kernel, n_seq, steps), steps, False,
-        [(small, tb), (bct, tb // 8), (side_m, wdt_spec), (side_m, misc_spec), (conv, tb), (z, tb),
-         (wout_m, wout_spec), (cot_own, None)],
-        [(wide, tb), (sds((tall, NS, cp), f32), tb), (wide, tb), (sds((tall, cp), bf16), tb),
-         (sds((tall, d_model), bf16), tb), (sds((n_seq, n_dp, slots, d_model), bf16), None)],
-        [vec, vec, by_state, turned_misc, by_state, pltpu.SemaphoreType.DMA]
-        + gather_sems(n_seq // 2, n_dp),
-        "scan_forward", 3,
+        [(small, tb), (side_m, wdt_spec), (side_m, misc_spec), (conv, tb), (z, tb),
+         (wout_m, wout_spec), (cot_own, None), (grad_slots, None)],
+        [(wide, tb), (wide, tb), (wide, tb), (sds((tall, NS, cp), f32), tb), (wide, tb),
+         (sds((tall, cp), bf16), tb), (sds((here, d_model), f32), 0),
+         (sds((n_seq, n_dp, slots, d_model), bf16), None)],
+        [vec, by_state, turned_misc, by_state, pltpu.VMEM((2 * NS, tb), f32)]
+        + gather_sems(n_seq // 2, n_dp) + made_scratch(n_seq // 2, 2, here // 2, d_model),
+        "scan_forward", 3, {7: 7},
     )
     grad_slots = grad_slots.reshape(n_seq * n_dp * slots, d_model)
-    mixer_out = seq_scatter(part, n_seq, 2, 2)
     resid = row_values + mixer_out
 
     normed2, norm2_pullback = jax.vjp(rms_norm, resid, gains[1])
@@ -1209,40 +1358,42 @@
     grad_resid, grad_gmoe = norm2_pullback(grad_moe_in)
     grad_resid = grad_resid + cotangent.astype(f32)
     gml = seq_gather(grad_resid.astype(bf16), n_seq, 2, 7)
-    grad_rank, gbct, gu, gz, gwout, gwdt, gmisc, expert_out = chunked(
+    gu, gz, gwout, gwdt, gmisc, gwz, expert_out, gsmall = chunked(
         partial(back_kernel, n_seq, steps), steps, True,
-        [(gml, tb), (wout_m, wout_spec), (gated, tb), (conv, tb), (z, tb), (ssm, tb), (dtp, tb), (hs, tb),
-         (hs, -tb), (bct, tb // 8), (small, tb), (side_m, wdt_spec), (side_m, misc_spec),
-         (expert_terms, 0)],
-        [(sds((tall, sp), f32), tb), (sds((tall // 8, 2 * NS, 8), f32), tb // 8), (wide, tb),
-         (sds((tall, cp), bf16), tb), (sds((n_dp, cpd, d_model), bf16), 0), (sds((cp, sp), f32), 0),
-         (sds((32, cp), f32), 0), (sds((n_dp, slots, d_model), bf16), None)],
-        [vec] * 5 + [by_state, turned_misc, by_state, pltpu.VMEM((cp, d_model), f32), by_state]
-        + collect_scratch(n_seq, n_dp, slots, d_model),
+        [(gml, tb), (wout_m, wout_spec), (gated, tb), (u_all, tb), (z, tb), (ssm, tb), (delta, tb), (dtp, tb),
+         (hs, tb), (hs, -tb), (small, tb), (side_m, wdt_spec), (side_m, misc_spec), (expert_terms, 0),
+         (normed, tb)],
+        [(wide, tb), (sds((tall, cp), bf16), tb), (sds((n_dp, cpd, d_model), bf16), 0),
+         (sds((cp, sp), f32), 0), (sds((32, cp), f32), 0), (sds((n_dp, n_seq, rows_in, cp), bf16), 0),
+         (sds((n_dp, slots, d_model), bf16), None),
+         (sds((n_seq, tb, sp), bf16), None)],
+        [vec] * 4 + [by_state, turned_misc, by_state, pltpu.VMEM((2 * NS, tb), f32),
+                     pltpu.VMEM((tb, NS, cp), bf16), pltpu.VMEM((cp, d_model), f32), by_state,
+                     pltpu.VMEM((d_model, cp), f32)]
+        + collect_scratch(n_seq, n_dp, slots, d_model) + sum_scratch(n_seq, tb, sp),
         "scan_backward", 6,
     )
+    gsmall = gsmall.reshape(tall, sp)
     result = (resid + returned(expert_out)).astype(bf16)
-    grad_bc = gbct.transpose(0, 2, 1).reshape(tall, 2 * NS)
-    gsmall = jnp.concatenate([grad_rank[:, :rank], grad_bc], axis=1)
-    gsmall = seq_sum(jnp.pad(gsmall, ((0, 0), (0, sp - n_small))).astype(bf16), n_seq, 8)
-    gpart, gw, gpack = chunked(
-        out_kernel, steps, True,
+    grad_tokens, grad_wout, gpack, grad_win, ggains = chunked(
+        partial(out_kernel, n_seq, steps), steps, True,
         [(gsmall, tb), (side_m, wx_spec), (side_m, misc_spec), (conv, tb), (x, tb), (gu, tb), (gz, tb),
-         (normed, tb), (w_mine, 0), (gwdt, 0), (gmisc, 0)],
-        [(sds((tall, d_model), bf16), tb), (sds((n_dp, n_seq, rows_in, 2 * cp), bf16), 0),
-         (sds((n_dp, cpd, 384), f32), 0)],
+         (normed, tb), (w_mine, 0), (gwdt, 0), (gmisc, 0), (gwout, 0), (gwz, 0), (tokens, 0), (grad_resid, 0),
+         (gains, 0), (grad_gmoe[None], 0)],
+        [(sds((here, d_model), f32), 0), (sds((cpd, d_model), f32), 0), (sds((cpd, 384), f32), 0),
+         (sds((rows_in, 2 * 4 * n_seq * cpd), f32), 0), (sds((2, d_model), f32), 0)],
         [pltpu.VMEM((tb + 8, cp), f32), turned_misc, pltpu.VMEM((cp, sp), f32),
-         pltpu.VMEM((d_model, 2 * cp), f32), turned_misc], "mix_out",
-    )
-    grad_tokens, grad_wout, gpack, grad_win, ggains = finish_call(
-        gpart, gwout, gw, gpack, tokens, grad_resid, gains, grad_gmoe[None], n_seq, 9
+         pltpu.VMEM((d_model, cp), f32), turned_misc,
+         pltpu.VMEM((n_dp, n_seq, rows_in, cp), bf16), pltpu.VMEM((n_dp, cpd, 384), f32)]
+        + finish_scratch(n_seq, here, d_model, rows_in, cp, cpd, 384), "finish", 9,
     )
     own = gain_mix.shape[0]
     ggains = lax.dynamic_slice(
         ggains, (0, (lax.axis_index("dp") * n_seq + lax.axis_index("seq")) * own), (2, own)
     )
     return (
-        result, grad_tokens, ggains[0], grad_win, gpack[:, 256:260], gpack[:, :n_small],
+        result, grad_tokens, ggains[0], grad_win, gpack[:, 256:260],
+        jnp.concatenate([gpack[:, :rank], gpack[:, B_AT : C_AT + NS]], axis=1),
         gpack[:, 128 : 128 + rank], gpack[:, 264], gpack[:, 272 : 272 + NS], gpack[:, 265],
         grad_wout, ggains[1], grad_up[None], grad_down[None],
     )

time: 481 us -> 461 us (0.958)
  Pallas kernels: 417 us -> 404 us
    pallas_call x4 -> x0, Pallas kernels: 114 us -> none  [the longest x1 49 us: finish_call(): pl.pallas_call(partial(finish_kernel, n_seq), in_specs=[vmem] * 8, out_sp...]
    pallas_call x4, Pallas kernels: 148 us -> 240 us  [chunked(): pl.pallas_call(kernel, grid=(steps,), in_specs=[spec(a.shape, r) for a, r...]
    pallas_call x1, Pallas kernels: 29.4 us -> 35.7 us  [seq_gather(): pl.pallas_call(partial(gather_kernel, n_seq), in_specs=[pl.BlockSpec(memo...]
where the time goes in v4:
time: 461 us; the launch traced here: 460 us
  Pallas kernels  404 us (88%)
  matrix products  26.4 us (6%)
  local copies, waits for them, and re-layouts  24.5 us (5%)
    pallas_call x4, Pallas kernels, chunked(): pl.pallas_call(kernel, grid=(steps,), in_specs=[spec(a.shape, r) for a, r...  240 us
    pallas_call x1, Pallas kernels, start_call(): pl.pallas_call(partial(start_kernel, n_seq), in_specs=[anyw, vmem, anyw,...  46.2 us
    pallas_call x1, Pallas kernels, dispatch_call(): pl.pallas_call(partial(dispatch_kernel, n_seq, n_dp), in_specs=[pl.BlockS...  44.7 us
    pallas_call x1, Pallas kernels, collect_call(): pl.pallas_call(partial(collect_kernel, n_seq), in_specs=[vmem], out_specs...  37.3 us
    pallas_call x1, Pallas kernels, seq_gather(): pl.pallas_call(partial(gather_kernel, n_seq), in_specs=[pl.BlockSpec(memo...  35.7 us
    dot_general x9, matrix products, mm(): return lax.dot_general(left, right, dims, preferred_element_type=f32)  26.4 us

profile of v4, /device:TPU:0, one launch (start us, length us, event | category | flops | bytes accessed | tf_op | source)
XLA Modules:
  0.0 460.2 jit_solution(14798931431026000942)
XLA Ops:
  0.6 0.0 copy-start
  0.7 1.4 fusion.24.gains
  2.0 0.8 copy.38
  2.8 0.8 copy.39
  3.6 0.8 copy.41
  4.4 0.8 copy.40
  5.1 0.8 slice.60
  6.0 1.5 concatenate.6.side
  7.5 1.4 copy.42.route
  8.9 46.2 %startup.1 = (bf16[8,2,64,1152]{3,2,1,0:T(8,128)(2,1)}, bf16[4,8,36,768]{3,2,1,0:T(8,128)(2,1)}, bf16[6,72,1152]{2,1,0:T(8,128)(2,1)}, bf16[6,72,384]{2,1,0:T(8,...) custom-call(bf16[2,64,1152]{2,1,0:T(8,128)(2,1)} %bitcast.78, ...), custom_call_target="tpu_custom_call" | custom-call | tf_op jit(solution)/shard_map/startup/pallas_call | solution.py:1073
  55.1 0.9 slice_bitcast_fusion
  56.0 0.7 reshape.104.gain.gains
  56.7 0.1 mul.97
  56.8 3.7 reshape.105.w
  60.5 34.2 %mix_in.1 = (f32[1024,384]{1,0:T(8,128)}, f32[1024,384]{1,0:T(8,128)}, f32[1024,384]{1,0:T(8,128)}, bf16[1024,1152]{1,0:T(8,128)(2,1)}, bf16[8,128,128]{2,1,0:T(8,128)(2,1)}, /*index=5*/bf16[8,4,40,1152]{3,2,1,0:T(8,128)(2,1)}) custom-call(bf16[1024,1152]{1,0:T(8,128)(2,1)} %bitcast.79, f32[2,1152]{1,0:T(2,128)} %reshape.104.gain.gains, ...), custom_call_target="tpu_custom_call" | custom-call | tf_op jit(solution)/shard_map/mix_in/pallas_call | solution.py:400
  94.7 0.0 copy-start.4
  94.7 64.5 %scan_forward.1 = (f32[1024,384]{1,0:T(8,128)}, f32[1024,384]{1,0:T(8,128)}, f32[1024,384]{1,0:T(8,128)}, f32[1024,16,384]{2,1,0:T(8,128)}, f32[1024,384]{1,0:T(...) custom-call(bf16[1024,128]{1,0:T(8,128)(2,1)} %bitcast.83, ...), custom_call_target="tpu_custom_call", output_to_operand_aliasing={{7}: (7, {})} | custom-call | tf_op jit(solution)/shard_map/scan_forward/pallas_call | solution.py:400
  159.3 1.2 multiply_reduce_fusion.2
  160.5 1.1 convolution_convert_fusion.2
  161.6 44.7 %dispatch.1 = bf16[8,4,40,1152]{3,2,1,0:T(8,128)(2,1)} custom-call(bf16[4,40,1152]{2,1,0:T(8,128)(2,1)} %bitcast.80), custom_call_target="tpu_custom_call" | custom-call | tf_op jit(solution)/shard_map/dispatch/pallas_call | solution.py:648
  206.4 0.0 copy-start.9
  206.4 7.5 %multiply_convert_fusion = (bf16[1280,384]{1,0:T(8,128)(2,1)S(1)}, f32[1280,384]{1,0:T(8,128)S(1)}, f32[1280,384]{1,0:T(8,128)S(1)}) fusion(bf16[1280,1152]{1,0:T(8,128)(2,1)} %bitcast.73, bf16[1,384,1152]{2,1,0:T(8,128)(2,1)S(1)} %copy-done), kind=kOutput, calls=%fused_computation.9 | convolution fusion | flops 1164410880 | bytes 8749056 | tf_op jit(solution)/shard_map/dot_general | solution.py:24
  213.9 2.4 add_convert_fusion
  216.3 2.7 convolution_bitcast_fusion
  219.0 2.7 convolution_bitcast_fusion.1
  221.7 3.3 convolution_convert_fusion.1
  225.1 37.3 %collect.1 = bf16[4,40,1152]{2,1,0:T(8,128)(2,1)} custom-call(bf16[8,4,40,1152]{3,2,1,0:T(8,128)(2,1)} %bitcast.75), custom_call_target="tpu_custom_call" | custom-call | tf_op jit(solution)/shard_map/collect/pallas_call | solution.py:822
  262.4 1.4 multiply_reduce_fusion
  263.8 0.6 reshape.119.ggmoe
  264.5 1.1 fusion.27
  265.6 3.4 convolution_convert_fusion
  268.9 35.7 %seq_gather.1 = bf16[8,2,64,1152]{3,2,1,0:T(8,128)(2,1)} custom-call(bf16[2,64,1152]{2,1,0:T(8,128)(2,1)} %bitcast.82), custom_call_target="tpu_custom_call" | custom-call | tf_op jit(solution)/shard_map/seq_gather/pallas_call | solution.py:603
  304.6 75.0 %scan_backward.1 = (f32[1024,384]{1,0:T(8,128)}, bf16[1024,384]{1,0:T(8,128)(2,1)}, bf16[4,72,1152]{2,1,0:T(8,128)(2,1)}, f32[384,128]{1,0:T(8,128)}, f32[32,384...) custom-call(bf16[1024,1152]{1,0:T(8,128)(2,1)} %bitcast.69, ...), custom_call_target="tpu_custom_call" | custom-call | tf_op jit(solution)/shard_map/scan_backward/pallas_call | solution.py:400
  379.6 1.9 fusion
  381.5 66.3 %finish.1 = (f32[128,1152]{1,0:T(8,128)}, f32[72,1152]{1,0:T(8,128)}, f32[72,384]{1,0:T(8,128)}, f32[36,4608]{1,0:T(8,128)}, f32[2,1152]{1,0:T(2,128)}) custom-call(bf16[1024,128]{1,0:T(8,128)(2,1)} %bitcast.86, bf16[432,384]{1,0:T(8,128)(2,1)} %bitcast.67, bf16[432,384]{1,0:T(8,128)(2,1)} %bitcast.68, f32[1024,384]{1,0:T(8,128)} %get-tuple-element.54.conv, ...), custom_call_target="tpu_custom_call" | custom-call | tf_op jit(solution)/shard_map/finish/pallas_call | solution.py:400
  447.9 0.8 constant_dynamic-slice_fusion
  448.7 0.5 slice_bitcast_fusion.1
  449.2 1.6 slice_reduce_fusion
  450.8 0.8 slice.71
  451.7 0.8 slice.74
  452.5 0.7 copy.46
  453.2 0.8 slice.69
  454.0 1.4 fusion.29
  455.4 0.7 copy.45
  456.0 0.7 pad_maximum_fusion
  456.7 1.9 copy.51
  458.6 0.9 copy.52
  459.5 0.7 copy.53
  (32 shorter events, 0.1 us)
Async XLA Ops:
  0.6 205.7 %copy-start = (bf16[1,384,1152]{2,1,0:T(8,128)(2,1)S(1)}, bf16[1,384,1152]{2,1,0:T(8,128)(2,1)}, u32[]{:S(2)}) copy-start(bf16[1,384,1152]{2,1,0:T(8,128)(2,1)} %param.28) | copy-start | bytes 2654212
  94.7 64.6 %copy-start.4 = (bf16[128,1152]{1,0:T(8,128)(2,1)S(1)}, bf16[128,1152]{1,0:T(8,128)(2,1)}, u32[]{:S(2)}) copy-start(bf16[128,1152]{1,0:T(8,128)(2,1)} %tok.1) | copy-start | bytes 884740
  94.7 65.8 %copy-start.7 = (bf16[128,160]{1,0:T(8,128)(2,1)S(1)}, bf16[128,160]{1,0:T(8,128)(2,1)}, u32[]{:S(2)}) copy-start(bf16[128,160]{1,0:T(8,128)(2,1)} %get-tuple-element.59) | copy-start | bytes 122884
  206.4 7.6 %copy-start.3 = (bf16[8,4,40,1152]{3,2,1,0:T(8,128)(2,1)S(1)}, bf16[8,4,40,1152]{3,2,1,0:T(8,128)(2,1)}, u32[]{:S(2)}) copy-start(bf16[8,4,40,1152]{3,2,1,0:T(8,128)(2,1)} %get-tuple-element.60) | copy-start | bytes 8847364
  206.4 7.6 %copy-start.9 = (bf16[1,384,1152]{2,1,0:T(8,128)(2,1)S(1)}, bf16[1,384,1152]{2,1,0:T(8,128)(2,1)}, u32[]{:S(2)}) copy-start(bf16[1,384,1152]{2,1,0:T(8,128)(2,1)} %param.29) | copy-start | bytes 2654212
  213.9 2.4 copy-start.10
  216.3 2.7 copy-start.2
  225.1 39.4 %copy-start.5 = (bf16[128,1152]{1,0:T(8,128)(2,1)S(1)}, bf16[128,1152]{1,0:T(8,128)(2,1)}, u32[]{:S(2)}) copy-start(bf16[128,1152]{1,0:T(8,128)(2,1)} %cot.1) | copy-start | bytes 884740
  262.4 3.2 copy-start.11
  447.9 10.8 %copy-start.6 = (f32[36,4608]{1,0:T(8,128)S(1)}, f32[36,4608]{1,0:T(8,128)}, u32[]{:S(2)}) copy-start(f32[36,4608]{1,0:T(8,128)} %get-tuple-element.143) | copy-start | bytes 1990660
  447.9 11.6 %copy-start.8 = (f32[72,1152]{1,0:T(8,128)S(1)}, f32[72,1152]{1,0:T(8,128)}, u32[]{:S(2)}) copy-start(f32[72,1152]{1,0:T(8,128)} %get-tuple-element.150) | copy-start | bytes 995332
  449.2 11.0 %copy-start.1 = (bf16[1,384,1152]{2,1,0:T(8,128)(2,1)S(1)}, bf16[1,384,1152]{2,1,0:T(8,128)(2,1)}, u32[]{:S(2)}) copy-start(bf16[1,384,1152]{2,1,0:T(8,128)(2,1)} %param.28) | copy-start | bytes 2654212
